TPU v7x, 512 devices: a whole 4x8x8 slice. The times are simulated.
512 devices in a mesh: rows: 64 (over z, y_hi, x), cols: 8 (over y_lo, core).
Axes of the slice: x: 4, y: 8 (y_hi: 2, y_lo: 4; y = y_hi * 4 + y_lo), z: 8, core: 2. Of those that a mesh axis runs over, the one named last changes fastest.
Arguments:
- pair_map: bfloat16 [32, 512, 8192], P(None, 'cols', 'rows'), may hold values from -44 to 44
- conv_in: bfloat16 [32, 288], replicated, may hold values from -0.375 to 0.375
- embed_weight: bfloat16 [2048, 256], replicated, may hold values from -0.125 to 0.125
- qkv_weight: bfloat16 [256, 768], replicated, may hold values from -0.5 to 0.5
- key_bias: bfloat16 [1024, 64, 8], P('rows', 'cols'), may hold values from -4 to 260
- out_weight: bfloat16 [256, 256], replicated, may hold values from -0.375 to 0.375
- unpatch: bfloat16 [256, 2048], replicated, may hold values from -0.375 to 0.375
- conv_out: bfloat16 [32, 288], replicated, may hold values from -0.375 to 0.375
Outputs:
- trunk_out: bfloat16 [32, 512, 8192], P(None, 'cols', 'rows')
All inputs are finite; a program needn't handle non-finite values.
Results may differ from a plain program's by a relative error of at most 0.014.
Values may be sent and summed in bfloat16 or wider, within the bound.
No kernel may reach another device: no remote copies, remote signals or barrier semaphores. Data moves between devices by JAX's collectives and lax.ppermute only.
A program may use at most 128 MiB of HBM per device.

v0:
```python
import jax
import jax.numpy as jnp
from jax import lax
from jax.sharding import PartitionSpec as P

C = 32
PATCH = 8
D = 256
HEADS = 8
HEAD_DIM = 32


epsilon = 1e-05


def padded_2(block, sides, width):
    for axis, dim in sides:
        count = lax.axis_size(axis)
        forward = [(i, i + 1) for i in range(count - 1)]
        backward = [(target, source) for source, target in forward]
        low = lax.ppermute(
            lax.slice_in_dim(block, block.shape[dim] - width, None, axis=dim), axis, forward
        )
        high = lax.ppermute(lax.slice_in_dim(block, 0, width, axis=dim), axis, backward)
        block = jnp.concatenate([low, block, high], axis=dim)
    return block


def conv_valid(padded, weight):
    channels = padded.shape[0]
    extent_one = padded.shape[1] - 2
    extent_two = padded.shape[2] - 2
    stacked = jnp.concatenate(
        [
            padded[:, shift_col : shift_col + extent_one, shift_row : shift_row + extent_two]
            for shift_col in range(3)
            for shift_row in range(3)
        ],
        axis=0,
    )
    product = jnp.dot(
        weight,
        stacked.reshape(9 * channels, extent_one * extent_two),
        preferred_element_type=jnp.float32,
    )
    return product.reshape(weight.shape[0], extent_one, extent_two)


def convolve(local_map, weight, fetch_rim):
    return conv_valid(fetch_rim(local_map), weight)


def fetch_input(local_map):
    return padded_2(local_map, (("rows", 2), ("cols", 1)), 1)


def fetch_output(local_map):
    return padded_2(local_map, (("rows", 2), ("cols", 1)), 1)


def layer_norm(tokens):
    values = tokens.astype(jnp.float32)
    row_mean = jnp.mean(values, axis=1, keepdims=True)
    centered = values - row_mean
    row_var = jnp.mean(centered * centered, axis=1, keepdims=True)
    return (centered * lax.rsqrt(row_var + epsilon)).astype(jnp.bfloat16)


def attend(qkv_rows, bias_row):
    seq_length = qkv_rows.shape[0]
    block_rows = min(512, seq_length)
    queries = qkv_rows[:, :HEAD_DIM]
    key_rows = qkv_rows[:, HEAD_DIM : 2 * HEAD_DIM]
    value_rows = qkv_rows[:, 2 * HEAD_DIM :]
    key_shift = bias_row.astype(jnp.float32)[None, :]
    score_scale = HEAD_DIM ** (-0.5)

    def one_block(query_block):
        scores = (
            jnp.dot(query_block, key_rows.T, preferred_element_type=jnp.float32) * score_scale
            + key_shift
        )
        row_peak = jnp.max(scores, axis=1, keepdims=True)
        weights = jnp.exp(scores - row_peak)
        soft_weights = (weights / jnp.sum(weights, axis=1, keepdims=True)).astype(jnp.bfloat16)
        return jnp.dot(soft_weights, value_rows, preferred_element_type=jnp.float32).astype(
            jnp.bfloat16
        )

    result = lax.map(one_block, queries.reshape(seq_length // block_rows, block_rows, HEAD_DIM))
    return result.reshape(seq_length, HEAD_DIM)


def attend_many(qkv_items, bias_items):

    def attend_pair(pair_item):
        return attend(pair_item[0], pair_item[1])

    return lax.map(attend_pair, (qkv_items, bias_items))


def per_device(
    pair_map, conv_in, embed_weight, qkv_weight, key_bias, out_weight, unpatch, conv_out
):
    col_cells = pair_map.shape[1]
    row_cells = pair_map.shape[2]
    patch_cols = col_cells // PATCH
    patch_rows = row_cells // PATCH
    first_conv = convolve(pair_map, conv_in, fetch_input)
    mixed_map = (pair_map.astype(jnp.float32) + jax.nn.silu(first_conv)).astype(jnp.bfloat16)
    patches = (
        mixed_map.reshape(C, patch_cols, PATCH, patch_rows, PATCH)
        .transpose(3, 1, 0, 2, 4)
        .reshape(patch_rows * patch_cols, C * PATCH * PATCH)
    )
    tokens = jnp.dot(patches, embed_weight, preferred_element_type=jnp.float32).astype(jnp.bfloat16)
    normed = layer_norm(tokens)
    projected = jnp.dot(normed, qkv_weight, preferred_element_type=jnp.float32).astype(jnp.bfloat16)
    split_qkv = projected.reshape(patch_rows, patch_cols, 3, HEADS, HEAD_DIM)
    row_groups = lax.axis_size("rows")
    pair_share = patch_cols * HEADS // row_groups
    packed = split_qkv.transpose(1, 3, 0, 2, 4).reshape(
        row_groups, pair_share, patch_rows, 3 * HEAD_DIM
    )
    biases = key_bias.transpose(1, 2, 0).reshape(row_groups, pair_share, patch_rows)
    qkv_in = lax.all_to_all(packed, "rows", split_axis=0, concat_axis=2, tiled=True)
    bias_in = lax.all_to_all(biases, "rows", split_axis=0, concat_axis=2, tiled=True)
    outputs = attend_many(qkv_in[0], bias_in[0])
    returned = lax.all_to_all(outputs[None], "rows", split_axis=2, concat_axis=0, tiled=True)
    attended = (
        returned.reshape(patch_cols, HEADS, patch_rows, HEAD_DIM)
        .transpose(2, 0, 1, 3)
        .reshape(patch_rows * patch_cols, D)
    )
    updated = (
        tokens.astype(jnp.float32)
        + jnp.dot(attended, out_weight, preferred_element_type=jnp.float32)
    ).astype(jnp.bfloat16)
    expanded = jnp.dot(updated, unpatch, preferred_element_type=jnp.float32)
    expanded = (
        expanded.reshape(patch_rows, patch_cols, C, PATCH, PATCH)
        .transpose(2, 1, 3, 0, 4)
        .reshape(C, col_cells, row_cells)
    )
    merged = (mixed_map.astype(jnp.float32) + expanded).astype(jnp.bfloat16)
    second_conv = convolve(merged, conv_out, fetch_output)
    return (merged.astype(jnp.float32) + second_conv).astype(jnp.bfloat16)


def solution(mesh):
    placed = (P(None, "cols", "rows"), P(), P(), P(), P("rows", "cols", None), P(), P(), P())
    return jax.shard_map(
        per_device, mesh=mesh, in_specs=placed, out_specs=P(None, "cols", "rows"), check_vma=False
    )
```

profile of v0, /device:TPU:54, one launch (start us, length us, event | category | flops | bytes accessed | tf_op | source)
XLA Modules:
  0.0 233.4 jit_solution(9308667724155780518)
XLA Ops:
  1.6 5.5 %collective-permute-start = (bf16[32,64,1]{2,1,0:T(8,128)(2,1)S(1)}, bf16[32,64,1]{2,1,0:T(8,128)(2,1)S(1)}, u32[]{:S(2)}, u32[]{:S(2)}) collective-permute-start(bf16[32,64,1]{2,1,0:T(8,128)(2,1)S(1)} %get-tuple-element.74), channel_id=1, source_target_pairs={{0,8},{8,16},{16,24},{24,32},{32,40},{40,48},{48,56},{56,64},{64,7... | collective-permute-start | bytes 12296 | tf_op jit(solution)/shard_map/ppermute | solution.py:21
  7.1 1.9 collective-permute-start.1
  9.1 20.2 %collective-permute-done = bf16[32,64,1]{2,1,0:T(8,128)(2,1)S(1)} collective-permute-done((bf16[32,64,1]{2,1,0:T(8,128)(2,1)S(1)}, bf16[32,64,1]{2,1,0:T(8,128)(2,1)S(1)}, u32[]{:S(2)}, u32[]{:S(2)}) %collective-permute-start) | collective-permute-done | bytes 4128 | tf_op jit(solution)/shard_map/ppermute | solution.py:21
  29.3 11.0 %collective-permute-done.1 = bf16[32,64,1]{2,1,0:T(8,128)(2,1)S(1)} collective-permute-done((bf16[32,64,1]{2,1,0:T(8,128)(2,1)S(1)}, bf16[32,64,1]{2,1,0:T(8,128)(2,1)S(1)}, u32[]{:S(2)}, u32[]{:S(2)}) %collective-permute-start.1) | collective-permute-done | bytes 4128 | tf_op jit(solution)/shard_map/ppermute | solution.py:24
  42.5 2.4 %collective-permute-start.2 = (bf16[32,1,130]{2,1,0:T(2,128)(2,1)S(1)}, bf16[32,1,130]{2,1,0:T(2,128)(2,1)S(1)}, u32[]{:S(2)}, u32[]{:S(2)}) collective-permute-start(bf16[32,1,130]{2,1,0:T(2,128)(2,1)S(1)} %get-tuple-element.71), channel_id=1, source_target_pairs={{0,1},{1,2},{2,3},{3,4},{4,5},{5,6},{6,7},{8,9},{9,10},{10,11},{11... | collective-permute-start | bytes 24968 | tf_op jit(solution)/shard_map/ppermute | solution.py:21
  45.5 17.7 %all-to-all-start.1 = ((bf16[64,1,16]{2,1,0:T(2,128)(2,1)}), bf16[64,1,16]{2,1,0:T(2,128)(2,1)S(1)}, u32[]{:S(2)}, u32[]{:S(2)}) async-start(bf16[64,1,16]{2,1,0:T(2,128)(2,1)} %copy.111), calls=%async_computation.1 | async-start | bytes 65536 | tf_op jit(solution)/shard_map/all_to_all | solution.py:127
  67.7 2.8 %fusion.15 = f32[4,8,64,128]{3,1,2,0:T(8,128)S(1)} fusion(bf16[32,288]{1,0:T(8,128)(2,1)S(1)} %copy-done.4, bf16[36,8,64,128]{3,2,1,0:T(8,128)(2,1)S(1)} %bitcast.95), kind=kOutput, calls=%fused_computation.19 | convolution fusion | flops 150994944 | bytes 5785600 | tf_op jit(solution)/shard_map/dot_general | solution.py:41
  72.8 8.5 %copy.108 = bf16[16,8,32,8,8]{4,3,2,1,0:T(8,128)(2,1)} copy(bf16[16,8,32,8,8]{2,4,0,3,1:T(8,128)(2,1)} %bitcast.94) | data formatting | bytes 1048576 | tf_op jit(solution)/shard_map/transpose | solution.py:113
  81.3 12.9 %reshape.90 = bf16[128,2048]{1,0:T(8,128)(2,1)S(1)} reshape(bf16[16,8,32,8,8]{4,3,2,1,0:T(8,128)(2,1)} %copy.108) | data formatting | bytes 1048576 | tf_op jit(solution)/shard_map/reshape | solution.py:114
  100.4 15.1 %all-to-all-start = ((bf16[64,1,16,96]{3,2,1,0:T(8,128)(2,1)}), bf16[64,1,16,96]{3,2,1,0:T(8,128)(2,1)S(1)}, u32[]{:S(2)}, u32[]{:S(2)}) async-start(bf16[64,1,16,96]{3,2,1,0:T(8,128)(2,1)} %bitcast.7), calls=%async_computation | async-start | bytes 524288 | tf_op jit(solution)/shard_map/all_to_all | solution.py:126
  115.7 11.8 %all-to-all-done = bf16[64,1,16,96]{3,2,1,0:T(8,128)(2,1)S(1)} async-done(((bf16[64,1,16,96]{3,2,1,0:T(8,128)(2,1)}), bf16[64,1,16,96]{3,2,1,0:T(8,128)(2,1)S(1)}, u32[]{:S(2)}, u32[]{:S(2)}) %all-to-all-start) | async-done | bytes 196640 | tf_op jit(solution)/shard_map/all_to_all | solution.py:126
  127.7 3.6 %while.17 = (s32[]{:T(128)}, bf16[2,512,32]{1,2,0:T(8,128)(2,1)S(1)}, bf16[2,512,32]{2,1,0:T(8,128)(2,1)S(1)}, bf16[1024,32]{1,0:T(8,128)(2,1)S(1)}, f32[1,1024]...) while((s32[]{:T(128)}, bf16[2,512,32]{1,2,0:T(8,128)(2,1)S(1)}, ...), condition=%wide.region_5.6_spmd, body=%wide.region_2.5_spmd.sunk | while | flops 73415680 | bytes 7002205 | solution.py:90
  132.4 2.3 reduce.4
  134.8 18.7 %all_to_all.12 = bf16[64,2,256]{2,1,0:T(2,128)(2,1)S(1)} all-to-all(bf16[64,2,256]{2,1,0:T(2,128)(2,1)S(1)} %reshape.109), channel_id=1, replica_groups=mesh['rows'=64,'cols'=8] {'rows'}, dimensions={0} | all-to-all | bytes 131072 | tf_op jit(solution)/shard_map/all_to_all | solution.py:129
  154.6 11.1 %reshape.97 = f32[16,8,32,8,8]{4,3,2,1,0:T(8,128)} reshape(f32[128,2048]{1,0:T(8,128)S(1)} %fusion.23) | data formatting | bytes 2097152 | tf_op jit(solution)/shard_map/reshape | solution.py:141
  165.7 11.5 %copy.115 = f32[32,8,8,16,8]{0,4,3,2,1:T(8,128)} copy(f32[32,8,8,16,8]{4,2,0,1,3:T(8,128)} %bitcast.92) | data formatting | bytes 2097152 | tf_op jit(solution)/shard_map/transpose | solution.py:142
  177.2 3.0 %copy.116 = f32[32,64,128]{2,1,0:T(8,128)S(1)} copy(f32[32,64,128]{0,2,1:T(8,128)} %bitcast.93) | data formatting | bytes 2097152 | tf_op jit(solution)/shard_map/reshape | solution.py:143
  180.6 8.8 %collective-permute-start.4 = (bf16[32,64,1]{2,1,0:T(8,128)(2,1)S(1)}, bf16[32,64,1]{2,1,0:T(8,128)(2,1)S(1)}, u32[]{:S(2)}, u32[]{:S(2)}) collective-permute-start(bf16[32,64,1]{2,1,0:T(8,128)(2,1)S(1)} %get-tuple-element.72), channel_id=1, source_target_pairs={{0,8},{8,16},{16,24},{24,32},{32,40},{40,48},{48,56},{56,64},{64,7... | collective-permute-start | bytes 12296 | tf_op jit(solution)/shard_map/ppermute | solution.py:21
  191.3 13.7 %collective-permute-done.4 = bf16[32,64,1]{2,1,0:T(8,128)(2,1)S(1)} collective-permute-done((bf16[32,64,1]{2,1,0:T(8,128)(2,1)S(1)}, bf16[32,64,1]{2,1,0:T(8,128)(2,1)S(1)}, u32[]{:S(2)}, u32[]{:S(2)}) %collective-permute-start.4) | collective-permute-done | bytes 4128 | tf_op jit(solution)/shard_map/ppermute | solution.py:21
  205.0 11.0 %collective-permute-done.5 = bf16[32,64,1]{2,1,0:T(8,128)(2,1)S(1)} collective-permute-done((bf16[32,64,1]{2,1,0:T(8,128)(2,1)S(1)}, bf16[32,64,1]{2,1,0:T(8,128)(2,1)S(1)}, u32[]{:S(2)}, u32[]{:S(2)}) %collective-permute-start.5) | collective-permute-done | bytes 4128 | tf_op jit(solution)/shard_map/ppermute | solution.py:24
  216.3 3.5 %collective-permute-start.7 = (bf16[32,1,130]{2,1,0:T(2,128)(2,1)S(1)}, bf16[32,1,130]{2,1,0:T(2,128)(2,1)S(1)}, u32[]{:S(2)}, u32[]{:S(2)}) collective-permute-start(bf16[32,1,130]{2,1,0:T(2,128)(2,1)S(1)} %get-tuple-element.66), channel_id=1, source_target_pairs={{1,0},{2,1},{3,2},{4,3},{5,4},{6,5},{7,6},{9,8},{10,9},{11,10},{12... | collective-permute-start | bytes 24968 | tf_op jit(solution)/shard_map/ppermute | solution.py:24
  219.8 2.1 collective-permute-start.6
  222.0 3.1 %collective-permute-done.6 = bf16[32,1,130]{2,1,0:T(2,128)(2,1)S(1)} collective-permute-done((bf16[32,1,130]{2,1,0:T(2,128)(2,1)S(1)}, bf16[32,1,130]{2,1,0:T(2,128)(2,1)S(1)}, u32[]{:S(2)}, u32[]{:S(2)}) %collective-permute-start.6) | collective-permute-done | bytes 8352 | tf_op jit(solution)/shard_map/ppermute | solution.py:21
  229.4 2.8 %fusion.18 = f32[4,8,64,128]{3,1,2,0:T(8,128)S(1)} fusion(bf16[32,288]{1,0:T(8,128)(2,1)S(1)} %copy-done.5, bf16[36,8,64,128]{3,2,1,0:T(8,128)(2,1)S(1)} %bitcast.96), kind=kOutput, calls=%fused_computation.20 | convolution fusion | flops 150994944 | bytes 5785600 | tf_op jit(solution)/shard_map/dot_general | solution.py:41
  (79 shorter events, 31.4 us)
Async XLA Ops:
  0.0 154.2 %copy-start = (bf16[256,2048]{1,0:T(8,128)(2,1)S(1)}, bf16[256,2048]{1,0:T(8,128)(2,1)}, u32[]{:S(2)}) copy-start(bf16[256,2048]{1,0:T(8,128)(2,1)} %param.16) | copy-start | bytes 3145732
  0.0 40.3 %copy-start.1 = (bf16[32,64,128]{2,1,0:T(8,128)(2,1)S(1)}, bf16[32,64,128]{2,1,0:T(8,128)(2,1)}, u32[]{:S(2)}) copy-start(bf16[32,64,128]{2,1,0:T(8,128)(2,1)} %param.10) | copy-start | bytes 1572868
  0.0 44.9 %copy-start.6 = (bf16[16,8,8]{0,2,1:T(8,128)(2,1)S(1)}, bf16[16,8,8]{0,2,1:T(8,128)(2,1)}, u32[]{:S(2)}) copy-start(bf16[16,8,8]{0,2,1:T(8,128)(2,1)} %param.14) | copy-start | bytes 6148
  1.6 27.7 %collective-permute-start = (bf16[32,64,1]{2,1,0:T(8,128)(2,1)S(1)}, bf16[32,64,1]{2,1,0:T(8,128)(2,1)S(1)}, u32[]{:S(2)}, u32[]{:S(2)}) collective-permute-start(bf16[32,64,1]{2,1,0:T(8,128)(2,1)S(1)} %get-tuple-element.74), channel_id=1, source_target_pairs={{0,8},{8,16},{16,24},{24,32},{32,40},{40,48},{48,56},{56,64},{64,7... | collective-permute-start | bytes 12296 | tf_op jit(solution)/shard_map/ppermute | solution.py:21
  7.1 33.2 %collective-permute-start.1 = (bf16[32,64,1]{2,1,0:T(8,128)(2,1)S(1)}, bf16[32,64,1]{2,1,0:T(8,128)(2,1)S(1)}, u32[]{:S(2)}, u32[]{:S(2)}) collective-permute-start(bf16[32,64,1]{2,1,0:T(8,128)(2,1)S(1)} %get-tuple-element.75), channel_id=1, source_target_pairs={{8,0},{16,8},{24,16},{32,24},{40,32},{48,40},{56,48},{64,56},{72,6... | collective-permute-start | bytes 12296 | tf_op jit(solution)/shard_map/ppermute | solution.py:24
  40.5 22.7 %collective-permute-start.3 = (bf16[32,1,130]{2,1,0:T(2,128)(2,1)S(1)}, bf16[32,1,130]{2,1,0:T(2,128)(2,1)S(1)}, u32[]{:S(2)}, u32[]{:S(2)}) collective-permute-start(bf16[32,1,130]{2,1,0:T(2,128)(2,1)S(1)} %get-tuple-element.70), channel_id=1, source_target_pairs={{1,0},{2,1},{3,2},{4,3},{5,4},{6,5},{7,6},{9,8},{10,9},{11,10},{12... | collective-permute-start | bytes 24968 | tf_op jit(solution)/shard_map/ppermute | solution.py:24
  42.5 20.8 %collective-permute-start.2 = (bf16[32,1,130]{2,1,0:T(2,128)(2,1)S(1)}, bf16[32,1,130]{2,1,0:T(2,128)(2,1)S(1)}, u32[]{:S(2)}, u32[]{:S(2)}) collective-permute-start(bf16[32,1,130]{2,1,0:T(2,128)(2,1)S(1)} %get-tuple-element.71), channel_id=1, source_target_pairs={{0,1},{1,2},{2,3},{3,4},{4,5},{5,6},{6,7},{8,9},{9,10},{10,11},{11... | collective-permute-start | bytes 24968 | tf_op jit(solution)/shard_map/ppermute | solution.py:21
  45.5 54.9 %all-to-all-start.1 = ((bf16[64,1,16]{2,1,0:T(2,128)(2,1)}), bf16[64,1,16]{2,1,0:T(2,128)(2,1)S(1)}, u32[]{:S(2)}, u32[]{:S(2)}) async-start(bf16[64,1,16]{2,1,0:T(2,128)(2,1)} %copy.111), calls=%async_computation.1 | async-start | bytes 65536 | tf_op jit(solution)/shard_map/all_to_all | solution.py:127
  65.7 1.9 copy-start.4
  81.3 12.9 %copy-start.2 = (bf16[2048,256]{1,0:T(8,128)(2,1)S(1)}, bf16[2048,256]{1,0:T(8,128)(2,1)}, u32[]{:S(2)}) copy-start(bf16[2048,256]{1,0:T(8,128)(2,1)} %param.12) | copy-start | bytes 3145732
  100.4 27.1 %all-to-all-start = ((bf16[64,1,16,96]{3,2,1,0:T(8,128)(2,1)}), bf16[64,1,16,96]{3,2,1,0:T(8,128)(2,1)S(1)}, u32[]{:S(2)}, u32[]{:S(2)}) async-start(bf16[64,1,16,96]{3,2,1,0:T(8,128)(2,1)} %bitcast.7), calls=%async_computation | async-start | bytes 524288 | tf_op jit(solution)/shard_map/all_to_all | solution.py:126
  131.3 22.8 %copy-start.3 = (bf16[256,256]{1,0:T(8,128)(2,1)S(1)}, bf16[256,256]{1,0:T(8,128)(2,1)}, u32[]{:S(2)}) copy-start(bf16[256,256]{1,0:T(8,128)(2,1)} %param.15) | copy-start | bytes 393220
  180.6 24.4 %collective-permute-start.4 = (bf16[32,64,1]{2,1,0:T(8,128)(2,1)S(1)}, bf16[32,64,1]{2,1,0:T(8,128)(2,1)S(1)}, u32[]{:S(2)}, u32[]{:S(2)}) collective-permute-start(bf16[32,64,1]{2,1,0:T(8,128)(2,1)S(1)} %get-tuple-element.72), channel_id=1, source_target_pairs={{0,8},{8,16},{16,24},{24,32},{32,40},{40,48},{48,56},{56,64},{64,7... | collective-permute-start | bytes 12296 | tf_op jit(solution)/shard_map/ppermute | solution.py:21
  189.4 26.6 %collective-permute-start.5 = (bf16[32,64,1]{2,1,0:T(8,128)(2,1)S(1)}, bf16[32,64,1]{2,1,0:T(8,128)(2,1)S(1)}, u32[]{:S(2)}, u32[]{:S(2)}) collective-permute-start(bf16[32,64,1]{2,1,0:T(8,128)(2,1)S(1)} %get-tuple-element.73), channel_id=1, source_target_pairs={{8,0},{16,8},{24,16},{32,24},{40,32},{48,40},{56,48},{64,56},{72,6... | collective-permute-start | bytes 12296 | tf_op jit(solution)/shard_map/ppermute | solution.py:24
  216.3 5.7 %collective-permute-start.7 = (bf16[32,1,130]{2,1,0:T(2,128)(2,1)S(1)}, bf16[32,1,130]{2,1,0:T(2,128)(2,1)S(1)}, u32[]{:S(2)}, u32[]{:S(2)}) collective-permute-start(bf16[32,1,130]{2,1,0:T(2,128)(2,1)S(1)} %get-tuple-element.66), channel_id=1, source_target_pairs={{1,0},{2,1},{3,2},{4,3},{5,4},{6,5},{7,6},{9,8},{10,9},{11,10},{12... | collective-permute-start | bytes 24968 | tf_op jit(solution)/shard_map/ppermute | solution.py:24
  219.8 5.2 %collective-permute-start.6 = (bf16[32,1,130]{2,1,0:T(2,128)(2,1)S(1)}, bf16[32,1,130]{2,1,0:T(2,128)(2,1)S(1)}, u32[]{:S(2)}, u32[]{:S(2)}) collective-permute-start(bf16[32,1,130]{2,1,0:T(2,128)(2,1)S(1)} %get-tuple-element.67), channel_id=1, source_target_pairs={{0,1},{1,2},{2,3},{3,4},{4,5},{5,6},{6,7},{8,9},{9,10},{10,11},{11... | collective-permute-start | bytes 24968 | tf_op jit(solution)/shard_map/ppermute | solution.py:21
  227.5 1.9 copy-start.5
where the time goes:
time: 234 us; the launch traced here: 233 us
  waiting for transfers between devices  70.8 us (30%)
  local copies, waits for them, and re-layouts  62.3 us (27%)
  starting transfers between devices  61 us (26%)
  blocking collectives  18.7 us (8%)
  matrix products  10.2 us (4%)
  other arithmetic  9.92 us (4%)
    ppermute x4, waiting for transfers between devices, padded_2(): lax.ppermute(lax.slice_in_dim(block, block.shape[dim] - width, None, axis...  37 us
    ppermute x4, waiting for transfers between devices, padded_2(): lax.ppermute(lax.slice_in_dim(block, 0, width, axis=dim), axis, backward)  22.1 us
    ppermute x4, starting transfers between devices, padded_2(): lax.ppermute(lax.slice_in_dim(block, block.shape[dim] - width, None, axis...  18.8 us
    all_to_all x1, blocking collectives, per_device(): lax.all_to_all(outputs[None], 'rows', split_axis=2, concat_axis=0, tiled=...  18.7 us
    all_to_all x1, starting transfers between devices, per_device(): lax.all_to_all(biases, 'rows', split_axis=0, concat_axis=2, tiled=True)  17.7 us
    all_to_all x1, starting transfers between devices, per_device(): lax.all_to_all(packed, 'rows', split_axis=0, concat_axis=2, tiled=True)  15.1 us
    reshape x1, local copies, waits for them, and re-layouts, per_device(): patches = mixed_map.reshape(C, patch_cols, PATCH, patch_rows, PATCH).tran...  12.9 us
    all_to_all x1, waiting for transfers between devices, per_device(): lax.all_to_all(packed, 'rows', split_axis=0, concat_axis=2, tiled=True)  11.8 us
  transfers between devices with their start and end apart: 10, of which 6 were waited for; matrix products, arithmetic and copies ran while one was open for 16% of the time, Pallas kernels for 0%

commit v1 on v0

v1 whole, which is shorter than its diff:
```python
import jax
import jax.numpy as jnp
from jax import lax
from jax.experimental import pallas as pl
from jax.experimental.pallas import tpu as pltpu
from jax.sharding import PartitionSpec as P

C = 32
PATCH = 8
D = 256
HEADS = 8
HEAD_DIM = 32
W = 64
L = 128
PC = W // PATCH
PR = L // PATCH
GROUPS = 64
SEQ = GROUPS * PR
QUAD = 4
epsilon = 1e-05

f32 = jnp.float32
bf16 = jnp.bfloat16
NT = (((1,), (1,)), ((), ()))


def iota(shape, dim):
    return lax.broadcasted_iota(jnp.int32, shape, dim)


def one_hot(condition):
    return jnp.where(condition, 1.0, 0.0).astype(bf16)


def column_edges(slab_of, edges_ref):
    lane = iota((C, L), 1)
    edges = jnp.zeros((C, L), f32)
    for w in range(W):
        slab = slab_of(w)
        first = pltpu.roll(slab, w, 1) if w else slab
        last = pltpu.roll(slab, (W + w + 1) % L, 1) if (W + w + 1) % L else slab
        edges = jnp.where(lane == w, first, edges)
        edges = jnp.where(lane == W + w, last, edges)
    edges_ref[...] = edges.astype(bf16)


def turn_kernel(x_ref, turned_ref, edges_ref, turned_f32):
    turned_f32[...] = jnp.swapaxes(x_ref[...].astype(f32), 0, 1)
    turned_ref[...] = turned_f32[...].astype(bf16)
    column_edges(lambda w: turned_f32[w], edges_ref)


def weights_kernel(embed_ref, unpatch_ref, embed_out, unpatch_out):
    for source, target in ((embed_ref[...].astype(f32), embed_out), (unpatch_ref[...].astype(f32).T, unpatch_out)):
        turned = jnp.swapaxes(source.reshape(C, PATCH * PATCH, D), 0, 1)
        for i in range(PATCH):
            for j in range(PATCH):
                target[i, j * C : (j + 1) * C, :] = turned[j * PATCH + i].astype(bf16)


def fill_taps(map_ref, low_row, high_row, low_col, high_col, taps):
    lane = iota((C, L), 1)
    row_low = low_row[...].astype(f32)
    row_high = high_row[...].astype(f32)
    below = [low_col[n].astype(f32) for n in range(4)]
    above = [high_col[n].astype(f32) for n in range(4)]
    for w in range(-1, W + 1):
        if w < 0:
            slab, left, right = below[1], below[2][:, L - 1 : L], below[3][:, W - 1 : W]
        elif w == W:
            slab, left, right = above[0], above[2][:, W : W + 1], above[3][:, 0:1]
        else:
            slab = map_ref[w].astype(f32)
            left, right = row_low[:, W + w : W + w + 1], row_high[:, w : w + 1]
        taps[w + 1, 0:C, :] = jnp.where(lane == 0, left, pltpu.roll(slab, 1, 1)).astype(bf16)
        taps[w + 1, C : 2 * C, :] = slab.astype(bf16)
        taps[w + 1, 2 * C : 3 * C, :] = jnp.where(lane == L - 1, right, pltpu.roll(slab, L - 1, 1)).astype(bf16)


def banded(weight):
    weight = weight.astype(f32)
    rows = []
    for i in range(QUAD):
        pieces = [weight]
        if i:
            pieces.insert(0, jnp.zeros((C, 3 * C * i), f32))
        if i < QUAD - 1:
            pieces.append(jnp.zeros((C, 3 * C * (QUAD - 1 - i)), f32))
        rows.append(jnp.concatenate(pieces, axis=1))
    return jnp.concatenate(rows, axis=0).astype(bf16)


def conv_quad(band, taps, group):
    window = taps[group * QUAD : group * QUAD + QUAD + 2].reshape((QUAD + 2) * 3 * C, L)
    return jnp.dot(band, window, preferred_element_type=f32)


def front_kernel(
    map_ref, low_row, high_row, low_col, high_col, conv_ref, embed_ref, qkv_ref, bias_ref,
    mixed_ref, tokens_ref, packed_ref, taps, gathered,
):
    fill_taps(map_ref, low_row, high_row, low_col, high_col, taps)
    band = banded(conv_ref[...])
    row = iota((L, L), 0)
    select = one_hot(iota((L, L), 1) == (row % PR) * PATCH + row // PR)
    for p in range(PC):
        for half in range(PATCH // QUAD):
            group = p * (PATCH // QUAD) + half
            value = conv_quad(band, taps, group)
            value = value / (1.0 + jnp.exp(-value))
            for i in range(QUAD):
                w = group * QUAD + i
                cell = taps[w + 1, C : 2 * C, :].astype(f32) + value[i * C : (i + 1) * C]
                mixed_ref[w] = cell.astype(bf16)
        block = mixed_ref[p * PATCH : (p + 1) * PATCH].reshape(PATCH * C, L)
        sorted_cells = lax.dot_general(select, block, NT, preferred_element_type=f32).astype(bf16)
        for i in range(PATCH):
            gathered[p * PR : (p + 1) * PR, i * D : (i + 1) * D] = sorted_cells[i * PR : (i + 1) * PR]
    tokens = jnp.dot(
        gathered[...], embed_ref[...].reshape(PATCH * D, D), preferred_element_type=f32
    ).astype(bf16)
    tokens_ref[...] = tokens
    values = tokens.astype(f32)
    centered = values - jnp.mean(values, axis=1, keepdims=True)
    spread = jnp.mean(centered * centered, axis=1, keepdims=True)
    normed = (centered * lax.rsqrt(spread + epsilon)).astype(bf16)
    projected = jnp.dot(normed, qkv_ref[...], preferred_element_type=f32)
    bias = bias_ref[...].astype(f32)
    filler = jnp.zeros((PR * PC, L - 3 * HEAD_DIM - 1), f32)
    for h in range(HEADS):
        pieces = [projected[:, g * D + h * HEAD_DIM : g * D + (h + 1) * HEAD_DIM] for g in range(3)]
        tile = jnp.concatenate(pieces + [bias[:, h : h + 1], filler], axis=1).astype(bf16)
        for p in range(PC):
            packed_ref[p * HEADS + h] = tile[p * PR : (p + 1) * PR]


def attention_kernel(packed_ref, out_ref, rows_f32):
    rows = packed_ref[...].reshape(SEQ, L)
    lane = iota((SEQ, L), 1)
    wide = rows.astype(f32)
    rows_f32[...] = pltpu.roll(jnp.where(lane < HEAD_DIM, wide, 0.0), HEAD_DIM, 1)
    pick = one_hot((iota((8, L), 1) == 3 * HEAD_DIM))
    bias = lax.dot_general(pick, rows, NT, preferred_element_type=f32)[0:1]
    values = jnp.where((lane >= 2 * HEAD_DIM) & (lane < 3 * HEAD_DIM), wide, 0.0)
    scale = HEAD_DIM ** (-0.5)
    total = jnp.zeros((SEQ // 4, L), f32)
    for quarter in range(4):
        queries = rows_f32[pl.ds(quarter, SEQ // 4, stride=4), :].astype(bf16)
        scores = lax.dot_general(queries, rows, NT, preferred_element_type=f32) * scale + bias
        peak = jnp.max(scores, axis=1, keepdims=True)
        weights = jnp.exp(scores - peak)
        share = (weights * (1.0 / jnp.sum(weights, axis=1, keepdims=True))).astype(bf16)
        shift = (quarter * HEAD_DIM - 2 * HEAD_DIM) % L
        placed = (pltpu.roll(values, shift, 1) if shift else values).astype(bf16)
        total = total + jnp.dot(share, placed, preferred_element_type=f32)
    out_ref[...] = total.astype(bf16)


def merge_kernel(
    returned_ref, tokens_ref, out_weight_ref, unpatch_ref, mixed_ref,
    merged_ref, edges_ref, returned_f32, rows_f32, repeated,
):
    returned_f32[...] = returned_ref[...].astype(f32)
    for low in range(4):
        heads = [returned_f32[pl.ds(h * 4 + low, PC, stride=HEADS * 4), :] for h in range(HEADS)]
        for high in range(4):
            line = jnp.concatenate([x[:, high * HEAD_DIM : (high + 1) * HEAD_DIM] for x in heads], axis=1)
            at = (low * 4 + high) * PC
            rows_f32[at : at + PC, :] = line
    place = iota((PR * PC, PR * PC), 0)
    order = one_hot(iota((PR * PC, PR * PC), 1) == (place % PR) * PC + place // PR)
    attended = jnp.dot(order, rows_f32[...].astype(bf16), preferred_element_type=f32).astype(bf16)
    updated = (
        tokens_ref[...].astype(f32) + jnp.dot(attended, out_weight_ref[...], preferred_element_type=f32)
    ).astype(bf16)
    repeat = one_hot(iota((PC * L, PR * PC), 0) // PATCH == iota((PC * L, PR * PC), 1))
    repeated[...] = jnp.dot(repeat, updated, preferred_element_type=f32)
    inner = iota((L, D), 0) % PATCH
    for p in range(PC):
        block = repeated[p * L : (p + 1) * L, :]
        grown = jnp.zeros((D, L), f32)
        for i in range(PATCH):
            part = jnp.where(inner == i, block, 0.0).astype(bf16)
            grown = grown + lax.dot_general(unpatch_ref[i], part, NT, preferred_element_type=f32)
        cells = mixed_ref[p * PATCH : (p + 1) * PATCH].astype(f32) + grown.reshape(PATCH, C, L)
        merged_ref[p * PATCH : (p + 1) * PATCH] = cells.astype(bf16)
    column_edges(lambda w: merged_ref[w].astype(f32), edges_ref)


def back_kernel(map_ref, low_row, high_row, low_col, high_col, conv_ref, out_ref, taps, result):
    fill_taps(map_ref, low_row, high_row, low_col, high_col, taps)
    band = banded(conv_ref[...])
    for group in range(W // QUAD):
        value = conv_quad(band, taps, group)
        for i in range(QUAD):
            w = group * QUAD + i
            result[w] = taps[w + 1, C : 2 * C, :].astype(f32) + value[i * C : (i + 1) * C]
    out_ref[...] = jnp.swapaxes(result[...], 0, 1).astype(bf16)


def shape(*dims, dtype=bf16):
    return jax.ShapeDtypeStruct(dims, dtype)


def call(kernel, outs, scratch, *args, flops=0):
    return pl.pallas_call(
        kernel,
        out_shape=outs,
        scratch_shapes=scratch,
        name=kernel.__name__,
        cost_estimate=pl.CostEstimate(flops=flops, transcendentals=0, bytes_accessed=1 << 20),
        compiler_params=pltpu.CompilerParams(vmem_limit_bytes=56 << 20),
    )(*args)


def exchange(block, axis):
    count = lax.axis_size(axis)
    forward = [(i, i + 1) for i in range(count - 1)]
    backward = [(target, source) for source, target in forward]
    return lax.ppermute(block, axis, forward), lax.ppermute(block, axis, backward)


def rims(turned, edges):
    low_row, high_row = exchange(edges, "rows")
    strip = jnp.stack([turned[0], turned[W - 1], low_row, high_row])
    low_col, high_col = exchange(strip, "cols")
    return low_row, high_row, low_col, high_col


def per_device(pair_map, conv_in, embed_weight, qkv_weight, key_bias, out_weight, unpatch, conv_out):
    turned, edges = call(
        turn_kernel, (shape(W, C, L), shape(C, L)), [pltpu.VMEM((W, C, L), f32)], pair_map
    )
    embed_rows, unpatch_rows = call(
        weights_kernel, (shape(PATCH, D, D), shape(PATCH, D, D)), [], embed_weight, unpatch, flops=1 << 32
    )
    bias = key_bias.transpose(1, 0, 2).reshape(PR * PC, HEADS)
    mixed, tokens, packed = call(
        front_kernel,
        (shape(W, C, L), shape(PR * PC, D), shape(GROUPS, PR, L)),
        [pltpu.VMEM((W + 2, 3 * C, L), bf16), pltpu.VMEM((PR * PC, PATCH * D), bf16)],
        turned, *rims(turned, edges), conv_in, embed_rows, qkv_weight, bias,
    )
    arrived = lax.all_to_all(packed, "rows", split_axis=0, concat_axis=0, tiled=True)
    heads_out = call(
        attention_kernel, shape(SEQ // 4, L), [pltpu.VMEM((SEQ, L), f32)], arrived
    )
    returned = lax.all_to_all(
        heads_out.reshape(GROUPS, 4, L), "rows", split_axis=0, concat_axis=0, tiled=True
    ).reshape(GROUPS * 4, L)
    merged, edges = call(
        merge_kernel,
        (shape(W, C, L), shape(C, L)),
        [pltpu.VMEM((GROUPS * 4, L), f32), pltpu.VMEM((PR * PC, D), f32), pltpu.VMEM((PC * L, D), f32)],
        returned, tokens, out_weight, unpatch_rows, mixed,
    )
    return call(
        back_kernel,
        shape(C, W, L),
        [pltpu.VMEM((W + 2, 3 * C, L), bf16), pltpu.VMEM((W, C, L), f32)],
        merged, *rims(merged, edges), conv_out,
    )


def solution(mesh):
    placed = (P(None, "cols", "rows"), P(), P(), P(), P("rows", "cols", None), P(), P(), P())
    return jax.shard_map(
        per_device, mesh=mesh, in_specs=placed, out_specs=P(None, "cols", "rows"), check_vma=False
    )
```

time: 234 us -> 128 us (0.55)
  the two profiles are of different devices: /device:TPU:54 before, /device:TPU:48 now
where the time goes in v1:
time: 128 us; the launch traced here: 127 us
  blocking collectives  50.6 us (40%)
  starting transfers between devices  26.2 us (20%)
  Pallas kernels  24.4 us (19%)
  waiting for transfers between devices  21.1 us (16%)
  local copies, waits for them, and re-layouts  4.5 us (4%)
    all_to_all x1, blocking collectives, per_device(): lax.all_to_all(packed, 'rows', split_axis=0, concat_axis=0, tiled=True)  29.5 us
    pallas_call x6, Pallas kernels, call(): pl.pallas_call(kernel, out_shape=outs, scratch_shapes=scratch, name=kerne...  24.4 us
    all_to_all x1, blocking collectives, per_device(): lax.all_to_all(heads_out.reshape(GROUPS, 4, L), 'rows', split_axis=0, con...  21.1 us
    ppermute x4, waiting for transfers between devices, exchange(): lax.ppermute(block, axis, forward)  21 us
    ppermute x4, starting transfers between devices, exchange(): lax.ppermute(block, axis, backward)  17.6 us
    ppermute x4, starting transfers between devices, exchange(): lax.ppermute(block, axis, forward)  8.65 us
  transfers between devices with their start and end apart: 8, of which 3 were waited for; matrix products, arithmetic and copies ran while one was open for 2% of the time, Pallas kernels for 3%

profile of v1, /device:TPU:48, one launch (start us, length us, event | category | flops | bytes accessed | tf_op | source)
XLA Modules:
  0.0 127.0 jit_solution(8168619176896448031)
XLA Ops:
  0.0 2.2 %turn_kernel.1 = (bf16[64,32,128]{2,1,0:T(8,128)(2,1)}, bf16[32,128]{1,0:T(8,128)(2,1)}) custom-call(bf16[32,64,128]{2,1,0:T(8,128)(2,1)} %x_ref.1), custom_call_target="tpu_custom_call" | custom-call | bytes 1048576 | tf_op jit(solution)/shard_map/turn_kernel/pallas_call | solution.py:206
  2.2 6.0 %collective-permute-start.1 = (bf16[32,128]{1,0:T(8,128)(2,1)}, bf16[32,128]{1,0:T(8,128)(2,1)S(1)}, u32[]{:S(2)}, u32[]{:S(2)}) collective-permute-start(bf16[32,128]{1,0:T(8,128)(2,1)} %get-tuple-element.15), channel_id=1, source_target_pairs={{8,0},{16,8},{24,16},{32,24},{40,32},{48,40},{56,48},{64,56},{72,6... | collective-permute-start | bytes 24584 | tf_op jit(solution)/shard_map/ppermute | solution.py:220
  8.2 1.9 %collective-permute-start = (bf16[32,128]{1,0:T(8,128)(2,1)}, bf16[32,128]{1,0:T(8,128)(2,1)S(1)}, u32[]{:S(2)}, u32[]{:S(2)}) collective-permute-start(bf16[32,128]{1,0:T(8,128)(2,1)} %get-tuple-element.15), channel_id=1, source_target_pairs={{0,8},{8,16},{16,24},{24,32},{32,40},{40,48},{48,56},{56,64},{64,7... | collective-permute-start | bytes 24584 | tf_op jit(solution)/shard_map/ppermute | solution.py:220
  10.2 0.7 fusion.1
  10.9 9.1 %collective-permute-done.low_row = bf16[32,128]{1,0:T(8,128)(2,1)S(1)} collective-permute-done((bf16[32,128]{1,0:T(8,128)(2,1)}, bf16[32,128]{1,0:T(8,128)(2,1)S(1)}, u32[]{:S(2)}, u32[]{:S(2)}) %collective-permute-start) | collective-permute-done | bytes 8224 | tf_op jit(solution)/shard_map/ppermute | solution.py:220
  20.6 2.0 %collective-permute-start.3 = (bf16[4,32,128]{2,1,0:T(8,128)(2,1)S(1)}, bf16[4,32,128]{2,1,0:T(8,128)(2,1)S(1)}, u32[]{:S(2)}, u32[]{:S(2)}) collective-permute-start(bf16[4,32,128]{2,1,0:T(8,128)(2,1)S(1)} %pad_maximum_fusion), channel_id=1, source_target_pairs={{1,0},{2,1},{3,2},{4,3},{5,4},{6,5},{7,6},{9,8},{10,9},{11,10},{12... | collective-permute-start | bytes 98312 | tf_op jit(solution)/shard_map/ppermute | solution.py:220
  22.7 2.4 %collective-permute-start.2 = (bf16[4,32,128]{2,1,0:T(8,128)(2,1)S(1)}, bf16[4,32,128]{2,1,0:T(8,128)(2,1)S(1)}, u32[]{:S(2)}, u32[]{:S(2)}) collective-permute-start(bf16[4,32,128]{2,1,0:T(8,128)(2,1)S(1)} %pad_maximum_fusion), channel_id=1, source_target_pairs={{0,1},{1,2},{2,3},{3,4},{4,5},{5,6},{6,7},{8,9},{9,10},{10,11},{11... | collective-permute-start | bytes 98312 | tf_op jit(solution)/shard_map/ppermute | solution.py:220
  25.1 3.8 %weights_kernel.1 = (bf16[8,256,256]{2,1,0:T(8,128)(2,1)}, bf16[8,256,256]{2,1,0:T(8,128)(2,1)}) custom-call(bf16[2048,256]{1,0:T(8,128)(2,1)} %embed_ref.1, bf16[256,2048]{1,0:T(8,128)(2,1)} %unpatch_ref.1), custom_call_target="tpu_custom_call" | custom-call | flops 4294967296 | bytes 1048576 | tf_op jit(solution)/shard_map/weights_kernel/pallas_call | solution.py:206
  28.8 0.7 copy.9
  29.5 0.6 copy-done
  30.1 5.6 %front_kernel.1 = (bf16[64,32,128]{2,1,0:T(8,128)(2,1)}, bf16[128,256]{1,0:T(8,128)(2,1)}, bf16[64,16,128]{2,1,0:T(8,128)(2,1)}) custom-call(bf16[64,32,128]{2,1,0:T(8,128)(2,1)} %get-tuple-element.14.map_ref, bf16[32,128]{1,0:T(8,128)(2,1)} %copy-done.3, bf16[32,128]{1,0:T(8,128)(2,1)} %copy-done.2, bf16[4,32,128]{2,1,0:T(8,128)(2,1)} %copy-done.1, ...), custom_call_target="tpu_custom_call" | custom-call | bytes 1048576 | tf_op jit(solution)/shard_map/front_kernel/pallas_call | solution.py:206
  35.8 29.5 %all_to_all.10.packed_ref = bf16[64,16,128]{2,1,0:T(8,128)(2,1)} all-to-all(bf16[64,16,128]{2,1,0:T(8,128)(2,1)} %get-tuple-element.17), channel_id=1, replica_groups=mesh['rows'=64,'cols'=8] {'rows'}, dimensions={0} | all-to-all | bytes 524288 | tf_op jit(solution)/shard_map/all_to_all | solution.py:244
  65.3 4.1 %attention_kernel.1 = bf16[256,128]{1,0:T(8,128)(2,1)} custom-call(bf16[64,16,128]{2,1,0:T(8,128)(2,1)} %all_to_all.10.packed_ref), custom_call_target="tpu_custom_call" | custom-call | bytes 1048576 | tf_op jit(solution)/shard_map/attention_kernel/pallas_call | solution.py:206
  69.4 21.1 %all_to_all.11 = bf16[64,4,128]{2,1,0:T(4,128)(2,1)} all-to-all(bf16[64,4,128]{2,1,0:T(4,128)(2,1)} %bitcast.9), channel_id=1, replica_groups=mesh['rows'=64,'cols'=8] {'rows'}, dimensions={0} | all-to-all | bytes 131072 | tf_op jit(solution)/shard_map/all_to_all | solution.py:248
  90.5 5.3 %merge_kernel.1 = (bf16[64,32,128]{2,1,0:T(8,128)(2,1)}, bf16[32,128]{1,0:T(8,128)(2,1)}) custom-call(bf16[256,128]{1,0:T(8,128)(2,1)} %bitcast.8, bf16[128,256]{1,0:T(8,128)(2,1)} %get-tuple-element.18.tokens_ref, bf16[256,256]{1,0:T(8,128)(2,1)} %out_weight_ref.1, bf16[8,256,256]{2,1,0:T(8,128)(2,1)} %get-tuple-element.19.unpatch_ref, ...), custom_call_target="tpu_custom_call" | custom-call | bytes 1048576 | tf_op jit(solution)/shard_map/merge_kernel/pallas_call | solution.py:206
  95.8 7.7 %collective-permute-start.5 = (bf16[32,128]{1,0:T(8,128)(2,1)}, bf16[32,128]{1,0:T(8,128)(2,1)S(1)}, u32[]{:S(2)}, u32[]{:S(2)}) collective-permute-start(bf16[32,128]{1,0:T(8,128)(2,1)} %get-tuple-element.22), channel_id=1, source_target_pairs={{8,0},{16,8},{24,16},{32,24},{40,32},{48,40},{56,48},{64,56},{72,6... | collective-permute-start | bytes 24584 | tf_op jit(solution)/shard_map/ppermute | solution.py:220
  103.4 1.9 %collective-permute-start.4 = (bf16[32,128]{1,0:T(8,128)(2,1)}, bf16[32,128]{1,0:T(8,128)(2,1)S(1)}, u32[]{:S(2)}, u32[]{:S(2)}) collective-permute-start(bf16[32,128]{1,0:T(8,128)(2,1)} %get-tuple-element.22), channel_id=1, source_target_pairs={{0,8},{8,16},{16,24},{24,32},{32,40},{40,48},{48,56},{56,64},{64,7... | collective-permute-start | bytes 24584 | tf_op jit(solution)/shard_map/ppermute | solution.py:220
  105.3 0.7 fusion
  106.1 9.1 %collective-permute-done.4.low_row = bf16[32,128]{1,0:T(8,128)(2,1)S(1)} collective-permute-done((bf16[32,128]{1,0:T(8,128)(2,1)}, bf16[32,128]{1,0:T(8,128)(2,1)S(1)}, u32[]{:S(2)}, u32[]{:S(2)}) %collective-permute-start.4) | collective-permute-done | bytes 8224 | tf_op jit(solution)/shard_map/ppermute | solution.py:220
  115.8 1.9 %collective-permute-start.7 = (bf16[4,32,128]{2,1,0:T(8,128)(2,1)S(1)}, bf16[4,32,128]{2,1,0:T(8,128)(2,1)S(1)}, u32[]{:S(2)}, u32[]{:S(2)}) collective-permute-start(bf16[4,32,128]{2,1,0:T(8,128)(2,1)S(1)} %pad_maximum_fusion.1), channel_id=1, source_target_pairs={{1,0},{2,1},{3,2},{4,3},{5,4},{6,5},{7,6},{9,8},{10,9},{11,10},{12... | collective-permute-start | bytes 98312 | tf_op jit(solution)/shard_map/ppermute | solution.py:220
  117.7 2.4 %collective-permute-start.6 = (bf16[4,32,128]{2,1,0:T(8,128)(2,1)S(1)}, bf16[4,32,128]{2,1,0:T(8,128)(2,1)S(1)}, u32[]{:S(2)}, u32[]{:S(2)}) collective-permute-start(bf16[4,32,128]{2,1,0:T(8,128)(2,1)S(1)} %pad_maximum_fusion.1), channel_id=1, source_target_pairs={{0,1},{1,2},{2,3},{3,4},{4,5},{5,6},{6,7},{8,9},{9,10},{10,11},{11... | collective-permute-start | bytes 98312 | tf_op jit(solution)/shard_map/ppermute | solution.py:220
  120.1 2.8 %collective-permute-done.6.low_col = bf16[4,32,128]{2,1,0:T(8,128)(2,1)S(1)} collective-permute-done((bf16[4,32,128]{2,1,0:T(8,128)(2,1)S(1)}, bf16[4,32,128]{2,1,0:T(8,128)(2,1)S(1)}, u32[]{:S(2)}, u32[]{:S(2)}) %collective-permute-start.6) | collective-permute-done | bytes 32800 | tf_op jit(solution)/shard_map/ppermute | solution.py:220
  122.9 0.6 copy-done.7
  123.5 3.4 %back_kernel.1 = bf16[32,64,128]{2,1,0:T(8,128)(2,1)} custom-call(bf16[64,32,128]{2,1,0:T(8,128)(2,1)} %get-tuple-element.21.map_ref, bf16[32,128]{1,0:T(8,128)(2,1)} %copy-done.5, bf16[32,128]{1,0:T(8,128)(2,1)} %copy-done.4, bf16[4,32,128]{2,1,0:T(8,128)(2,1)} %copy-done.7, bf16[4,32,128]{2,1,0:T(8,128)(2,1)} %copy-done.6, bf16[32,288]{1,0:T(8,128)(2,1)} %conv_ref.3), custom_call_target="tpu_custom_call" | custom-call | bytes 1048576 | tf_op jit(solution)/shard_map/back_kernel/pallas_call | solution.py:206
  (23 shorter events, 1.2 us)
Async XLA Ops:
  2.2 8.7 %collective-permute-start.1 = (bf16[32,128]{1,0:T(8,128)(2,1)}, bf16[32,128]{1,0:T(8,128)(2,1)S(1)}, u32[]{:S(2)}, u32[]{:S(2)}) collective-permute-start(bf16[32,128]{1,0:T(8,128)(2,1)} %get-tuple-element.15), channel_id=1, source_target_pairs={{8,0},{16,8},{24,16},{32,24},{40,32},{48,40},{56,48},{64,56},{72,6... | collective-permute-start | bytes 24584 | tf_op jit(solution)/shard_map/ppermute | solution.py:220
  8.2 11.8 %collective-permute-start = (bf16[32,128]{1,0:T(8,128)(2,1)}, bf16[32,128]{1,0:T(8,128)(2,1)S(1)}, u32[]{:S(2)}, u32[]{:S(2)}) collective-permute-start(bf16[32,128]{1,0:T(8,128)(2,1)} %get-tuple-element.15), channel_id=1, source_target_pairs={{0,8},{8,16},{16,24},{24,32},{32,40},{40,48},{48,56},{56,64},{64,7... | collective-permute-start | bytes 24584 | tf_op jit(solution)/shard_map/ppermute | solution.py:220
  10.9 9.1 %copy-start.2 = (bf16[32,128]{1,0:T(8,128)(2,1)}, bf16[32,128]{1,0:T(8,128)(2,1)S(1)}, u32[]{:S(2)}) copy-start(bf16[32,128]{1,0:T(8,128)(2,1)S(1)} %collective-permute-done.1.high_row) | copy-start | bytes 24580
  20.0 0.6 copy-start.3
  20.6 8.2 %copy-start.8 = (bf16[16,8,8]{0,2,1:T(8,128)(2,1)S(1)}, bf16[16,8,8]{0,2,1:T(8,128)(2,1)}, u32[]{:S(2)}) copy-start(bf16[16,8,8]{0,2,1:T(8,128)(2,1)} %param.12) | copy-start | bytes 6148
  20.6 8.9 %collective-permute-start.3 = (bf16[4,32,128]{2,1,0:T(8,128)(2,1)S(1)}, bf16[4,32,128]{2,1,0:T(8,128)(2,1)S(1)}, u32[]{:S(2)}, u32[]{:S(2)}) collective-permute-start(bf16[4,32,128]{2,1,0:T(8,128)(2,1)S(1)} %pad_maximum_fusion), channel_id=1, source_target_pairs={{1,0},{2,1},{3,2},{4,3},{5,4},{6,5},{7,6},{9,8},{10,9},{11,10},{12... | collective-permute-start | bytes 98312 | tf_op jit(solution)/shard_map/ppermute | solution.py:220
  22.7 6.9 %collective-permute-start.2 = (bf16[4,32,128]{2,1,0:T(8,128)(2,1)S(1)}, bf16[4,32,128]{2,1,0:T(8,128)(2,1)S(1)}, u32[]{:S(2)}, u32[]{:S(2)}) collective-permute-start(bf16[4,32,128]{2,1,0:T(8,128)(2,1)S(1)} %pad_maximum_fusion), channel_id=1, source_target_pairs={{0,1},{1,2},{2,3},{3,4},{4,5},{5,6},{6,7},{8,9},{9,10},{10,11},{11... | collective-permute-start | bytes 98312 | tf_op jit(solution)/shard_map/ppermute | solution.py:220
  29.5 0.6 copy-start
  29.5 0.6 copy-start.1
  95.8 10.3 %collective-permute-start.5 = (bf16[32,128]{1,0:T(8,128)(2,1)}, bf16[32,128]{1,0:T(8,128)(2,1)S(1)}, u32[]{:S(2)}, u32[]{:S(2)}) collective-permute-start(bf16[32,128]{1,0:T(8,128)(2,1)} %get-tuple-element.22), channel_id=1, source_target_pairs={{8,0},{16,8},{24,16},{32,24},{40,32},{48,40},{56,48},{64,56},{72,6... | collective-permute-start | bytes 24584 | tf_op jit(solution)/shard_map/ppermute | solution.py:220
  103.4 11.8 %collective-permute-start.4 = (bf16[32,128]{1,0:T(8,128)(2,1)}, bf16[32,128]{1,0:T(8,128)(2,1)S(1)}, u32[]{:S(2)}, u32[]{:S(2)}) collective-permute-start(bf16[32,128]{1,0:T(8,128)(2,1)} %get-tuple-element.22), channel_id=1, source_target_pairs={{0,8},{8,16},{16,24},{24,32},{32,40},{40,48},{48,56},{56,64},{64,7... | collective-permute-start | bytes 24584 | tf_op jit(solution)/shard_map/ppermute | solution.py:220
  106.1 9.1 %copy-start.4 = (bf16[32,128]{1,0:T(8,128)(2,1)}, bf16[32,128]{1,0:T(8,128)(2,1)S(1)}, u32[]{:S(2)}) copy-start(bf16[32,128]{1,0:T(8,128)(2,1)S(1)} %collective-permute-done.5.high_row) | copy-start | bytes 24580
  115.2 0.6 copy-start.5
  115.8 4.3 %collective-permute-start.7 = (bf16[4,32,128]{2,1,0:T(8,128)(2,1)S(1)}, bf16[4,32,128]{2,1,0:T(8,128)(2,1)S(1)}, u32[]{:S(2)}, u32[]{:S(2)}) collective-permute-start(bf16[4,32,128]{2,1,0:T(8,128)(2,1)S(1)} %pad_maximum_fusion.1), channel_id=1, source_target_pairs={{1,0},{2,1},{3,2},{4,3},{5,4},{6,5},{7,6},{9,8},{10,9},{11,10},{12... | collective-permute-start | bytes 98312 | tf_op jit(solution)/shard_map/ppermute | solution.py:220
  117.7 5.2 %collective-permute-start.6 = (bf16[4,32,128]{2,1,0:T(8,128)(2,1)S(1)}, bf16[4,32,128]{2,1,0:T(8,128)(2,1)S(1)}, u32[]{:S(2)}, u32[]{:S(2)}) collective-permute-start(bf16[4,32,128]{2,1,0:T(8,128)(2,1)S(1)} %pad_maximum_fusion.1), channel_id=1, source_target_pairs={{0,1},{1,2},{2,3},{3,4},{4,5},{5,6},{6,7},{8,9},{9,10},{10,11},{11... | collective-permute-start | bytes 98312 | tf_op jit(solution)/shard_map/ppermute | solution.py:220
  120.1 2.8 %copy-start.6 = (bf16[4,32,128]{2,1,0:T(8,128)(2,1)}, bf16[4,32,128]{2,1,0:T(8,128)(2,1)S(1)}, u32[]{:S(2)}) copy-start(bf16[4,32,128]{2,1,0:T(8,128)(2,1)S(1)} %collective-permute-done.7.high_col) | copy-start | bytes 98308
  122.9 0.6 copy-start.7

commit v2 on v1

--- a/solution.py
+++ b/solution.py
@@ -44,9 +44,11 @@
     edges_ref[...] = edges.astype(bf16)
 
 
-def turn_kernel(x_ref, turned_ref, edges_ref, turned_f32):
+def turn_kernel(x_ref, turned_ref, edges_ref, ends_ref, turned_f32):
     turned_f32[...] = jnp.swapaxes(x_ref[...].astype(f32), 0, 1)
     turned_ref[...] = turned_f32[...].astype(bf16)
+    ends_ref[0] = turned_ref[0]
+    ends_ref[1] = turned_ref[W - 1]
     column_edges(lambda w: turned_f32[w], edges_ref)
 
 
@@ -125,11 +127,12 @@
     spread = jnp.mean(centered * centered, axis=1, keepdims=True)
     normed = (centered * lax.rsqrt(spread + epsilon)).astype(bf16)
     projected = jnp.dot(normed, qkv_ref[...], preferred_element_type=f32)
-    bias = bias_ref[...].astype(f32)
+    bias = bias_ref[...].astype(f32).reshape(PC * HEADS, PR).T
     filler = jnp.zeros((PR * PC, L - 3 * HEAD_DIM - 1), f32)
     for h in range(HEADS):
         pieces = [projected[:, g * D + h * HEAD_DIM : g * D + (h + 1) * HEAD_DIM] for g in range(3)]
-        tile = jnp.concatenate(pieces + [bias[:, h : h + 1], filler], axis=1).astype(bf16)
+        column = [bias[:, p * HEADS + h : p * HEADS + h + 1] for p in range(PC)]
+        tile = jnp.concatenate(pieces + [jnp.concatenate(column, axis=0), filler], axis=1).astype(bf16)
         for p in range(PC):
             packed_ref[p * HEADS + h] = tile[p * PR : (p + 1) * PR]
 
@@ -158,7 +161,7 @@
 
 def merge_kernel(
     returned_ref, tokens_ref, out_weight_ref, unpatch_ref, mixed_ref,
-    merged_ref, edges_ref, returned_f32, rows_f32, repeated,
+    merged_ref, edges_ref, ends_ref, returned_f32, rows_f32, repeated,
 ):
     returned_f32[...] = returned_ref[...].astype(f32)
     for low in range(4):
@@ -184,6 +187,8 @@
             grown = grown + lax.dot_general(unpatch_ref[i], part, NT, preferred_element_type=f32)
         cells = mixed_ref[p * PATCH : (p + 1) * PATCH].astype(f32) + grown.reshape(PATCH, C, L)
         merged_ref[p * PATCH : (p + 1) * PATCH] = cells.astype(bf16)
+    ends_ref[0] = merged_ref[0]
+    ends_ref[1] = merged_ref[W - 1]
     column_edges(lambda w: merged_ref[w].astype(f32), edges_ref)
 
 
@@ -199,18 +204,19 @@
 
 
 def shape(*dims, dtype=bf16):
-    return jax.ShapeDtypeStruct(dims, dtype)
+    return pltpu.VMEM(dims, dtype)
 
 
 def call(kernel, outs, scratch, *args, flops=0):
     return pl.pallas_call(
         kernel,
         out_shape=outs,
+        in_specs=[pl.BlockSpec(memory_space=pltpu.VMEM)] * len(args),
         scratch_shapes=scratch,
         name=kernel.__name__,
         cost_estimate=pl.CostEstimate(flops=flops, transcendentals=0, bytes_accessed=1 << 20),
-        compiler_params=pltpu.CompilerParams(vmem_limit_bytes=56 << 20),
-    )(*args)
+        compiler_params=pltpu.CompilerParams(vmem_limit_bytes=24 << 20),
+    )(*(pltpu.with_memory_space_constraint(x, pltpu.VMEM) for x in args))
 
 
 def exchange(block, axis):
@@ -220,26 +226,26 @@
     return lax.ppermute(block, axis, forward), lax.ppermute(block, axis, backward)
 
 
-def rims(turned, edges):
-    low_row, high_row = exchange(edges, "rows")
-    strip = jnp.stack([turned[0], turned[W - 1], low_row, high_row])
+def rims(ends, edges, *ready):
+    low_row, high_row, *ready = lax.optimization_barrier((*exchange(edges, "rows"), *ready))
+    strip = jnp.concatenate([ends, low_row[None], high_row[None]])
     low_col, high_col = exchange(strip, "cols")
-    return low_row, high_row, low_col, high_col
+    return low_row, high_row, low_col, high_col, *ready
 
 
 def per_device(pair_map, conv_in, embed_weight, qkv_weight, key_bias, out_weight, unpatch, conv_out):
-    turned, edges = call(
-        turn_kernel, (shape(W, C, L), shape(C, L)), [pltpu.VMEM((W, C, L), f32)], pair_map
+    turned, edges, ends = call(
+        turn_kernel, (shape(W, C, L), shape(C, L), shape(2, C, L)), [pltpu.VMEM((W, C, L), f32)], pair_map
     )
     embed_rows, unpatch_rows = call(
         weights_kernel, (shape(PATCH, D, D), shape(PATCH, D, D)), [], embed_weight, unpatch, flops=1 << 32
     )
-    bias = key_bias.transpose(1, 0, 2).reshape(PR * PC, HEADS)
+    *borders, embed_rows, unpatch_rows = rims(ends, edges, embed_rows, unpatch_rows)
     mixed, tokens, packed = call(
         front_kernel,
         (shape(W, C, L), shape(PR * PC, D), shape(GROUPS, PR, L)),
         [pltpu.VMEM((W + 2, 3 * C, L), bf16), pltpu.VMEM((PR * PC, PATCH * D), bf16)],
-        turned, *rims(turned, edges), conv_in, embed_rows, qkv_weight, bias,
+        turned, *borders, conv_in, embed_rows, qkv_weight, key_bias.transpose(1, 2, 0),
     )
     arrived = lax.all_to_all(packed, "rows", split_axis=0, concat_axis=0, tiled=True)
     heads_out = call(
@@ -248,17 +254,17 @@
     returned = lax.all_to_all(
         heads_out.reshape(GROUPS, 4, L), "rows", split_axis=0, concat_axis=0, tiled=True
     ).reshape(GROUPS * 4, L)
-    merged, edges = call(
+    merged, edges, ends = call(
         merge_kernel,
-        (shape(W, C, L), shape(C, L)),
+        (shape(W, C, L), shape(C, L), shape(2, C, L)),
         [pltpu.VMEM((GROUPS * 4, L), f32), pltpu.VMEM((PR * PC, D), f32), pltpu.VMEM((PC * L, D), f32)],
         returned, tokens, out_weight, unpatch_rows, mixed,
     )
     return call(
         back_kernel,
-        shape(C, W, L),
+        jax.ShapeDtypeStruct((C, W, L), bf16),
         [pltpu.VMEM((W + 2, 3 * C, L), bf16), pltpu.VMEM((W, C, L), f32)],
-        merged, *rims(merged, edges), conv_out,
+        merged, *rims(ends, edges), conv_out,
     )
 
 

time: 128 us -> 113 us (0.88)
  Pallas kernels: 24.4 us -> 13.1 us
  blocking collectives: 50.6 us -> 48.1 us
    pallas_call x6, Pallas kernels: 24.4 us -> 13.1 us  [call(): pl.pallas_call(kernel, out_shape=outs, in_specs=[pl.BlockSpec(memory_spac...]
    all_to_all x1, blocking collectives: 21.1 us -> 19.6 us  [per_device(): lax.all_to_all(heads_out.reshape(GROUPS, 4, L), 'rows', split_axis=0, con...]
    slice x2 -> x0, local copies, waits for them, and re-layouts: 1.44 us -> none  [rims(): strip = jnp.stack([turned[0], turned[W - 1], low_row, high_row])]
    unnamed x18 -> x16, local copies, waits for them, and re-layouts: 2.37 us -> 3.51 us
  transfers between devices with their start and end apart: 8 -> 8, of which waited for: 3 -> 4; matrix products, arithmetic and copies ran while one was open for 2% -> 0% of each run, Pallas kernels for 3% -> 1%
where the time goes in v2:
time: 113 us
  blocking collectives  48.1 us (43%)
  starting transfers between devices  26.4 us (23%)
  waiting for transfers between devices  21.2 us (19%)
  Pallas kernels  13.1 us (12%)
  local copies, waits for them, and re-layouts  3.51 us (3%)
    all_to_all x1, blocking collectives, per_device(): lax.all_to_all(packed, 'rows', split_axis=0, concat_axis=0, tiled=True)  28.5 us
    ppermute x4, waiting for transfers between devices, exchange(): lax.ppermute(block, axis, forward)  21.2 us
    all_to_all x1, blocking collectives, per_device(): lax.all_to_all(heads_out.reshape(GROUPS, 4, L), 'rows', split_axis=0, con...  19.6 us
    ppermute x4, starting transfers between devices, exchange(): lax.ppermute(block, axis, backward)  17.8 us
    pallas_call x6, Pallas kernels, call(): pl.pallas_call(kernel, out_shape=outs, in_specs=[pl.BlockSpec(memory_spac...  13.1 us
    ppermute x4, starting transfers between devices, exchange(): lax.ppermute(block, axis, forward)  8.65 us
    unnamed x16, local copies, waits for them, and re-layouts  3.51 us
  transfers between devices with their start and end apart: 8, of which 4 were waited for; matrix products, arithmetic and copies ran while one was open for 0% of the time, Pallas kernels for 1%

profile of v2, /device:TPU:48, one launch (start us, length us, event | category | flops | bytes accessed | tf_op | source)
XLA Modules:
  0.0 112.5 jit_solution(1276311761044826572)
XLA Ops:
  0.0 1.0 copy-done
  1.0 0.5 turn_kernel.1
  1.5 0.0 copy-start.1
  1.5 6.1 %collective-permute-start.1 = (bf16[32,128]{1,0:T(8,128)(2,1)S(1)}, bf16[32,128]{1,0:T(8,128)(2,1)S(1)}, u32[]{:S(2)}, u32[]{:S(2)}) collective-permute-start(bf16[32,128]{1,0:T(8,128)(2,1)S(1)} %get-tuple-element.23), channel_id=1, source_target_pairs={{8,0},{16,8},{24,16},{32,24},{40,32},{48,40},{56,48},{64,56},{72,6... | collective-permute-start | bytes 24584 | tf_op jit(solution)/shard_map/ppermute | solution.py:226
  7.7 1.9 %collective-permute-start = (bf16[32,128]{1,0:T(8,128)(2,1)S(1)}, bf16[32,128]{1,0:T(8,128)(2,1)S(1)}, u32[]{:S(2)}, u32[]{:S(2)}) collective-permute-start(bf16[32,128]{1,0:T(8,128)(2,1)S(1)} %get-tuple-element.23), channel_id=1, source_target_pairs={{0,8},{8,16},{16,24},{24,32},{32,40},{40,48},{48,56},{56,64},{64,7... | collective-permute-start | bytes 24584 | tf_op jit(solution)/shard_map/ppermute | solution.py:226
  9.6 1.2 %copy-done.6 = bf16[2048,256]{1,0:T(8,128)(2,1)S(1)} copy-done((bf16[2048,256]{1,0:T(8,128)(2,1)S(1)}, bf16[2048,256]{1,0:T(8,128)(2,1)}, u32[]{:S(2)}) %copy-start.6) | copy-done | bytes 1048600
  10.8 1.2 %copy-done.7 = bf16[256,2048]{1,0:T(8,128)(2,1)S(1)} copy-done((bf16[256,2048]{1,0:T(8,128)(2,1)S(1)}, bf16[256,2048]{1,0:T(8,128)(2,1)}, u32[]{:S(2)}) %copy-start.7) | copy-done | bytes 1048600
  12.1 1.2 %weights_kernel.1 = (bf16[8,256,256]{2,1,0:T(8,128)(2,1)S(1)}, bf16[8,256,256]{2,1,0:T(8,128)(2,1)S(1)}) custom-call(bf16[2048,256]{1,0:T(8,128)(2,1)S(1)} %copy-done.6, bf16[256,2048]{1,0:T(8,128)(2,1)S(1)} %copy-done.7), custom_call_target="tpu_custom_call" | custom-call | flops 4294967296 | bytes 1048576 | tf_op jit(solution)/shard_map/weights_kernel/pallas_call | solution.py:211
  13.3 5.9 %collective-permute-done.low_row = bf16[32,128]{1,0:T(8,128)(2,1)S(1)} collective-permute-done((bf16[32,128]{1,0:T(8,128)(2,1)S(1)}, bf16[32,128]{1,0:T(8,128)(2,1)S(1)}, u32[]{:S(2)}, u32[]{:S(2)}) %collective-permute-start) | collective-permute-done | bytes 8224 | tf_op jit(solution)/shard_map/ppermute | solution.py:226
  19.3 2.1 %collective-permute-start.3 = (bf16[4,32,128]{2,1,0:T(8,128)(2,1)S(1)}, bf16[4,32,128]{2,1,0:T(8,128)(2,1)S(1)}, u32[]{:S(2)}, u32[]{:S(2)}) collective-permute-start(bf16[4,32,128]{2,1,0:T(8,128)(2,1)S(1)} %pad_maximum_fusion), channel_id=1, source_target_pairs={{1,0},{2,1},{3,2},{4,3},{5,4},{6,5},{7,6},{9,8},{10,9},{11,10},{12... | collective-permute-start | bytes 98312 | tf_op jit(solution)/shard_map/ppermute | solution.py:226
  21.3 2.4 %collective-permute-start.2 = (bf16[4,32,128]{2,1,0:T(8,128)(2,1)S(1)}, bf16[4,32,128]{2,1,0:T(8,128)(2,1)S(1)}, u32[]{:S(2)}, u32[]{:S(2)}) collective-permute-start(bf16[4,32,128]{2,1,0:T(8,128)(2,1)S(1)} %pad_maximum_fusion), channel_id=1, source_target_pairs={{0,1},{1,2},{2,3},{3,4},{4,5},{5,6},{6,7},{8,9},{9,10},{10,11},{11... | collective-permute-start | bytes 98312 | tf_op jit(solution)/shard_map/ppermute | solution.py:226
  23.7 2.8 %collective-permute-done.2.low_col = bf16[4,32,128]{2,1,0:T(8,128)(2,1)S(1)} collective-permute-done((bf16[4,32,128]{2,1,0:T(8,128)(2,1)S(1)}, bf16[4,32,128]{2,1,0:T(8,128)(2,1)S(1)}, u32[]{:S(2)}, u32[]{:S(2)}) %collective-permute-start.2) | collective-permute-done | bytes 32800 | tf_op jit(solution)/shard_map/ppermute | solution.py:226
  26.6 3.5 %front_kernel.1 = (bf16[64,32,128]{2,1,0:T(8,128)(2,1)S(1)}, bf16[128,256]{1,0:T(8,128)(2,1)S(1)}, bf16[64,16,128]{2,1,0:T(8,128)(2,1)S(1)}) custom-call(bf16[64,32,128]{2,1,0:T(8,128)(2,1)S(1)} %get-tuple-element.22.map_ref, bf16[32,128]{1,0:T(8,128)(2,1)S(1)} %collective-permute-done.low_row, bf16[32,128]{1,0:T(8,128)(2,1)S(1)} %collective-permute-done.1.high_row, ...), custom_call_target="tpu_custom_call" | custom-call | bytes 1048576 | tf_op jit(solution)/shard_map/front_kernel/pallas_call | solution.py:211
  30.1 28.5 %all_to_all.10.packed_ref = bf16[64,16,128]{2,1,0:T(8,128)(2,1)S(1)} all-to-all(bf16[64,16,128]{2,1,0:T(8,128)(2,1)S(1)} %get-tuple-element.30), channel_id=1, replica_groups=mesh['rows'=64,'cols'=8] {'rows'}, dimensions={0} | all-to-all | bytes 524288 | tf_op jit(solution)/shard_map/all_to_all | solution.py:250
  58.6 2.5 %attention_kernel.1 = bf16[256,128]{1,0:T(8,128)(2,1)S(1)} custom-call(bf16[64,16,128]{2,1,0:T(8,128)(2,1)S(1)} %all_to_all.10.packed_ref), custom_call_target="tpu_custom_call" | custom-call | bytes 1048576 | tf_op jit(solution)/shard_map/attention_kernel/pallas_call | solution.py:211
  61.1 19.6 %all_to_all.11 = bf16[64,4,128]{2,1,0:T(4,128)(2,1)S(1)} all-to-all(bf16[64,4,128]{2,1,0:T(4,128)(2,1)S(1)} %bitcast.8), channel_id=1, replica_groups=mesh['rows'=64,'cols'=8] {'rows'}, dimensions={0} | all-to-all | bytes 131072 | tf_op jit(solution)/shard_map/all_to_all | solution.py:254
  80.7 3.1 %merge_kernel.1 = (bf16[64,32,128]{2,1,0:T(8,128)(2,1)S(1)}, bf16[32,128]{1,0:T(8,128)(2,1)S(1)}, bf16[2,32,128]{2,1,0:T(8,128)(2,1)S(1)}) custom-call(bf16[256,128]{1,0:T(8,128)(2,1)S(1)} %bitcast.7, bf16[128,256]{1,0:T(8,128)(2,1)S(1)} %get-tuple-element.31.tokens_ref, bf16[256,256]{1,0:T(8,128)(2,1)S(1)} %copy-done.2, ...), custom_call_target="tpu_custom_call" | custom-call | bytes 1048576 | tf_op jit(solution)/shard_map/merge_kernel/pallas_call | solution.py:211
  83.8 7.6 %collective-permute-start.5 = (bf16[32,128]{1,0:T(8,128)(2,1)S(1)}, bf16[32,128]{1,0:T(8,128)(2,1)S(1)}, u32[]{:S(2)}, u32[]{:S(2)}) collective-permute-start(bf16[32,128]{1,0:T(8,128)(2,1)S(1)} %get-tuple-element.35), channel_id=1, source_target_pairs={{8,0},{16,8},{24,16},{32,24},{40,32},{48,40},{56,48},{64,56},{72,6... | collective-permute-start | bytes 24584 | tf_op jit(solution)/shard_map/ppermute | solution.py:226
  91.5 1.9 %collective-permute-start.4 = (bf16[32,128]{1,0:T(8,128)(2,1)S(1)}, bf16[32,128]{1,0:T(8,128)(2,1)S(1)}, u32[]{:S(2)}, u32[]{:S(2)}) collective-permute-start(bf16[32,128]{1,0:T(8,128)(2,1)S(1)} %get-tuple-element.35), channel_id=1, source_target_pairs={{0,8},{8,16},{16,24},{24,32},{32,40},{40,48},{48,56},{56,64},{64,7... | collective-permute-start | bytes 24584 | tf_op jit(solution)/shard_map/ppermute | solution.py:226
  93.4 9.6 %collective-permute-done.4.low_row = bf16[32,128]{1,0:T(8,128)(2,1)S(1)} collective-permute-done((bf16[32,128]{1,0:T(8,128)(2,1)S(1)}, bf16[32,128]{1,0:T(8,128)(2,1)S(1)}, u32[]{:S(2)}, u32[]{:S(2)}) %collective-permute-start.4) | collective-permute-done | bytes 8224 | tf_op jit(solution)/shard_map/ppermute | solution.py:226
  103.0 1.9 %collective-permute-start.7 = (bf16[4,32,128]{2,1,0:T(8,128)(2,1)S(1)}, bf16[4,32,128]{2,1,0:T(8,128)(2,1)S(1)}, u32[]{:S(2)}, u32[]{:S(2)}) collective-permute-start(bf16[4,32,128]{2,1,0:T(8,128)(2,1)S(1)} %pad_maximum_fusion.1), channel_id=1, source_target_pairs={{1,0},{2,1},{3,2},{4,3},{5,4},{6,5},{7,6},{9,8},{10,9},{11,10},{12... | collective-permute-start | bytes 98312 | tf_op jit(solution)/shard_map/ppermute | solution.py:226
  105.0 2.4 %collective-permute-start.6 = (bf16[4,32,128]{2,1,0:T(8,128)(2,1)S(1)}, bf16[4,32,128]{2,1,0:T(8,128)(2,1)S(1)}, u32[]{:S(2)}, u32[]{:S(2)}) collective-permute-start(bf16[4,32,128]{2,1,0:T(8,128)(2,1)S(1)} %pad_maximum_fusion.1), channel_id=1, source_target_pairs={{0,1},{1,2},{2,3},{3,4},{4,5},{5,6},{6,7},{8,9},{9,10},{10,11},{11... | collective-permute-start | bytes 98312 | tf_op jit(solution)/shard_map/ppermute | solution.py:226
  107.4 2.8 %collective-permute-done.6.low_col = bf16[4,32,128]{2,1,0:T(8,128)(2,1)S(1)} collective-permute-done((bf16[4,32,128]{2,1,0:T(8,128)(2,1)S(1)}, bf16[4,32,128]{2,1,0:T(8,128)(2,1)S(1)}, u32[]{:S(2)}, u32[]{:S(2)}) %collective-permute-start.6) | collective-permute-done | bytes 32800 | tf_op jit(solution)/shard_map/ppermute | solution.py:226
  110.2 2.3 %back_kernel.1 = bf16[32,64,128]{2,1,0:T(8,128)(2,1)} custom-call(bf16[64,32,128]{2,1,0:T(8,128)(2,1)S(1)} %get-tuple-element.34.map_ref, bf16[32,128]{1,0:T(8,128)(2,1)S(1)} %collective-permute-done.4.low_row, bf16[32,128]{1,0:T(8,128)(2,1)S(1)} %collective-permute-done.5.high_row, bf16[4,32,128]{2,1,0:T(8,128)(2,1)S(1)} %collective-permute-done.6.low_col, ...), custom_call_target="tpu_custom_call" | custom-call | bytes 1048576 | tf_op jit(solution)/shard_map/back_kernel/pallas_call | solution.py:211
  (18 shorter events, 0.1 us)
Async XLA Ops:
  0.0 1.0 copy-start
  1.5 25.0 %copy-start.1 = (bf16[256,768]{1,0:T(8,128)(2,1)S(1)}, bf16[256,768]{1,0:T(8,128)(2,1)}, u32[]{:S(2)}) copy-start(bf16[256,768]{1,0:T(8,128)(2,1)} %qkv_ref.1) | copy-start | bytes 1179652
  1.5 11.8 %collective-permute-start.1 = (bf16[32,128]{1,0:T(8,128)(2,1)S(1)}, bf16[32,128]{1,0:T(8,128)(2,1)S(1)}, u32[]{:S(2)}, u32[]{:S(2)}) collective-permute-start(bf16[32,128]{1,0:T(8,128)(2,1)S(1)} %get-tuple-element.23), channel_id=1, source_target_pairs={{8,0},{16,8},{24,16},{32,24},{40,32},{48,40},{56,48},{64,56},{72,6... | collective-permute-start | bytes 24584 | tf_op jit(solution)/shard_map/ppermute | solution.py:226
  7.7 11.6 %collective-permute-start = (bf16[32,128]{1,0:T(8,128)(2,1)S(1)}, bf16[32,128]{1,0:T(8,128)(2,1)S(1)}, u32[]{:S(2)}, u32[]{:S(2)}) collective-permute-start(bf16[32,128]{1,0:T(8,128)(2,1)S(1)} %get-tuple-element.23), channel_id=1, source_target_pairs={{0,8},{8,16},{16,24},{24,32},{32,40},{40,48},{48,56},{56,64},{64,7... | collective-permute-start | bytes 24584 | tf_op jit(solution)/shard_map/ppermute | solution.py:226
  9.6 1.2 %copy-start.6 = (bf16[2048,256]{1,0:T(8,128)(2,1)S(1)}, bf16[2048,256]{1,0:T(8,128)(2,1)}, u32[]{:S(2)}) copy-start(bf16[2048,256]{1,0:T(8,128)(2,1)} %embed_ref.1) | copy-start | bytes 3145732
  10.8 1.2 %copy-start.7 = (bf16[256,2048]{1,0:T(8,128)(2,1)S(1)}, bf16[256,2048]{1,0:T(8,128)(2,1)}, u32[]{:S(2)}) copy-start(bf16[256,2048]{1,0:T(8,128)(2,1)} %unpatch_ref.1) | copy-start | bytes 3145732
  19.2 7.3 %copy-start.3 = (bf16[32,288]{1,0:T(8,128)(2,1)S(1)}, bf16[32,288]{1,0:T(8,128)(2,1)}, u32[]{:S(2)}) copy-start(bf16[32,288]{1,0:T(8,128)(2,1)} %conv_ref.2) | copy-start | bytes 55300
  19.2 7.3 %copy-start.5 = (bf16[16,8,8]{0,2,1:T(8,128)(2,1)S(1)}, bf16[16,8,8]{0,2,1:T(8,128)(2,1)}, u32[]{:S(2)}) copy-start(bf16[16,8,8]{0,2,1:T(8,128)(2,1)} %param.12) | copy-start | bytes 6148
  19.3 4.5 %collective-permute-start.3 = (bf16[4,32,128]{2,1,0:T(8,128)(2,1)S(1)}, bf16[4,32,128]{2,1,0:T(8,128)(2,1)S(1)}, u32[]{:S(2)}, u32[]{:S(2)}) collective-permute-start(bf16[4,32,128]{2,1,0:T(8,128)(2,1)S(1)} %pad_maximum_fusion), channel_id=1, source_target_pairs={{1,0},{2,1},{3,2},{4,3},{5,4},{6,5},{7,6},{9,8},{10,9},{11,10},{12... | collective-permute-start | bytes 98312 | tf_op jit(solution)/shard_map/ppermute | solution.py:226
  21.3 5.2 %collective-permute-start.2 = (bf16[4,32,128]{2,1,0:T(8,128)(2,1)S(1)}, bf16[4,32,128]{2,1,0:T(8,128)(2,1)S(1)}, u32[]{:S(2)}, u32[]{:S(2)}) collective-permute-start(bf16[4,32,128]{2,1,0:T(8,128)(2,1)S(1)} %pad_maximum_fusion), channel_id=1, source_target_pairs={{0,1},{1,2},{2,3},{3,4},{4,5},{5,6},{6,7},{8,9},{9,10},{10,11},{11... | collective-permute-start | bytes 98312 | tf_op jit(solution)/shard_map/ppermute | solution.py:226
  61.1 19.6 %copy-start.2 = (bf16[256,256]{1,0:T(8,128)(2,1)S(1)}, bf16[256,256]{1,0:T(8,128)(2,1)}, u32[]{:S(2)}) copy-start(bf16[256,256]{1,0:T(8,128)(2,1)} %out_weight_ref.1) | copy-start | bytes 393220
  83.8 9.6 %collective-permute-start.5 = (bf16[32,128]{1,0:T(8,128)(2,1)S(1)}, bf16[32,128]{1,0:T(8,128)(2,1)S(1)}, u32[]{:S(2)}, u32[]{:S(2)}) collective-permute-start(bf16[32,128]{1,0:T(8,128)(2,1)S(1)} %get-tuple-element.35), channel_id=1, source_target_pairs={{8,0},{16,8},{24,16},{32,24},{40,32},{48,40},{56,48},{64,56},{72,6... | collective-permute-start | bytes 24584 | tf_op jit(solution)/shard_map/ppermute | solution.py:226
  91.5 11.6 %collective-permute-start.4 = (bf16[32,128]{1,0:T(8,128)(2,1)S(1)}, bf16[32,128]{1,0:T(8,128)(2,1)S(1)}, u32[]{:S(2)}, u32[]{:S(2)}) collective-permute-start(bf16[32,128]{1,0:T(8,128)(2,1)S(1)} %get-tuple-element.35), channel_id=1, source_target_pairs={{0,8},{8,16},{16,24},{24,32},{32,40},{40,48},{48,56},{56,64},{64,7... | collective-permute-start | bytes 24584 | tf_op jit(solution)/shard_map/ppermute | solution.py:226
  103.0 7.2 %copy-start.4 = (bf16[32,288]{1,0:T(8,128)(2,1)S(1)}, bf16[32,288]{1,0:T(8,128)(2,1)}, u32[]{:S(2)}) copy-start(bf16[32,288]{1,0:T(8,128)(2,1)} %conv_ref.3) | copy-start | bytes 55300
  103.0 4.3 %collective-permute-start.7 = (bf16[4,32,128]{2,1,0:T(8,128)(2,1)S(1)}, bf16[4,32,128]{2,1,0:T(8,128)(2,1)S(1)}, u32[]{:S(2)}, u32[]{:S(2)}) collective-permute-start(bf16[4,32,128]{2,1,0:T(8,128)(2,1)S(1)} %pad_maximum_fusion.1), channel_id=1, source_target_pairs={{1,0},{2,1},{3,2},{4,3},{5,4},{6,5},{7,6},{9,8},{10,9},{11,10},{12... | collective-permute-start | bytes 98312 | tf_op jit(solution)/shard_map/ppermute | solution.py:226
  105.0 5.2 %collective-permute-start.6 = (bf16[4,32,128]{2,1,0:T(8,128)(2,1)S(1)}, bf16[4,32,128]{2,1,0:T(8,128)(2,1)S(1)}, u32[]{:S(2)}, u32[]{:S(2)}) collective-permute-start(bf16[4,32,128]{2,1,0:T(8,128)(2,1)S(1)} %pad_maximum_fusion.1), channel_id=1, source_target_pairs={{0,1},{1,2},{2,3},{3,4},{4,5},{5,6},{6,7},{8,9},{9,10},{10,11},{11... | collective-permute-start | bytes 98312 | tf_op jit(solution)/shard_map/ppermute | solution.py:226

commit v3 on v2

--- a/solution.py
+++ b/solution.py
@@ -16,6 +16,9 @@
 PR = L // PATCH
 GROUPS = 64
 SEQ = GROUPS * PR
+OWN = PR * PC
+WIDE = OWN + 2 * PC
+WINDOW = 8
 QUAD = 4
 epsilon = 1e-05
 
@@ -60,20 +63,19 @@
                 target[i, j * C : (j + 1) * C, :] = turned[j * PATCH + i].astype(bf16)
 
 
-def fill_taps(map_ref, low_row, high_row, low_col, high_col, taps):
+def fill_taps(map_ref, strip, low_strip, high_strip, taps):
     lane = iota((C, L), 1)
-    row_low = low_row[...].astype(f32)
-    row_high = high_row[...].astype(f32)
-    below = [low_col[n].astype(f32) for n in range(4)]
-    above = [high_col[n].astype(f32) for n in range(4)]
+    outer = strip[2].astype(f32)
+    below = [low_strip[n].astype(f32) for n in range(3)]
+    above = [high_strip[n].astype(f32) for n in range(3)]
     for w in range(-1, W + 1):
         if w < 0:
-            slab, left, right = below[1], below[2][:, L - 1 : L], below[3][:, W - 1 : W]
+            slab, left, right = below[1], below[2][:, L - 1 : L], below[2][:, W - 1 : W]
         elif w == W:
-            slab, left, right = above[0], above[2][:, W : W + 1], above[3][:, 0:1]
+            slab, left, right = above[0], above[2][:, W : W + 1], above[2][:, 0:1]
         else:
             slab = map_ref[w].astype(f32)
-            left, right = row_low[:, W + w : W + w + 1], row_high[:, w : w + 1]
+            left, right = outer[:, W + w : W + w + 1], outer[:, w : w + 1]
         taps[w + 1, 0:C, :] = jnp.where(lane == 0, left, pltpu.roll(slab, 1, 1)).astype(bf16)
         taps[w + 1, C : 2 * C, :] = slab.astype(bf16)
         taps[w + 1, 2 * C : 3 * C, :] = jnp.where(lane == L - 1, right, pltpu.roll(slab, L - 1, 1)).astype(bf16)
@@ -98,10 +100,10 @@
 
 
 def front_kernel(
-    map_ref, low_row, high_row, low_col, high_col, conv_ref, embed_ref, qkv_ref, bias_ref,
-    mixed_ref, tokens_ref, packed_ref, taps, gathered,
+    map_ref, strip_ref, low_strip, high_strip, conv_ref, embed_ref, qkv_ref, bias_ref,
+    mixed_ref, tokens_ref, packed_ref, rim_ref, taps, gathered, tokens_f32, rim_f32,
 ):
-    fill_taps(map_ref, low_row, high_row, low_col, high_col, taps)
+    fill_taps(map_ref, strip_ref, low_strip, high_strip, taps)
     band = banded(conv_ref[...])
     row = iota((L, L), 0)
     select = one_hot(iota((L, L), 1) == (row % PR) * PATCH + row // PR)
@@ -123,6 +125,13 @@
     ).astype(bf16)
     tokens_ref[...] = tokens
     values = tokens.astype(f32)
+    for half in range(2):
+        tokens_f32[...] = values[:, half * L : (half + 1) * L]
+        for n, r in enumerate((0, PR - 1)):
+            at = (2 * half + n) * PC
+            rim_f32[at : at + PC, :] = tokens_f32[pl.ds(r, PC, stride=PR), :]
+    rim_ref[1] = rim_f32[...].astype(bf16)
+    column_edges(lambda w: mixed_ref[w].astype(f32), rim_ref.at[0])
     centered = values - jnp.mean(values, axis=1, keepdims=True)
     spread = jnp.mean(centered * centered, axis=1, keepdims=True)
     normed = (centered * lax.rsqrt(spread + epsilon)).astype(bf16)
@@ -137,7 +146,7 @@
             packed_ref[p * HEADS + h] = tile[p * PR : (p + 1) * PR]
 
 
-def attention_kernel(packed_ref, out_ref, rows_f32):
+def attention_kernel(packed_ref, out_ref, rows_f32, padded, windows):
     rows = packed_ref[...].reshape(SEQ, L)
     lane = iota((SEQ, L), 1)
     wide = rows.astype(f32)
@@ -156,27 +165,59 @@
         shift = (quarter * HEAD_DIM - 2 * HEAD_DIM) % L
         placed = (pltpu.roll(values, shift, 1) if shift else values).astype(bf16)
         total = total + jnp.dot(share, placed, preferred_element_type=f32)
-    out_ref[...] = total.astype(bf16)
+    pad = jnp.zeros((8, L), f32)
+    padded[0:8, :] = pad
+    padded[8 : 8 + SEQ // 4, :] = total
+    padded[8 + SEQ // 4 :, :] = pad
+    for n in range(WINDOW):
+        start = 7 + min(n, 5)
+        windows[pl.ds(n, GROUPS, stride=WINDOW), :] = padded[pl.ds(start, GROUPS, stride=4), :]
+    out_ref[...] = windows[...].reshape(GROUPS, WINDOW, L).astype(bf16)
 
 
 def merge_kernel(
-    returned_ref, tokens_ref, out_weight_ref, unpatch_ref, mixed_ref,
-    merged_ref, edges_ref, ends_ref, returned_f32, rows_f32, repeated,
+    returned_ref, tokens_ref, low_rim, high_rim, out_weight_ref, unpatch_ref, mixed_ref,
+    merged_ref, strip_ref, returned_f32, rows_f32, repeated,
 ):
-    returned_f32[...] = returned_ref[...].astype(f32)
-    for low in range(4):
-        heads = [returned_f32[pl.ds(h * 4 + low, PC, stride=HEADS * 4), :] for h in range(HEADS)]
-        for high in range(4):
+    returned_f32[...] = returned_ref[...].astype(f32).reshape(GROUPS * WINDOW, L)
+    for n in range(6):
+        heads = [
+            returned_f32[pl.ds(h * WINDOW + n, PC, stride=HEADS * WINDOW), :] for h in range(HEADS)
+        ]
+        for high in {0: (3,), 5: (0,)}.get(n, range(4)):
             line = jnp.concatenate([x[:, high * HEAD_DIM : (high + 1) * HEAD_DIM] for x in heads], axis=1)
-            at = (low * 4 + high) * PC
+            at = {0: OWN, 5: OWN + PC}.get(n, ((n - 1) * 4 + high) * PC)
             rows_f32[at : at + PC, :] = line
-    place = iota((PR * PC, PR * PC), 0)
-    order = one_hot(iota((PR * PC, PR * PC), 1) == (place % PR) * PC + place // PR)
+    place, source = iota((WIDE, WIDE), 0), iota((WIDE, WIDE), 1)
+    order = one_hot(source == jnp.where(place < OWN, (place % PR) * PC + place // PR, place))
     attended = jnp.dot(order, rows_f32[...].astype(bf16), preferred_element_type=f32).astype(bf16)
+    low, high = low_rim[1].astype(f32), high_rim[1].astype(f32)
+    tokens = jnp.concatenate(
+        [
+            tokens_ref[...].astype(f32),
+            jnp.concatenate([low[PC : 2 * PC], low[3 * PC : 4 * PC]], axis=1),
+            jnp.concatenate([high[0:PC], high[2 * PC : 3 * PC]], axis=1),
+        ],
+        axis=0,
+    )
     updated = (
-        tokens_ref[...].astype(f32) + jnp.dot(attended, out_weight_ref[...], preferred_element_type=f32)
+        tokens + jnp.dot(attended, out_weight_ref[...], preferred_element_type=f32)
     ).astype(bf16)
-    repeat = one_hot(iota((PC * L, PR * PC), 0) // PATCH == iota((PC * L, PR * PC), 1))
+    place, source = iota((L, WIDE), 0), iota((L, WIDE), 1)
+    spread = one_hot(source == jnp.where(place < W, OWN + PC + place // PATCH, OWN + place // PATCH - PC))
+    near = jnp.dot(spread, updated, preferred_element_type=f32)
+    after = iota((L, D), 0) < W
+    grown = lax.dot_general(
+        unpatch_ref[0], jnp.where(after, near, 0.0).astype(bf16), NT, preferred_element_type=f32
+    ) + lax.dot_general(
+        unpatch_ref[PATCH - 1], jnp.where(after, 0.0, near).astype(bf16), NT, preferred_element_type=f32
+    )
+    lane = iota((C, L), 1)
+    outer = jnp.where(lane < W, high_rim[0].astype(f32), low_rim[0].astype(f32))
+    for j in range(PATCH):
+        outer = outer + jnp.where(lane % PATCH == j, grown[j * C : (j + 1) * C], 0.0)
+    strip_ref[2] = outer.astype(bf16)
+    repeat = one_hot(iota((PC * L, WIDE), 0) // PATCH == iota((PC * L, WIDE), 1))
     repeated[...] = jnp.dot(repeat, updated, preferred_element_type=f32)
     inner = iota((L, D), 0) % PATCH
     for p in range(PC):
@@ -187,13 +228,12 @@
             grown = grown + lax.dot_general(unpatch_ref[i], part, NT, preferred_element_type=f32)
         cells = mixed_ref[p * PATCH : (p + 1) * PATCH].astype(f32) + grown.reshape(PATCH, C, L)
         merged_ref[p * PATCH : (p + 1) * PATCH] = cells.astype(bf16)
-    ends_ref[0] = merged_ref[0]
-    ends_ref[1] = merged_ref[W - 1]
-    column_edges(lambda w: merged_ref[w].astype(f32), edges_ref)
-
-
-def back_kernel(map_ref, low_row, high_row, low_col, high_col, conv_ref, out_ref, taps, result):
-    fill_taps(map_ref, low_row, high_row, low_col, high_col, taps)
+    strip_ref[0] = merged_ref[0]
+    strip_ref[1] = merged_ref[W - 1]
+
+
+def back_kernel(map_ref, strip_ref, low_strip, high_strip, conv_ref, out_ref, taps, result):
+    fill_taps(map_ref, strip_ref, low_strip, high_strip, taps)
     band = banded(conv_ref[...])
     for group in range(W // QUAD):
         value = conv_quad(band, taps, group)
@@ -226,13 +266,6 @@
     return lax.ppermute(block, axis, forward), lax.ppermute(block, axis, backward)
 
 
-def rims(ends, edges, *ready):
-    low_row, high_row, *ready = lax.optimization_barrier((*exchange(edges, "rows"), *ready))
-    strip = jnp.concatenate([ends, low_row[None], high_row[None]])
-    low_col, high_col = exchange(strip, "cols")
-    return low_row, high_row, low_col, high_col, *ready
-
-
 def per_device(pair_map, conv_in, embed_weight, qkv_weight, key_bias, out_weight, unpatch, conv_out):
     turned, edges, ends = call(
         turn_kernel, (shape(W, C, L), shape(C, L), shape(2, C, L)), [pltpu.VMEM((W, C, L), f32)], pair_map
@@ -240,31 +273,43 @@
     embed_rows, unpatch_rows = call(
         weights_kernel, (shape(PATCH, D, D), shape(PATCH, D, D)), [], embed_weight, unpatch, flops=1 << 32
     )
-    *borders, embed_rows, unpatch_rows = rims(ends, edges, embed_rows, unpatch_rows)
-    mixed, tokens, packed = call(
+    low_row, high_row, embed_rows, unpatch_rows = lax.optimization_barrier(
+        (*exchange(edges, "rows"), embed_rows, unpatch_rows)
+    )
+    outer = jnp.where(iota((C, L), 1) < W, high_row, low_row)
+    strip = jnp.concatenate([ends, outer[None]])
+    mixed, tokens, packed, rim = call(
         front_kernel,
-        (shape(W, C, L), shape(PR * PC, D), shape(GROUPS, PR, L)),
-        [pltpu.VMEM((W + 2, 3 * C, L), bf16), pltpu.VMEM((PR * PC, PATCH * D), bf16)],
-        turned, *borders, conv_in, embed_rows, qkv_weight, key_bias.transpose(1, 2, 0),
-    )
+        (shape(W, C, L), shape(OWN, D), shape(GROUPS, PR, L), shape(2, C, L)),
+        [
+            pltpu.VMEM((W + 2, 3 * C, L), bf16), pltpu.VMEM((OWN, PATCH * D), bf16),
+            pltpu.VMEM((OWN, L), f32), pltpu.VMEM((4 * PC, L), f32),
+        ],
+        turned, strip, *exchange(strip, "cols"), conv_in, embed_rows, qkv_weight, key_bias.transpose(1, 2, 0),
+    )
+    low_rim, high_rim = exchange(rim, "rows")
     arrived = lax.all_to_all(packed, "rows", split_axis=0, concat_axis=0, tiled=True)
     heads_out = call(
-        attention_kernel, shape(SEQ // 4, L), [pltpu.VMEM((SEQ, L), f32)], arrived
-    )
-    returned = lax.all_to_all(
-        heads_out.reshape(GROUPS, 4, L), "rows", split_axis=0, concat_axis=0, tiled=True
-    ).reshape(GROUPS * 4, L)
-    merged, edges, ends = call(
+        attention_kernel,
+        shape(GROUPS, WINDOW, L),
+        [
+            pltpu.VMEM((SEQ, L), f32), pltpu.VMEM((SEQ // 4 + 16, L), f32),
+            pltpu.VMEM((GROUPS * WINDOW, L), f32),
+        ],
+        arrived,
+    )
+    returned = lax.all_to_all(heads_out, "rows", split_axis=0, concat_axis=0, tiled=True)
+    merged, strip = call(
         merge_kernel,
-        (shape(W, C, L), shape(C, L), shape(2, C, L)),
-        [pltpu.VMEM((GROUPS * 4, L), f32), pltpu.VMEM((PR * PC, D), f32), pltpu.VMEM((PC * L, D), f32)],
-        returned, tokens, out_weight, unpatch_rows, mixed,
+        (shape(W, C, L), shape(3, C, L)),
+        [pltpu.VMEM((GROUPS * WINDOW, L), f32), pltpu.VMEM((WIDE, D), f32), pltpu.VMEM((PC * L, D), f32)],
+        returned, tokens, low_rim, high_rim, out_weight, unpatch_rows, mixed,
     )
     return call(
         back_kernel,
         jax.ShapeDtypeStruct((C, W, L), bf16),
         [pltpu.VMEM((W + 2, 3 * C, L), bf16), pltpu.VMEM((W, C, L), f32)],
-        merged, *rims(ends, edges), conv_out,
+        merged, strip, *exchange(strip, "cols"), conv_out,
     )
 
 

time: 113 us -> 105 us (0.929)
  the two profiles are of different devices: /device:TPU:48 before, /device:TPU:72 now
where the time goes in v3:
time: 105 us
  starting transfers between devices  35.9 us (34%)
  blocking collectives  28.6 us (27%)
  waiting for transfers between devices  22.7 us (22%)
  Pallas kernels  14 us (13%)
  local copies, waits for them, and re-layouts  3.51 us (3%)
    all_to_all x1, blocking collectives, per_device(): lax.all_to_all(packed, 'rows', split_axis=0, concat_axis=0, tiled=True)  28.6 us
    ppermute x4, waiting for transfers between devices, exchange(): lax.ppermute(block, axis, forward)  22.7 us
    ppermute x4, starting transfers between devices, exchange(): lax.ppermute(block, axis, backward)  21.5 us
    pallas_call x6, Pallas kernels, call(): pl.pallas_call(kernel, out_shape=outs, in_specs=[pl.BlockSpec(memory_spac...  14 us
    ppermute x4, starting transfers between devices, exchange(): lax.ppermute(block, axis, forward)  8.83 us
    all_to_all x1, starting transfers between devices, per_device(): lax.all_to_all(heads_out, 'rows', split_axis=0, concat_axis=0, tiled=True)  5.63 us
    unnamed x16, local copies, waits for them, and re-layouts  3.51 us
  transfers between devices with their start and end apart: 9, of which 4 were waited for; matrix products, arithmetic and copies ran while one was open for 0% of the time, Pallas kernels for 1%

profile of v3, /device:TPU:72, one launch (start us, length us, event | category | flops | bytes accessed | tf_op | source)
XLA Modules:
  0.0 104.9 jit_solution(6877321674516395713)
XLA Ops:
  0.0 1.0 copy-done
  1.0 0.5 turn_kernel.1
  1.5 0.0 copy-start.1
  1.5 8.3 %collective-permute-start.1 = (bf16[32,128]{1,0:T(8,128)(2,1)S(1)}, bf16[32,128]{1,0:T(8,128)(2,1)S(1)}, u32[]{:S(2)}, u32[]{:S(2)}) collective-permute-start(bf16[32,128]{1,0:T(8,128)(2,1)S(1)} %get-tuple-element.22), channel_id=1, source_target_pairs={{8,0},{16,8},{24,16},{32,24},{40,32},{48,40},{56,48},{64,56},{72,6... | collective-permute-start | bytes 24584 | tf_op jit(solution)/shard_map/ppermute | solution.py:266
  9.8 1.9 %collective-permute-start = (bf16[32,128]{1,0:T(8,128)(2,1)S(1)}, bf16[32,128]{1,0:T(8,128)(2,1)S(1)}, u32[]{:S(2)}, u32[]{:S(2)}) collective-permute-start(bf16[32,128]{1,0:T(8,128)(2,1)S(1)} %get-tuple-element.22), channel_id=1, source_target_pairs={{0,8},{8,16},{16,24},{24,32},{32,40},{40,48},{48,56},{56,64},{64,7... | collective-permute-start | bytes 24584 | tf_op jit(solution)/shard_map/ppermute | solution.py:266
  11.7 1.2 %copy-done.6 = bf16[2048,256]{1,0:T(8,128)(2,1)S(1)} copy-done((bf16[2048,256]{1,0:T(8,128)(2,1)S(1)}, bf16[2048,256]{1,0:T(8,128)(2,1)}, u32[]{:S(2)}) %copy-start.6) | copy-done | bytes 1048600
  12.9 1.2 %copy-done.7 = bf16[256,2048]{1,0:T(8,128)(2,1)S(1)} copy-done((bf16[256,2048]{1,0:T(8,128)(2,1)S(1)}, bf16[256,2048]{1,0:T(8,128)(2,1)}, u32[]{:S(2)}) %copy-start.7) | copy-done | bytes 1048600
  14.2 1.2 %weights_kernel.1 = (bf16[8,256,256]{2,1,0:T(8,128)(2,1)S(1)}, bf16[8,256,256]{2,1,0:T(8,128)(2,1)S(1)}) custom-call(bf16[2048,256]{1,0:T(8,128)(2,1)S(1)} %copy-done.6, bf16[256,2048]{1,0:T(8,128)(2,1)S(1)} %copy-done.7), custom_call_target="tpu_custom_call" | custom-call | flops 4294967296 | bytes 1048576 | tf_op jit(solution)/shard_map/weights_kernel/pallas_call | solution.py:251
  15.4 6.8 %collective-permute-done = bf16[32,128]{1,0:T(8,128)(2,1)S(1)} collective-permute-done((bf16[32,128]{1,0:T(8,128)(2,1)S(1)}, bf16[32,128]{1,0:T(8,128)(2,1)S(1)}, u32[]{:S(2)}, u32[]{:S(2)}) %collective-permute-start) | collective-permute-done | bytes 8224 | tf_op jit(solution)/shard_map/ppermute | solution.py:266
  22.3 1.9 %collective-permute-start.3 = (bf16[3,32,128]{2,1,0:T(8,128)(2,1)S(1)}, bf16[3,32,128]{2,1,0:T(8,128)(2,1)S(1)}, u32[]{:S(2)}, u32[]{:S(2)}) collective-permute-start(bf16[3,32,128]{2,1,0:T(8,128)(2,1)S(1)} %pad_maximum_fusion.strip_ref), channel_id=1, source_target_pairs={{1,0},{2,1},{3,2},{4,3},{5,4},{6,5},{7,6},{9,8},{10,9},{11,10},{12... | collective-permute-start | bytes 73736 | tf_op jit(solution)/shard_map/ppermute | solution.py:266
  24.2 2.4 %collective-permute-start.2 = (bf16[3,32,128]{2,1,0:T(8,128)(2,1)S(1)}, bf16[3,32,128]{2,1,0:T(8,128)(2,1)S(1)}, u32[]{:S(2)}, u32[]{:S(2)}) collective-permute-start(bf16[3,32,128]{2,1,0:T(8,128)(2,1)S(1)} %pad_maximum_fusion.strip_ref), channel_id=1, source_target_pairs={{0,1},{1,2},{2,3},{3,4},{4,5},{5,6},{6,7},{8,9},{9,10},{10,11},{11... | collective-permute-start | bytes 73736 | tf_op jit(solution)/shard_map/ppermute | solution.py:266
  26.6 2.7 %collective-permute-done.2.low_strip = bf16[3,32,128]{2,1,0:T(8,128)(2,1)S(1)} collective-permute-done((bf16[3,32,128]{2,1,0:T(8,128)(2,1)S(1)}, bf16[3,32,128]{2,1,0:T(8,128)(2,1)S(1)}, u32[]{:S(2)}, u32[]{:S(2)}) %collective-permute-start.2) | collective-permute-done | bytes 24608 | tf_op jit(solution)/shard_map/ppermute | solution.py:266
  29.4 3.6 %front_kernel.1 = (bf16[64,32,128]{2,1,0:T(8,128)(2,1)S(1)}, bf16[128,256]{1,0:T(8,128)(2,1)S(1)}, bf16[64,16,128]{2,1,0:T(8,128)(2,1)S(1)}, bf16[2,32,128]{2,1,0:T(8,128)(2,1)S(1)}) custom-call(bf16[64,32,128]{2,1,0:T(8,128)(2,1)S(1)} %get-tuple-element.20.map_ref, bf16[3,32,128]{2,1,0:T(8,128)(2,1)S(1)} %pad_maximum_fusion.strip_ref, ...), custom_call_target="tpu_custom_call" | custom-call | bytes 1048576 | tf_op jit(solution)/shard_map/front_kernel/pallas_call | solution.py:251
  33.0 28.6 %all_to_all.10.packed_ref = bf16[64,16,128]{2,1,0:T(8,128)(2,1)S(1)} all-to-all(bf16[64,16,128]{2,1,0:T(8,128)(2,1)S(1)} %get-tuple-element.28), channel_id=1, replica_groups=mesh['rows'=64,'cols'=8] {'rows'}, dimensions={0} | all-to-all | bytes 524288 | tf_op jit(solution)/shard_map/all_to_all | solution.py:291
  61.5 3.2 %attention_kernel.1 = bf16[64,8,128]{2,1,0:T(8,128)(2,1)} custom-call(bf16[64,16,128]{2,1,0:T(8,128)(2,1)S(1)} %all_to_all.10.packed_ref), custom_call_target="tpu_custom_call" | custom-call | bytes 1048576 | tf_op jit(solution)/shard_map/attention_kernel/pallas_call | solution.py:251
  64.7 5.6 %all-to-all-start.1 = ((bf16[64,8,128]{2,1,0:T(8,128)(2,1)}), bf16[64,8,128]{2,1,0:T(8,128)(2,1)S(1)}, u32[]{:S(2)}, u32[]{:S(2)}) async-start(bf16[64,8,128]{2,1,0:T(8,128)(2,1)} %attention_kernel.1), calls=%async_computation.1 | async-start | bytes 262144 | tf_op jit(solution)/shard_map/all_to_all | solution.py:301
  70.4 9.4 %collective-permute-start.5 = (bf16[2,32,128]{2,1,0:T(8,128)(2,1)S(1)}, bf16[2,32,128]{2,1,0:T(8,128)(2,1)S(1)}, u32[]{:S(2)}, u32[]{:S(2)}) collective-permute-start(bf16[2,32,128]{2,1,0:T(8,128)(2,1)S(1)} %get-tuple-element.30), channel_id=1, source_target_pairs={{8,0},{16,8},{24,16},{32,24},{40,32},{48,40},{56,48},{64,56},{72,6... | collective-permute-start | bytes 49160 | tf_op jit(solution)/shard_map/ppermute | solution.py:266
  79.8 2.1 %collective-permute-start.4 = (bf16[2,32,128]{2,1,0:T(8,128)(2,1)S(1)}, bf16[2,32,128]{2,1,0:T(8,128)(2,1)S(1)}, u32[]{:S(2)}, u32[]{:S(2)}) collective-permute-start(bf16[2,32,128]{2,1,0:T(8,128)(2,1)S(1)} %get-tuple-element.30), channel_id=1, source_target_pairs={{0,8},{8,16},{16,24},{24,32},{32,40},{40,48},{48,56},{56,64},{64,7... | collective-permute-start | bytes 49160 | tf_op jit(solution)/shard_map/ppermute | solution.py:266
  81.9 10.4 %collective-permute-done.4.low_rim = bf16[2,32,128]{2,1,0:T(8,128)(2,1)S(1)} collective-permute-done((bf16[2,32,128]{2,1,0:T(8,128)(2,1)S(1)}, bf16[2,32,128]{2,1,0:T(8,128)(2,1)S(1)}, u32[]{:S(2)}, u32[]{:S(2)}) %collective-permute-start.4) | collective-permute-done | bytes 16416 | tf_op jit(solution)/shard_map/ppermute | solution.py:266
  92.3 3.1 %merge_kernel.1 = (bf16[64,32,128]{2,1,0:T(8,128)(2,1)S(1)}, bf16[3,32,128]{2,1,0:T(8,128)(2,1)S(1)}) custom-call(bf16[64,8,128]{2,1,0:T(8,128)(2,1)S(1)} %all-to-all-done.1.returned_ref, bf16[128,256]{1,0:T(8,128)(2,1)S(1)} %get-tuple-element.29.tokens_ref, bf16[2,32,128]{2,1,0:T(8,128)(2,1)S(1)} %collective-permute-done.4.low_rim, ...), custom_call_target="tpu_custom_call" | custom-call | bytes 1048576 | tf_op jit(solution)/shard_map/merge_kernel/pallas_call | solution.py:251
  95.5 1.9 %collective-permute-start.7 = (bf16[3,32,128]{2,1,0:T(8,128)(2,1)S(1)}, bf16[3,32,128]{2,1,0:T(8,128)(2,1)S(1)}, u32[]{:S(2)}, u32[]{:S(2)}) collective-permute-start(bf16[3,32,128]{2,1,0:T(8,128)(2,1)S(1)} %get-tuple-element.34.strip_ref), channel_id=1, source_target_pairs={{1,0},{2,1},{3,2},{4,3},{5,4},{6,5},{7,6},{9,8},{10,9},{11,10},{12... | collective-permute-start | bytes 73736 | tf_op jit(solution)/shard_map/ppermute | solution.py:266
  97.4 2.4 %collective-permute-start.6 = (bf16[3,32,128]{2,1,0:T(8,128)(2,1)S(1)}, bf16[3,32,128]{2,1,0:T(8,128)(2,1)S(1)}, u32[]{:S(2)}, u32[]{:S(2)}) collective-permute-start(bf16[3,32,128]{2,1,0:T(8,128)(2,1)S(1)} %get-tuple-element.34.strip_ref), channel_id=1, source_target_pairs={{0,1},{1,2},{2,3},{3,4},{4,5},{5,6},{6,7},{8,9},{9,10},{10,11},{11... | collective-permute-start | bytes 73736 | tf_op jit(solution)/shard_map/ppermute | solution.py:266
  99.8 2.7 %collective-permute-done.6.low_strip = bf16[3,32,128]{2,1,0:T(8,128)(2,1)S(1)} collective-permute-done((bf16[3,32,128]{2,1,0:T(8,128)(2,1)S(1)}, bf16[3,32,128]{2,1,0:T(8,128)(2,1)S(1)}, u32[]{:S(2)}, u32[]{:S(2)}) %collective-permute-start.6) | collective-permute-done | bytes 24608 | tf_op jit(solution)/shard_map/ppermute | solution.py:266
  102.5 2.3 %back_kernel.1 = bf16[32,64,128]{2,1,0:T(8,128)(2,1)} custom-call(bf16[64,32,128]{2,1,0:T(8,128)(2,1)S(1)} %get-tuple-element.33.map_ref, bf16[3,32,128]{2,1,0:T(8,128)(2,1)S(1)} %get-tuple-element.34.strip_ref, bf16[3,32,128]{2,1,0:T(8,128)(2,1)S(1)} %collective-permute-done.6.low_strip, bf16[3,32,128]{2,1,0:T(8,128)(2,1)S(1)} %collective-permute-done.7.high_strip, ...), custom_call_target="tpu_custom_call" | custom-call | bytes 1048576 | tf_op jit(solution)/shard_map/back_kernel/pallas_call | solution.py:251
  (20 shorter events, 0.1 us)
Async XLA Ops:
  0.0 1.0 copy-start
  1.5 27.8 %copy-start.1 = (bf16[256,768]{1,0:T(8,128)(2,1)S(1)}, bf16[256,768]{1,0:T(8,128)(2,1)}, u32[]{:S(2)}) copy-start(bf16[256,768]{1,0:T(8,128)(2,1)} %qkv_ref.1) | copy-start | bytes 1179652
  1.5 13.9 %collective-permute-start.1 = (bf16[32,128]{1,0:T(8,128)(2,1)S(1)}, bf16[32,128]{1,0:T(8,128)(2,1)S(1)}, u32[]{:S(2)}, u32[]{:S(2)}) collective-permute-start(bf16[32,128]{1,0:T(8,128)(2,1)S(1)} %get-tuple-element.22), channel_id=1, source_target_pairs={{8,0},{16,8},{24,16},{32,24},{40,32},{48,40},{56,48},{64,56},{72,6... | collective-permute-start | bytes 24584 | tf_op jit(solution)/shard_map/ppermute | solution.py:266
  9.8 12.5 %collective-permute-start = (bf16[32,128]{1,0:T(8,128)(2,1)S(1)}, bf16[32,128]{1,0:T(8,128)(2,1)S(1)}, u32[]{:S(2)}, u32[]{:S(2)}) collective-permute-start(bf16[32,128]{1,0:T(8,128)(2,1)S(1)} %get-tuple-element.22), channel_id=1, source_target_pairs={{0,8},{8,16},{16,24},{24,32},{32,40},{40,48},{48,56},{56,64},{64,7... | collective-permute-start | bytes 24584 | tf_op jit(solution)/shard_map/ppermute | solution.py:266
  11.7 1.2 %copy-start.6 = (bf16[2048,256]{1,0:T(8,128)(2,1)S(1)}, bf16[2048,256]{1,0:T(8,128)(2,1)}, u32[]{:S(2)}) copy-start(bf16[2048,256]{1,0:T(8,128)(2,1)} %embed_ref.1) | copy-start | bytes 3145732
  12.9 1.2 %copy-start.7 = (bf16[256,2048]{1,0:T(8,128)(2,1)S(1)}, bf16[256,2048]{1,0:T(8,128)(2,1)}, u32[]{:S(2)}) copy-start(bf16[256,2048]{1,0:T(8,128)(2,1)} %unpatch_ref.1) | copy-start | bytes 3145732
  22.3 7.1 %copy-start.3 = (bf16[32,288]{1,0:T(8,128)(2,1)S(1)}, bf16[32,288]{1,0:T(8,128)(2,1)}, u32[]{:S(2)}) copy-start(bf16[32,288]{1,0:T(8,128)(2,1)} %conv_ref.2) | copy-start | bytes 55300
  22.3 7.1 %copy-start.5 = (bf16[16,8,8]{0,2,1:T(8,128)(2,1)S(1)}, bf16[16,8,8]{0,2,1:T(8,128)(2,1)}, u32[]{:S(2)}) copy-start(bf16[16,8,8]{0,2,1:T(8,128)(2,1)} %param.12) | copy-start | bytes 6148
  22.3 4.3 %collective-permute-start.3 = (bf16[3,32,128]{2,1,0:T(8,128)(2,1)S(1)}, bf16[3,32,128]{2,1,0:T(8,128)(2,1)S(1)}, u32[]{:S(2)}, u32[]{:S(2)}) collective-permute-start(bf16[3,32,128]{2,1,0:T(8,128)(2,1)S(1)} %pad_maximum_fusion.strip_ref), channel_id=1, source_target_pairs={{1,0},{2,1},{3,2},{4,3},{5,4},{6,5},{7,6},{9,8},{10,9},{11,10},{12... | collective-permute-start | bytes 73736 | tf_op jit(solution)/shard_map/ppermute | solution.py:266
  24.2 5.1 %collective-permute-start.2 = (bf16[3,32,128]{2,1,0:T(8,128)(2,1)S(1)}, bf16[3,32,128]{2,1,0:T(8,128)(2,1)S(1)}, u32[]{:S(2)}, u32[]{:S(2)}) collective-permute-start(bf16[3,32,128]{2,1,0:T(8,128)(2,1)S(1)} %pad_maximum_fusion.strip_ref), channel_id=1, source_target_pairs={{0,1},{1,2},{2,3},{3,4},{4,5},{5,6},{6,7},{8,9},{9,10},{10,11},{11... | collective-permute-start | bytes 73736 | tf_op jit(solution)/shard_map/ppermute | solution.py:266
  64.7 27.6 %copy-start.2 = (bf16[256,256]{1,0:T(8,128)(2,1)S(1)}, bf16[256,256]{1,0:T(8,128)(2,1)}, u32[]{:S(2)}) copy-start(bf16[256,256]{1,0:T(8,128)(2,1)} %out_weight_ref.1) | copy-start | bytes 393220
  64.7 27.6 %all-to-all-start.1 = ((bf16[64,8,128]{2,1,0:T(8,128)(2,1)}), bf16[64,8,128]{2,1,0:T(8,128)(2,1)S(1)}, u32[]{:S(2)}, u32[]{:S(2)}) async-start(bf16[64,8,128]{2,1,0:T(8,128)(2,1)} %attention_kernel.1), calls=%async_computation.1 | async-start | bytes 262144 | tf_op jit(solution)/shard_map/all_to_all | solution.py:301
  70.4 11.5 %collective-permute-start.5 = (bf16[2,32,128]{2,1,0:T(8,128)(2,1)S(1)}, bf16[2,32,128]{2,1,0:T(8,128)(2,1)S(1)}, u32[]{:S(2)}, u32[]{:S(2)}) collective-permute-start(bf16[2,32,128]{2,1,0:T(8,128)(2,1)S(1)} %get-tuple-element.30), channel_id=1, source_target_pairs={{8,0},{16,8},{24,16},{32,24},{40,32},{48,40},{56,48},{64,56},{72,6... | collective-permute-start | bytes 49160 | tf_op jit(solution)/shard_map/ppermute | solution.py:266
  79.8 12.5 %collective-permute-start.4 = (bf16[2,32,128]{2,1,0:T(8,128)(2,1)S(1)}, bf16[2,32,128]{2,1,0:T(8,128)(2,1)S(1)}, u32[]{:S(2)}, u32[]{:S(2)}) collective-permute-start(bf16[2,32,128]{2,1,0:T(8,128)(2,1)S(1)} %get-tuple-element.30), channel_id=1, source_target_pairs={{0,8},{8,16},{16,24},{24,32},{32,40},{40,48},{48,56},{56,64},{64,7... | collective-permute-start | bytes 49160 | tf_op jit(solution)/shard_map/ppermute | solution.py:266
  92.3 10.2 %copy-start.4 = (bf16[32,288]{1,0:T(8,128)(2,1)S(1)}, bf16[32,288]{1,0:T(8,128)(2,1)}, u32[]{:S(2)}) copy-start(bf16[32,288]{1,0:T(8,128)(2,1)} %conv_ref.3) | copy-start | bytes 55300
  95.5 4.3 %collective-permute-start.7 = (bf16[3,32,128]{2,1,0:T(8,128)(2,1)S(1)}, bf16[3,32,128]{2,1,0:T(8,128)(2,1)S(1)}, u32[]{:S(2)}, u32[]{:S(2)}) collective-permute-start(bf16[3,32,128]{2,1,0:T(8,128)(2,1)S(1)} %get-tuple-element.34.strip_ref), channel_id=1, source_target_pairs={{1,0},{2,1},{3,2},{4,3},{5,4},{6,5},{7,6},{9,8},{10,9},{11,10},{12... | collective-permute-start | bytes 73736 | tf_op jit(solution)/shard_map/ppermute | solution.py:266
  97.4 5.1 %collective-permute-start.6 = (bf16[3,32,128]{2,1,0:T(8,128)(2,1)S(1)}, bf16[3,32,128]{2,1,0:T(8,128)(2,1)S(1)}, u32[]{:S(2)}, u32[]{:S(2)}) collective-permute-start(bf16[3,32,128]{2,1,0:T(8,128)(2,1)S(1)} %get-tuple-element.34.strip_ref), channel_id=1, source_target_pairs={{0,1},{1,2},{2,3},{3,4},{4,5},{5,6},{6,7},{8,9},{9,10},{10,11},{11... | collective-permute-start | bytes 73736 | tf_op jit(solution)/shard_map/ppermute | solution.py:266

commit v4 on v3

--- a/solution.py
+++ b/solution.py
@@ -63,11 +63,10 @@
                 target[i, j * C : (j + 1) * C, :] = turned[j * PATCH + i].astype(bf16)
 
 
-def fill_taps(map_ref, strip, low_strip, high_strip, taps):
+def fill_taps(map_ref, strip, even_strip, other_strip, taps):
     lane = iota((C, L), 1)
     outer = strip[2].astype(f32)
-    below = [low_strip[n].astype(f32) for n in range(3)]
-    above = [high_strip[n].astype(f32) for n in range(3)]
+    below, above = zip(*(sides("cols", even_strip[n], other_strip[n]) for n in range(3)))
     for w in range(-1, W + 1):
         if w < 0:
             slab, left, right = below[1], below[2][:, L - 1 : L], below[2][:, W - 1 : W]
@@ -100,10 +99,10 @@
 
 
 def front_kernel(
-    map_ref, strip_ref, low_strip, high_strip, conv_ref, embed_ref, qkv_ref, bias_ref,
+    map_ref, strip_ref, even_strip, other_strip, conv_ref, embed_ref, qkv_ref, bias_ref,
     mixed_ref, tokens_ref, packed_ref, rim_ref, taps, gathered, tokens_f32, rim_f32,
 ):
-    fill_taps(map_ref, strip_ref, low_strip, high_strip, taps)
+    fill_taps(map_ref, strip_ref, even_strip, other_strip, taps)
     band = banded(conv_ref[...])
     row = iota((L, L), 0)
     select = one_hot(iota((L, L), 1) == (row % PR) * PATCH + row // PR)
@@ -176,7 +175,7 @@
 
 
 def merge_kernel(
-    returned_ref, tokens_ref, low_rim, high_rim, out_weight_ref, unpatch_ref, mixed_ref,
+    returned_ref, tokens_ref, even_rim, other_rim, out_weight_ref, unpatch_ref, mixed_ref,
     merged_ref, strip_ref, returned_f32, rows_f32, repeated,
 ):
     returned_f32[...] = returned_ref[...].astype(f32).reshape(GROUPS * WINDOW, L)
@@ -191,7 +190,7 @@
     place, source = iota((WIDE, WIDE), 0), iota((WIDE, WIDE), 1)
     order = one_hot(source == jnp.where(place < OWN, (place % PR) * PC + place // PR, place))
     attended = jnp.dot(order, rows_f32[...].astype(bf16), preferred_element_type=f32).astype(bf16)
-    low, high = low_rim[1].astype(f32), high_rim[1].astype(f32)
+    low, high = sides("rows", even_rim[1], other_rim[1])
     tokens = jnp.concatenate(
         [
             tokens_ref[...].astype(f32),
@@ -213,7 +212,8 @@
         unpatch_ref[PATCH - 1], jnp.where(after, 0.0, near).astype(bf16), NT, preferred_element_type=f32
     )
     lane = iota((C, L), 1)
-    outer = jnp.where(lane < W, high_rim[0].astype(f32), low_rim[0].astype(f32))
+    before, beyond = sides("rows", even_rim[0], other_rim[0])
+    outer = jnp.where(lane < W, beyond, before)
     for j in range(PATCH):
         outer = outer + jnp.where(lane % PATCH == j, grown[j * C : (j + 1) * C], 0.0)
     strip_ref[2] = outer.astype(bf16)
@@ -232,8 +232,8 @@
     strip_ref[1] = merged_ref[W - 1]
 
 
-def back_kernel(map_ref, strip_ref, low_strip, high_strip, conv_ref, out_ref, taps, result):
-    fill_taps(map_ref, strip_ref, low_strip, high_strip, taps)
+def back_kernel(map_ref, strip_ref, even_strip, other_strip, conv_ref, out_ref, taps, result):
+    fill_taps(map_ref, strip_ref, even_strip, other_strip, taps)
     band = banded(conv_ref[...])
     for group in range(W // QUAD):
         value = conv_quad(band, taps, group)
@@ -261,9 +261,17 @@
 
 def exchange(block, axis):
     count = lax.axis_size(axis)
-    forward = [(i, i + 1) for i in range(count - 1)]
-    backward = [(target, source) for source, target in forward]
-    return lax.ppermute(block, axis, forward), lax.ppermute(block, axis, backward)
+    swaps = []
+    for first in (0, 1):
+        pairs = [(i, i + 1) for i in range(first, count - 1, 2)]
+        swaps.append(lax.ppermute(block, axis, pairs + [(j, i) for i, j in pairs]))
+    return swaps
+
+
+def sides(axis, even, other):
+    odd = lax.axis_index(axis) % 2 == 1
+    even, other = even.astype(f32), other.astype(f32)
+    return jnp.where(odd, even, other), jnp.where(odd, other, even)
 
 
 def per_device(pair_map, conv_in, embed_weight, qkv_weight, key_bias, out_weight, unpatch, conv_out):
@@ -273,10 +281,10 @@
     embed_rows, unpatch_rows = call(
         weights_kernel, (shape(PATCH, D, D), shape(PATCH, D, D)), [], embed_weight, unpatch, flops=1 << 32
     )
-    low_row, high_row, embed_rows, unpatch_rows = lax.optimization_barrier(
-        (*exchange(edges, "rows"), embed_rows, unpatch_rows)
-    )
-    outer = jnp.where(iota((C, L), 1) < W, high_row, low_row)
+    even_row, other_row = exchange(edges, "rows")
+    edges, ends, embed_rows, unpatch_rows = lax.optimization_barrier((edges, ends, embed_rows, unpatch_rows))
+    odd = lax.axis_index("rows") % 2 == 1
+    outer = jnp.where((iota((C, L), 1) < W) == odd, other_row, even_row)
     strip = jnp.concatenate([ends, outer[None]])
     mixed, tokens, packed, rim = call(
         front_kernel,
@@ -287,7 +295,7 @@
         ],
         turned, strip, *exchange(strip, "cols"), conv_in, embed_rows, qkv_weight, key_bias.transpose(1, 2, 0),
     )
-    low_rim, high_rim = exchange(rim, "rows")
+    even_rim, other_rim = exchange(rim, "rows")
     arrived = lax.all_to_all(packed, "rows", split_axis=0, concat_axis=0, tiled=True)
     heads_out = call(
         attention_kernel,
@@ -303,7 +311,7 @@
         merge_kernel,
         (shape(W, C, L), shape(3, C, L)),
         [pltpu.VMEM((GROUPS * WINDOW, L), f32), pltpu.VMEM((WIDE, D), f32), pltpu.VMEM((PC * L, D), f32)],
-        returned, tokens, low_rim, high_rim, out_weight, unpatch_rows, mixed,
+        returned, tokens, even_rim, other_rim, out_weight, unpatch_rows, mixed,
     )
     return call(
         back_kernel,

time: 105 us -> 97.9 us (0.932)
  the two profiles are of different devices: /device:TPU:72 before, /device:TPU:1 now
where the time goes in v4:
time: 97.9 us; the launch traced here: 97.4 us
  blocking collectives  38 us (39%)
  starting transfers between devices  32.3 us (33%)
  Pallas kernels  14 us (14%)
  waiting for transfers between devices  9.25 us (9%)
  local copies, waits for them, and re-layouts  3.51 us (4%)
    all_to_all x1, blocking collectives, per_device(): lax.all_to_all(packed, 'rows', split_axis=0, concat_axis=0, tiled=True)  38 us
    ppermute x8, starting transfers between devices, exchange(): swaps.append(lax.ppermute(block, axis, pairs + [(j, i) for i, j in pairs]))  24.9 us
    pallas_call x6, Pallas kernels, call(): pl.pallas_call(kernel, out_shape=outs, in_specs=[pl.BlockSpec(memory_spac...  14 us
    all_to_all x1, starting transfers between devices, per_device(): lax.all_to_all(heads_out, 'rows', split_axis=0, concat_axis=0, tiled=True)  7.41 us
    all_to_all x1, waiting for transfers between devices, per_device(): lax.all_to_all(heads_out, 'rows', split_axis=0, concat_axis=0, tiled=True)  6.01 us
    unnamed x16, local copies, waits for them, and re-layouts  3.51 us
    ppermute x8, waiting for transfers between devices, exchange(): swaps.append(lax.ppermute(block, axis, pairs + [(j, i) for i, j in pairs]))  3.24 us
  transfers between devices with their start and end apart: 9, of which 4 were waited for; matrix products, arithmetic and copies ran while one was open for 0% of the time, Pallas kernels for 1%

profile of v4, /device:TPU:1, one launch (start us, length us, event | category | flops | bytes accessed | tf_op | source)
XLA Modules:
  0.0 97.4 jit_solution(12986787899570823097)
XLA Ops:
  0.0 1.0 %copy-done = bf16[32,64,128]{2,1,0:T(8,128)(2,1)S(1)} copy-done((bf16[32,64,128]{2,1,0:T(8,128)(2,1)S(1)}, bf16[32,64,128]{2,1,0:T(8,128)(2,1)}, u32[]{:S(2)}) %copy-start) | copy-done | bytes 524312
  1.0 0.5 turn_kernel.1
  1.5 3.9 %collective-permute-start.1 = (bf16[32,128]{1,0:T(8,128)(2,1)S(1)}, bf16[32,128]{1,0:T(8,128)(2,1)S(1)}, u32[]{:S(2)}, u32[]{:S(2)}) collective-permute-start(bf16[32,128]{1,0:T(8,128)(2,1)S(1)} %get-tuple-element.20), channel_id=1, source_target_pairs={{0,8},{16,24},{32,40},{48,56},{64,72},{80,88},{96,104},{112,120},{... | collective-permute-start | bytes 24584 | tf_op jit(solution)/shard_map/ppermute | solution.py:267
  5.5 0.7 collective-permute-start
  6.1 0.0 copy-start.6
  6.2 1.2 %copy-done.6 = bf16[2048,256]{1,0:T(8,128)(2,1)S(1)} copy-done((bf16[2048,256]{1,0:T(8,128)(2,1)S(1)}, bf16[2048,256]{1,0:T(8,128)(2,1)}, u32[]{:S(2)}) %copy-start.6) | copy-done | bytes 1048600
  7.4 1.2 %copy-done.7 = bf16[256,2048]{1,0:T(8,128)(2,1)S(1)} copy-done((bf16[256,2048]{1,0:T(8,128)(2,1)S(1)}, bf16[256,2048]{1,0:T(8,128)(2,1)}, u32[]{:S(2)}) %copy-start.7) | copy-done | bytes 1048600
  8.6 1.2 %weights_kernel.1 = (bf16[8,256,256]{2,1,0:T(8,128)(2,1)S(1)}, bf16[8,256,256]{2,1,0:T(8,128)(2,1)S(1)}) custom-call(bf16[2048,256]{1,0:T(8,128)(2,1)S(1)} %copy-done.6, bf16[256,2048]{1,0:T(8,128)(2,1)S(1)} %copy-done.7), custom_call_target="tpu_custom_call" | custom-call | flops 4294967296 | bytes 1048576 | tf_op jit(solution)/shard_map/weights_kernel/pallas_call | solution.py:251
  9.9 4.0 %collective-permute-start.3 = (bf16[3,32,128]{2,1,0:T(8,128)(2,1)S(1)}, bf16[3,32,128]{2,1,0:T(8,128)(2,1)S(1)}, u32[]{:S(2)}, u32[]{:S(2)}) collective-permute-start(bf16[3,32,128]{2,1,0:T(8,128)(2,1)S(1)} %pad_maximum_fusion.strip_ref), channel_id=1, source_target_pairs={{1,2},{3,4},{5,6},{2,1},{4,3},{6,5},{9,10},{11,12},{13,14},{10,9},... | collective-permute-start | bytes 73736 | tf_op jit(solution)/shard_map/ppermute | solution.py:267
  14.0 3.3 %collective-permute-start.2 = (bf16[3,32,128]{2,1,0:T(8,128)(2,1)S(1)}, bf16[3,32,128]{2,1,0:T(8,128)(2,1)S(1)}, u32[]{:S(2)}, u32[]{:S(2)}) collective-permute-start(bf16[3,32,128]{2,1,0:T(8,128)(2,1)S(1)} %pad_maximum_fusion.strip_ref), channel_id=1, source_target_pairs={{0,1},{2,3},{4,5},{6,7},{1,0},{3,2},{5,4},{7,6},{8,9},{10,11},{12,... | collective-permute-start | bytes 73736 | tf_op jit(solution)/shard_map/ppermute | solution.py:267
  17.4 0.8 collective-permute-done.2.even_strip
  18.2 3.6 %front_kernel.1 = (bf16[64,32,128]{2,1,0:T(8,128)(2,1)S(1)}, bf16[128,256]{1,0:T(8,128)(2,1)S(1)}, bf16[64,16,128]{2,1,0:T(8,128)(2,1)S(1)}, bf16[2,32,128]{2,1,0:T(8,128)(2,1)S(1)}) custom-call(bf16[64,32,128]{2,1,0:T(8,128)(2,1)S(1)} %get-tuple-element.19.map_ref, bf16[3,32,128]{2,1,0:T(8,128)(2,1)S(1)} %pad_maximum_fusion.strip_ref, ...), custom_call_target="tpu_custom_call" | custom-call | bytes 1048576 | tf_op jit(solution)/shard_map/front_kernel/pallas_call | solution.py:251
  21.8 38.0 %all_to_all.10.packed_ref = bf16[64,16,128]{2,1,0:T(8,128)(2,1)S(1)} all-to-all(bf16[64,16,128]{2,1,0:T(8,128)(2,1)S(1)} %get-tuple-element.26), channel_id=1, replica_groups=mesh['rows'=64,'cols'=8] {'rows'}, dimensions={0} | all-to-all | bytes 524288 | tf_op jit(solution)/shard_map/all_to_all | solution.py:299
  59.9 3.2 %attention_kernel.1 = bf16[64,8,128]{2,1,0:T(8,128)(2,1)} custom-call(bf16[64,16,128]{2,1,0:T(8,128)(2,1)S(1)} %all_to_all.10.packed_ref), custom_call_target="tpu_custom_call" | custom-call | bytes 1048576 | tf_op jit(solution)/shard_map/attention_kernel/pallas_call | solution.py:251
  63.0 7.4 %all-to-all-start.1 = ((bf16[64,8,128]{2,1,0:T(8,128)(2,1)}), bf16[64,8,128]{2,1,0:T(8,128)(2,1)S(1)}, u32[]{:S(2)}, u32[]{:S(2)}) async-start(bf16[64,8,128]{2,1,0:T(8,128)(2,1)} %attention_kernel.1), calls=%async_computation.1 | async-start | bytes 262144 | tf_op jit(solution)/shard_map/all_to_all | solution.py:309
  70.5 0.7 collective-permute-start.5
  71.1 5.5 %collective-permute-start.4 = (bf16[2,32,128]{2,1,0:T(8,128)(2,1)S(1)}, bf16[2,32,128]{2,1,0:T(8,128)(2,1)S(1)}, u32[]{:S(2)}, u32[]{:S(2)}) collective-permute-start(bf16[2,32,128]{2,1,0:T(8,128)(2,1)S(1)} %get-tuple-element.28), channel_id=1, source_target_pairs={{0,8},{16,24},{32,40},{48,56},{64,72},{80,88},{96,104},{112,120},{... | collective-permute-start | bytes 49160 | tf_op jit(solution)/shard_map/ppermute | solution.py:267
  76.7 1.3 %collective-permute-done.4.even_rim = bf16[2,32,128]{2,1,0:T(8,128)(2,1)S(1)} collective-permute-done((bf16[2,32,128]{2,1,0:T(8,128)(2,1)S(1)}, bf16[2,32,128]{2,1,0:T(8,128)(2,1)S(1)}, u32[]{:S(2)}, u32[]{:S(2)}) %collective-permute-start.4) | collective-permute-done | bytes 16416 | tf_op jit(solution)/shard_map/ppermute | solution.py:267
  77.9 6.0 %all-to-all-done.1.returned_ref = bf16[64,8,128]{2,1,0:T(8,128)(2,1)S(1)} async-done(((bf16[64,8,128]{2,1,0:T(8,128)(2,1)}), bf16[64,8,128]{2,1,0:T(8,128)(2,1)S(1)}, u32[]{:S(2)}, u32[]{:S(2)}) %all-to-all-start.1) | async-done | bytes 131104 | tf_op jit(solution)/shard_map/all_to_all | solution.py:309
  84.0 3.1 %merge_kernel.1 = (bf16[64,32,128]{2,1,0:T(8,128)(2,1)S(1)}, bf16[3,32,128]{2,1,0:T(8,128)(2,1)S(1)}) custom-call(bf16[64,8,128]{2,1,0:T(8,128)(2,1)S(1)} %all-to-all-done.1.returned_ref, bf16[128,256]{1,0:T(8,128)(2,1)S(1)} %get-tuple-element.27.tokens_ref, bf16[2,32,128]{2,1,0:T(8,128)(2,1)S(1)} %collective-permute-done.4.even_rim, ...), custom_call_target="tpu_custom_call" | custom-call | bytes 1048576 | tf_op jit(solution)/shard_map/merge_kernel/pallas_call | solution.py:251
  87.1 4.8 %collective-permute-start.7 = (bf16[3,32,128]{2,1,0:T(8,128)(2,1)S(1)}, bf16[3,32,128]{2,1,0:T(8,128)(2,1)S(1)}, u32[]{:S(2)}, u32[]{:S(2)}) collective-permute-start(bf16[3,32,128]{2,1,0:T(8,128)(2,1)S(1)} %get-tuple-element.32.strip_ref), channel_id=1, source_target_pairs={{1,2},{3,4},{5,6},{2,1},{4,3},{6,5},{9,10},{11,12},{13,14},{10,9},... | collective-permute-start | bytes 73736 | tf_op jit(solution)/shard_map/ppermute | solution.py:267
  91.9 1.9 %collective-permute-start.6 = (bf16[3,32,128]{2,1,0:T(8,128)(2,1)S(1)}, bf16[3,32,128]{2,1,0:T(8,128)(2,1)S(1)}, u32[]{:S(2)}, u32[]{:S(2)}) collective-permute-start(bf16[3,32,128]{2,1,0:T(8,128)(2,1)S(1)} %get-tuple-element.32.strip_ref), channel_id=1, source_target_pairs={{0,1},{2,3},{4,5},{6,7},{1,0},{3,2},{5,4},{7,6},{8,9},{10,11},{12,... | collective-permute-start | bytes 73736 | tf_op jit(solution)/shard_map/ppermute | solution.py:267
  93.9 1.2 %collective-permute-done.6.even_strip = bf16[3,32,128]{2,1,0:T(8,128)(2,1)S(1)} collective-permute-done((bf16[3,32,128]{2,1,0:T(8,128)(2,1)S(1)}, bf16[3,32,128]{2,1,0:T(8,128)(2,1)S(1)}, u32[]{:S(2)}, u32[]{:S(2)}) %collective-permute-start.6) | collective-permute-done | bytes 24608 | tf_op jit(solution)/shard_map/ppermute | solution.py:267
  95.0 2.3 %back_kernel.1 = bf16[32,64,128]{2,1,0:T(8,128)(2,1)} custom-call(bf16[64,32,128]{2,1,0:T(8,128)(2,1)S(1)} %get-tuple-element.31.map_ref, bf16[3,32,128]{2,1,0:T(8,128)(2,1)S(1)} %get-tuple-element.32.strip_ref, bf16[3,32,128]{2,1,0:T(8,128)(2,1)S(1)} %collective-permute-done.6.even_strip, bf16[3,32,128]{2,1,0:T(8,128)(2,1)S(1)} %collective-permute-done.7.other_strip, ...), custom_call_target="tpu_custom_call" | custom-call | bytes 1048576 | tf_op jit(solution)/shard_map/back_kernel/pallas_call | solution.py:251
  (20 shorter events, 0.1 us)
Async XLA Ops:
  0.0 1.0 %copy-start = (bf16[32,64,128]{2,1,0:T(8,128)(2,1)S(1)}, bf16[32,64,128]{2,1,0:T(8,128)(2,1)}, u32[]{:S(2)}) copy-start(bf16[32,64,128]{2,1,0:T(8,128)(2,1)} %x_ref.1) | copy-start | bytes 1572868
  1.5 8.3 %collective-permute-start.1 = (bf16[32,128]{1,0:T(8,128)(2,1)S(1)}, bf16[32,128]{1,0:T(8,128)(2,1)S(1)}, u32[]{:S(2)}, u32[]{:S(2)}) collective-permute-start(bf16[32,128]{1,0:T(8,128)(2,1)S(1)} %get-tuple-element.20), channel_id=1, source_target_pairs={{0,8},{16,24},{32,40},{48,56},{64,72},{80,88},{96,104},{112,120},{... | collective-permute-start | bytes 24584 | tf_op jit(solution)/shard_map/ppermute | solution.py:267
  5.5 4.4 %collective-permute-start = (bf16[32,128]{1,0:T(8,128)(2,1)S(1)}, bf16[32,128]{1,0:T(8,128)(2,1)S(1)}, u32[]{:S(2)}, u32[]{:S(2)}) collective-permute-start(bf16[32,128]{1,0:T(8,128)(2,1)S(1)} %get-tuple-element.20), channel_id=1, source_target_pairs={{8,16},{24,32},{40,48},{56,64},{72,80},{88,96},{104,112},{120,128}... | collective-permute-start | bytes 24584 | tf_op jit(solution)/shard_map/ppermute | solution.py:267
  6.1 1.2 %copy-start.6 = (bf16[2048,256]{1,0:T(8,128)(2,1)S(1)}, bf16[2048,256]{1,0:T(8,128)(2,1)}, u32[]{:S(2)}) copy-start(bf16[2048,256]{1,0:T(8,128)(2,1)} %embed_ref.1) | copy-start | bytes 3145732
  7.4 1.2 %copy-start.7 = (bf16[256,2048]{1,0:T(8,128)(2,1)S(1)}, bf16[256,2048]{1,0:T(8,128)(2,1)}, u32[]{:S(2)}) copy-start(bf16[256,2048]{1,0:T(8,128)(2,1)} %unpatch_ref.1) | copy-start | bytes 3145732
  8.6 9.6 %copy-start.1 = (bf16[256,768]{1,0:T(8,128)(2,1)S(1)}, bf16[256,768]{1,0:T(8,128)(2,1)}, u32[]{:S(2)}) copy-start(bf16[256,768]{1,0:T(8,128)(2,1)} %qkv_ref.1) | copy-start | bytes 1179652
  9.9 8.3 %copy-start.3 = (bf16[32,288]{1,0:T(8,128)(2,1)S(1)}, bf16[32,288]{1,0:T(8,128)(2,1)}, u32[]{:S(2)}) copy-start(bf16[32,288]{1,0:T(8,128)(2,1)} %conv_ref.2) | copy-start | bytes 55300
  9.9 8.3 %copy-start.5 = (bf16[16,8,8]{0,2,1:T(8,128)(2,1)S(1)}, bf16[16,8,8]{0,2,1:T(8,128)(2,1)}, u32[]{:S(2)}) copy-start(bf16[16,8,8]{0,2,1:T(8,128)(2,1)} %param.12) | copy-start | bytes 6148
  9.9 7.4 %collective-permute-start.3 = (bf16[3,32,128]{2,1,0:T(8,128)(2,1)S(1)}, bf16[3,32,128]{2,1,0:T(8,128)(2,1)S(1)}, u32[]{:S(2)}, u32[]{:S(2)}) collective-permute-start(bf16[3,32,128]{2,1,0:T(8,128)(2,1)S(1)} %pad_maximum_fusion.strip_ref), channel_id=1, source_target_pairs={{1,2},{3,4},{5,6},{2,1},{4,3},{6,5},{9,10},{11,12},{13,14},{10,9},... | collective-permute-start | bytes 73736 | tf_op jit(solution)/shard_map/ppermute | solution.py:267
  14.0 4.2 %collective-permute-start.2 = (bf16[3,32,128]{2,1,0:T(8,128)(2,1)S(1)}, bf16[3,32,128]{2,1,0:T(8,128)(2,1)S(1)}, u32[]{:S(2)}, u32[]{:S(2)}) collective-permute-start(bf16[3,32,128]{2,1,0:T(8,128)(2,1)S(1)} %pad_maximum_fusion.strip_ref), channel_id=1, source_target_pairs={{0,1},{2,3},{4,5},{6,7},{1,0},{3,2},{5,4},{7,6},{8,9},{10,11},{12,... | collective-permute-start | bytes 73736 | tf_op jit(solution)/shard_map/ppermute | solution.py:267
  63.0 20.9 %copy-start.2 = (bf16[256,256]{1,0:T(8,128)(2,1)S(1)}, bf16[256,256]{1,0:T(8,128)(2,1)}, u32[]{:S(2)}) copy-start(bf16[256,256]{1,0:T(8,128)(2,1)} %out_weight_ref.1) | copy-start | bytes 393220
  63.0 20.9 %all-to-all-start.1 = ((bf16[64,8,128]{2,1,0:T(8,128)(2,1)}), bf16[64,8,128]{2,1,0:T(8,128)(2,1)S(1)}, u32[]{:S(2)}, u32[]{:S(2)}) async-start(bf16[64,8,128]{2,1,0:T(8,128)(2,1)} %attention_kernel.1), calls=%async_computation.1 | async-start | bytes 262144 | tf_op jit(solution)/shard_map/all_to_all | solution.py:309
  70.5 6.2 %collective-permute-start.5 = (bf16[2,32,128]{2,1,0:T(8,128)(2,1)S(1)}, bf16[2,32,128]{2,1,0:T(8,128)(2,1)S(1)}, u32[]{:S(2)}, u32[]{:S(2)}) collective-permute-start(bf16[2,32,128]{2,1,0:T(8,128)(2,1)S(1)} %get-tuple-element.28), channel_id=1, source_target_pairs={{8,16},{24,32},{40,48},{56,64},{72,80},{88,96},{104,112},{120,128}... | collective-permute-start | bytes 49160 | tf_op jit(solution)/shard_map/ppermute | solution.py:267
  71.1 6.8 %collective-permute-start.4 = (bf16[2,32,128]{2,1,0:T(8,128)(2,1)S(1)}, bf16[2,32,128]{2,1,0:T(8,128)(2,1)S(1)}, u32[]{:S(2)}, u32[]{:S(2)}) collective-permute-start(bf16[2,32,128]{2,1,0:T(8,128)(2,1)S(1)} %get-tuple-element.28), channel_id=1, source_target_pairs={{0,8},{16,24},{32,40},{48,56},{64,72},{80,88},{96,104},{112,120},{... | collective-permute-start | bytes 49160 | tf_op jit(solution)/shard_map/ppermute | solution.py:267
  84.0 11.1 %copy-start.4 = (bf16[32,288]{1,0:T(8,128)(2,1)S(1)}, bf16[32,288]{1,0:T(8,128)(2,1)}, u32[]{:S(2)}) copy-start(bf16[32,288]{1,0:T(8,128)(2,1)} %conv_ref.3) | copy-start | bytes 55300
  87.1 6.7 %collective-permute-start.7 = (bf16[3,32,128]{2,1,0:T(8,128)(2,1)S(1)}, bf16[3,32,128]{2,1,0:T(8,128)(2,1)S(1)}, u32[]{:S(2)}, u32[]{:S(2)}) collective-permute-start(bf16[3,32,128]{2,1,0:T(8,128)(2,1)S(1)} %get-tuple-element.32.strip_ref), channel_id=1, source_target_pairs={{1,2},{3,4},{5,6},{2,1},{4,3},{6,5},{9,10},{11,12},{13,14},{10,9},... | collective-permute-start | bytes 73736 | tf_op jit(solution)/shard_map/ppermute | solution.py:267
  91.9 3.1 %collective-permute-start.6 = (bf16[3,32,128]{2,1,0:T(8,128)(2,1)S(1)}, bf16[3,32,128]{2,1,0:T(8,128)(2,1)S(1)}, u32[]{:S(2)}, u32[]{:S(2)}) collective-permute-start(bf16[3,32,128]{2,1,0:T(8,128)(2,1)S(1)} %get-tuple-element.32.strip_ref), channel_id=1, source_target_pairs={{0,1},{2,3},{4,5},{6,7},{1,0},{3,2},{5,4},{7,6},{8,9},{10,11},{12,... | collective-permute-start | bytes 73736 | tf_op jit(solution)/shard_map/ppermute | solution.py:267

commit v5 on v4

--- a/solution.py
+++ b/solution.py
@@ -21,6 +21,7 @@
 WINDOW = 8
 QUAD = 4
 epsilon = 1e-05
+LOG2_E = 1.4426950408889634
 
 f32 = jnp.float32
 bf16 = jnp.bfloat16
@@ -93,9 +94,12 @@
     return jnp.concatenate(rows, axis=0).astype(bf16)
 
 
-def conv_quad(band, taps, group):
-    window = taps[group * QUAD : group * QUAD + QUAD + 2].reshape((QUAD + 2) * 3 * C, L)
-    return jnp.dot(band, window, preferred_element_type=f32)
+def conv_pair(band, taps, group):
+    windows = [
+        taps[g * QUAD : g * QUAD + QUAD + 2].reshape((QUAD + 2) * 3 * C, L) for g in (group, group + 1)
+    ]
+    both = jnp.dot(band, jnp.concatenate(windows, axis=1), preferred_element_type=f32)
+    return both[:, :L], both[:, L:]
 
 
 def front_kernel(
@@ -107,12 +111,11 @@
     row = iota((L, L), 0)
     select = one_hot(iota((L, L), 1) == (row % PR) * PATCH + row // PR)
     for p in range(PC):
-        for half in range(PATCH // QUAD):
-            group = p * (PATCH // QUAD) + half
-            value = conv_quad(band, taps, group)
+        group = p * (PATCH // QUAD)
+        for half, value in enumerate(conv_pair(band, taps, group)):
             value = value / (1.0 + jnp.exp(-value))
             for i in range(QUAD):
-                w = group * QUAD + i
+                w = (group + half) * QUAD + i
                 cell = taps[w + 1, C : 2 * C, :].astype(f32) + value[i * C : (i + 1) * C]
                 mixed_ref[w] = cell.astype(bf16)
         block = mixed_ref[p * PATCH : (p + 1) * PATCH].reshape(PATCH * C, L)
@@ -153,17 +156,21 @@
     pick = one_hot((iota((8, L), 1) == 3 * HEAD_DIM))
     bias = lax.dot_general(pick, rows, NT, preferred_element_type=f32)[0:1]
     values = jnp.where((lane >= 2 * HEAD_DIM) & (lane < 3 * HEAD_DIM), wide, 0.0)
-    scale = HEAD_DIM ** (-0.5)
+    scale = HEAD_DIM ** (-0.5) * LOG2_E
+    bias = bias * LOG2_E
+    block_of = iota((SEQ // 4, L), 1) // HEAD_DIM
     total = jnp.zeros((SEQ // 4, L), f32)
     for quarter in range(4):
         queries = rows_f32[pl.ds(quarter, SEQ // 4, stride=4), :].astype(bf16)
         scores = lax.dot_general(queries, rows, NT, preferred_element_type=f32) * scale + bias
         peak = jnp.max(scores, axis=1, keepdims=True)
-        weights = jnp.exp(scores - peak)
-        share = (weights * (1.0 / jnp.sum(weights, axis=1, keepdims=True))).astype(bf16)
+        weights = jnp.exp2(scores - peak).astype(bf16)
         shift = (quarter * HEAD_DIM - 2 * HEAD_DIM) % L
-        placed = (pltpu.roll(values, shift, 1) if shift else values).astype(bf16)
-        total = total + jnp.dot(share, placed, preferred_element_type=f32)
+        placed = pltpu.roll(values, shift, 1) if shift else values
+        placed = jnp.where(lane // HEAD_DIM == quarter, placed, 1.0).astype(bf16)
+        product = jnp.dot(weights, placed, preferred_element_type=f32)
+        sums = pltpu.roll(product, HEAD_DIM, 1)
+        total = jnp.where(block_of == quarter, product / sums, total)
     pad = jnp.zeros((8, L), f32)
     padded[0:8, :] = pad
     padded[8 : 8 + SEQ // 4, :] = total
@@ -219,40 +226,54 @@
     strip_ref[2] = outer.astype(bf16)
     repeat = one_hot(iota((PC * L, WIDE), 0) // PATCH == iota((PC * L, WIDE), 1))
     repeated[...] = jnp.dot(repeat, updated, preferred_element_type=f32)
-    inner = iota((L, D), 0) % PATCH
-    for p in range(PC):
-        block = repeated[p * L : (p + 1) * L, :]
-        grown = jnp.zeros((D, L), f32)
+    inner = iota((2 * L, D), 0) % PATCH
+    for pair in range(PC // 2):
+        block = repeated[pair * 2 * L : (pair + 1) * 2 * L, :]
+        grown = jnp.zeros((D, 2 * L), f32)
         for i in range(PATCH):
             part = jnp.where(inner == i, block, 0.0).astype(bf16)
             grown = grown + lax.dot_general(unpatch_ref[i], part, NT, preferred_element_type=f32)
-        cells = mixed_ref[p * PATCH : (p + 1) * PATCH].astype(f32) + grown.reshape(PATCH, C, L)
-        merged_ref[p * PATCH : (p + 1) * PATCH] = cells.astype(bf16)
+        for side in range(2):
+            p = pair * 2 + side
+            cells = mixed_ref[p * PATCH : (p + 1) * PATCH].astype(f32)
+            cells = cells + grown[:, side * L : (side + 1) * L].reshape(PATCH, C, L)
+            merged_ref[p * PATCH : (p + 1) * PATCH] = cells.astype(bf16)
     strip_ref[0] = merged_ref[0]
     strip_ref[1] = merged_ref[W - 1]
 
 
-def back_kernel(map_ref, strip_ref, even_strip, other_strip, conv_ref, out_ref, taps, result):
+def back_kernel(map_ref, strip_ref, even_strip, other_strip, conv_ref, out_ref, taps, result, staged, done):
     fill_taps(map_ref, strip_ref, even_strip, other_strip, taps)
     band = banded(conv_ref[...])
-    for group in range(W // QUAD):
-        value = conv_quad(band, taps, group)
-        for i in range(QUAD):
-            w = group * QUAD + i
-            result[w] = taps[w + 1, C : 2 * C, :].astype(f32) + value[i * C : (i + 1) * C]
-    out_ref[...] = jnp.swapaxes(result[...], 0, 1).astype(bf16)
+    copies = []
+    for group in range(0, W // QUAD, 2):
+        for half, value in enumerate(conv_pair(band, taps, group)):
+            for i in range(QUAD):
+                w = (group + half) * QUAD + i
+                result[w] = taps[w + 1, C : 2 * C, :].astype(f32) + value[i * C : (i + 1) * C]
+        if group % 4 == 2:
+            part = group // 4
+            columns = slice(part * 2 * PATCH, (part + 1) * 2 * PATCH)
+            staged[:, columns, :] = jnp.swapaxes(result[columns], 0, 1).astype(bf16)
+            copies.append(
+                pltpu.make_async_copy(staged.at[:, columns, :], out_ref.at[:, columns, :], done.at[part])
+            )
+            copies[-1].start()
+    for copy in copies:
+        copy.wait()
 
 
 def shape(*dims, dtype=bf16):
     return pltpu.VMEM(dims, dtype)
 
 
-def call(kernel, outs, scratch, *args, flops=0):
+def call(kernel, outs, scratch, *args, flops=0, **specs):
     return pl.pallas_call(
         kernel,
         out_shape=outs,
         in_specs=[pl.BlockSpec(memory_space=pltpu.VMEM)] * len(args),
         scratch_shapes=scratch,
+        **specs,
         name=kernel.__name__,
         cost_estimate=pl.CostEstimate(flops=flops, transcendentals=0, bytes_accessed=1 << 20),
         compiler_params=pltpu.CompilerParams(vmem_limit_bytes=24 << 20),
@@ -316,8 +337,12 @@
     return call(
         back_kernel,
         jax.ShapeDtypeStruct((C, W, L), bf16),
-        [pltpu.VMEM((W + 2, 3 * C, L), bf16), pltpu.VMEM((W, C, L), f32)],
+        [
+            pltpu.VMEM((W + 2, 3 * C, L), bf16), pltpu.VMEM((W, C, L), f32),
+            pltpu.VMEM((C, W, L), bf16), pltpu.SemaphoreType.DMA((4,)),
+        ],
         merged, strip, *exchange(strip, "cols"), conv_out,
+        out_specs=pl.BlockSpec(memory_space=pl.ANY),
     )
 
 

time: 97.9 us -> 96.5 us (0.986)
  Pallas kernels: 14 us -> 12.6 us
    pallas_call x6, Pallas kernels: 14 us -> 12.6 us  [call(): pl.pallas_call(kernel, out_shape=outs, in_specs=[pl.BlockSpec(memory_spac...]
where the time goes in v5:
time: 96.5 us; the launch traced here: 96 us
  blocking collectives  38 us (39%)
  starting transfers between devices  32.2 us (33%)
  Pallas kernels  12.6 us (13%)
  waiting for transfers between devices  9.43 us (10%)
  local copies, waits for them, and re-layouts  3.51 us (4%)
    all_to_all x1, blocking collectives, per_device(): lax.all_to_all(packed, 'rows', split_axis=0, concat_axis=0, tiled=True)  38 us
    ppermute x8, starting transfers between devices, exchange(): swaps.append(lax.ppermute(block, axis, pairs + [(j, i) for i, j in pairs]))  24.7 us
    pallas_call x6, Pallas kernels, call(): pl.pallas_call(kernel, out_shape=outs, in_specs=[pl.BlockSpec(memory_spac...  12.6 us
    all_to_all x1, starting transfers between devices, per_device(): lax.all_to_all(heads_out, 'rows', split_axis=0, concat_axis=0, tiled=True)  7.42 us
    all_to_all x1, waiting for transfers between devices, per_device(): lax.all_to_all(heads_out, 'rows', split_axis=0, concat_axis=0, tiled=True)  6.01 us
    unnamed x16, local copies, waits for them, and re-layouts  3.51 us
    ppermute x8, waiting for transfers between devices, exchange(): swaps.append(lax.ppermute(block, axis, pairs + [(j, i) for i, j in pairs]))  3.42 us
  transfers between devices with their start and end apart: 9, of which 4 were waited for; matrix products, arithmetic and copies ran while one was open for 0% of the time, Pallas kernels for 1%

profile of v5, /device:TPU:1, one launch (start us, length us, event | category | flops | bytes accessed | tf_op | source)
XLA Modules:
  0.0 96.0 jit_solution(92849244647335349)
XLA Ops:
  0.0 1.0 %copy-done = bf16[32,64,128]{2,1,0:T(8,128)(2,1)S(1)} copy-done((bf16[32,64,128]{2,1,0:T(8,128)(2,1)S(1)}, bf16[32,64,128]{2,1,0:T(8,128)(2,1)}, u32[]{:S(2)}) %copy-start) | copy-done | bytes 524312
  1.0 0.5 turn_kernel.1
  1.5 3.9 %collective-permute-start.1 = (bf16[32,128]{1,0:T(8,128)(2,1)S(1)}, bf16[32,128]{1,0:T(8,128)(2,1)S(1)}, u32[]{:S(2)}, u32[]{:S(2)}) collective-permute-start(bf16[32,128]{1,0:T(8,128)(2,1)S(1)} %get-tuple-element.20), channel_id=1, source_target_pairs={{0,8},{16,24},{32,40},{48,56},{64,72},{80,88},{96,104},{112,120},{... | collective-permute-start | bytes 24584 | tf_op jit(solution)/shard_map/ppermute | solution.py:288
  5.5 0.7 collective-permute-start
  6.1 0.0 copy-start.6
  6.2 1.2 %copy-done.6 = bf16[2048,256]{1,0:T(8,128)(2,1)S(1)} copy-done((bf16[2048,256]{1,0:T(8,128)(2,1)S(1)}, bf16[2048,256]{1,0:T(8,128)(2,1)}, u32[]{:S(2)}) %copy-start.6) | copy-done | bytes 1048600
  7.4 1.2 %copy-done.7 = bf16[256,2048]{1,0:T(8,128)(2,1)S(1)} copy-done((bf16[256,2048]{1,0:T(8,128)(2,1)S(1)}, bf16[256,2048]{1,0:T(8,128)(2,1)}, u32[]{:S(2)}) %copy-start.7) | copy-done | bytes 1048600
  8.6 1.2 %weights_kernel.1 = (bf16[8,256,256]{2,1,0:T(8,128)(2,1)S(1)}, bf16[8,256,256]{2,1,0:T(8,128)(2,1)S(1)}) custom-call(bf16[2048,256]{1,0:T(8,128)(2,1)S(1)} %copy-done.6, bf16[256,2048]{1,0:T(8,128)(2,1)S(1)} %copy-done.7), custom_call_target="tpu_custom_call" | custom-call | flops 4294967296 | bytes 1048576 | tf_op jit(solution)/shard_map/weights_kernel/pallas_call | solution.py:271
  9.9 4.0 %collective-permute-start.3 = (bf16[3,32,128]{2,1,0:T(8,128)(2,1)S(1)}, bf16[3,32,128]{2,1,0:T(8,128)(2,1)S(1)}, u32[]{:S(2)}, u32[]{:S(2)}) collective-permute-start(bf16[3,32,128]{2,1,0:T(8,128)(2,1)S(1)} %pad_maximum_fusion.strip_ref), channel_id=1, source_target_pairs={{1,2},{3,4},{5,6},{2,1},{4,3},{6,5},{9,10},{11,12},{13,14},{10,9},... | collective-permute-start | bytes 73736 | tf_op jit(solution)/shard_map/ppermute | solution.py:288
  14.0 3.3 %collective-permute-start.2 = (bf16[3,32,128]{2,1,0:T(8,128)(2,1)S(1)}, bf16[3,32,128]{2,1,0:T(8,128)(2,1)S(1)}, u32[]{:S(2)}, u32[]{:S(2)}) collective-permute-start(bf16[3,32,128]{2,1,0:T(8,128)(2,1)S(1)} %pad_maximum_fusion.strip_ref), channel_id=1, source_target_pairs={{0,1},{2,3},{4,5},{6,7},{1,0},{3,2},{5,4},{7,6},{8,9},{10,11},{12,... | collective-permute-start | bytes 73736 | tf_op jit(solution)/shard_map/ppermute | solution.py:288
  17.4 0.8 collective-permute-done.2.even_strip
  18.2 3.8 %front_kernel.1 = (bf16[64,32,128]{2,1,0:T(8,128)(2,1)S(1)}, bf16[128,256]{1,0:T(8,128)(2,1)S(1)}, bf16[64,16,128]{2,1,0:T(8,128)(2,1)S(1)}, bf16[2,32,128]{2,1,0:T(8,128)(2,1)S(1)}) custom-call(bf16[64,32,128]{2,1,0:T(8,128)(2,1)S(1)} %get-tuple-element.19.map_ref, bf16[3,32,128]{2,1,0:T(8,128)(2,1)S(1)} %pad_maximum_fusion.strip_ref, ...), custom_call_target="tpu_custom_call" | custom-call | bytes 1048576 | tf_op jit(solution)/shard_map/front_kernel/pallas_call | solution.py:271
  22.0 38.0 %all_to_all.10.packed_ref = bf16[64,16,128]{2,1,0:T(8,128)(2,1)S(1)} all-to-all(bf16[64,16,128]{2,1,0:T(8,128)(2,1)S(1)} %get-tuple-element.26), channel_id=1, replica_groups=mesh['rows'=64,'cols'=8] {'rows'}, dimensions={0} | all-to-all | bytes 524288 | tf_op jit(solution)/shard_map/all_to_all | solution.py:320
  60.0 3.0 %attention_kernel.1 = bf16[64,8,128]{2,1,0:T(8,128)(2,1)} custom-call(bf16[64,16,128]{2,1,0:T(8,128)(2,1)S(1)} %all_to_all.10.packed_ref), custom_call_target="tpu_custom_call" | custom-call | bytes 1048576 | tf_op jit(solution)/shard_map/attention_kernel/pallas_call | solution.py:271
  63.0 7.4 %all-to-all-start.1 = ((bf16[64,8,128]{2,1,0:T(8,128)(2,1)}), bf16[64,8,128]{2,1,0:T(8,128)(2,1)S(1)}, u32[]{:S(2)}, u32[]{:S(2)}) async-start(bf16[64,8,128]{2,1,0:T(8,128)(2,1)} %attention_kernel.1), calls=%async_computation.1 | async-start | bytes 262144 | tf_op jit(solution)/shard_map/all_to_all | solution.py:330
  70.4 0.7 collective-permute-start.5
  71.1 5.3 %collective-permute-start.4 = (bf16[2,32,128]{2,1,0:T(8,128)(2,1)S(1)}, bf16[2,32,128]{2,1,0:T(8,128)(2,1)S(1)}, u32[]{:S(2)}, u32[]{:S(2)}) collective-permute-start(bf16[2,32,128]{2,1,0:T(8,128)(2,1)S(1)} %get-tuple-element.28), channel_id=1, source_target_pairs={{0,8},{16,24},{32,40},{48,56},{64,72},{80,88},{96,104},{112,120},{... | collective-permute-start | bytes 49160 | tf_op jit(solution)/shard_map/ppermute | solution.py:288
  76.5 1.4 %collective-permute-done.4.even_rim = bf16[2,32,128]{2,1,0:T(8,128)(2,1)S(1)} collective-permute-done((bf16[2,32,128]{2,1,0:T(8,128)(2,1)S(1)}, bf16[2,32,128]{2,1,0:T(8,128)(2,1)S(1)}, u32[]{:S(2)}, u32[]{:S(2)}) %collective-permute-start.4) | collective-permute-done | bytes 16416 | tf_op jit(solution)/shard_map/ppermute | solution.py:288
  77.9 6.0 %all-to-all-done.1.returned_ref = bf16[64,8,128]{2,1,0:T(8,128)(2,1)S(1)} async-done(((bf16[64,8,128]{2,1,0:T(8,128)(2,1)}), bf16[64,8,128]{2,1,0:T(8,128)(2,1)S(1)}, u32[]{:S(2)}, u32[]{:S(2)}) %all-to-all-start.1) | async-done | bytes 131104 | tf_op jit(solution)/shard_map/all_to_all | solution.py:330
  83.9 2.0 %merge_kernel.1 = (bf16[64,32,128]{2,1,0:T(8,128)(2,1)S(1)}, bf16[3,32,128]{2,1,0:T(8,128)(2,1)S(1)}) custom-call(bf16[64,8,128]{2,1,0:T(8,128)(2,1)S(1)} %all-to-all-done.1.returned_ref, bf16[128,256]{1,0:T(8,128)(2,1)S(1)} %get-tuple-element.27.tokens_ref, bf16[2,32,128]{2,1,0:T(8,128)(2,1)S(1)} %collective-permute-done.4.even_rim, ...), custom_call_target="tpu_custom_call" | custom-call | bytes 1048576 | tf_op jit(solution)/shard_map/merge_kernel/pallas_call | solution.py:271
  86.0 4.8 %collective-permute-start.7 = (bf16[3,32,128]{2,1,0:T(8,128)(2,1)S(1)}, bf16[3,32,128]{2,1,0:T(8,128)(2,1)S(1)}, u32[]{:S(2)}, u32[]{:S(2)}) collective-permute-start(bf16[3,32,128]{2,1,0:T(8,128)(2,1)S(1)} %get-tuple-element.32.strip_ref), channel_id=1, source_target_pairs={{1,2},{3,4},{5,6},{2,1},{4,3},{6,5},{9,10},{11,12},{13,14},{10,9},... | collective-permute-start | bytes 73736 | tf_op jit(solution)/shard_map/ppermute | solution.py:288
  90.8 1.9 %collective-permute-start.6 = (bf16[3,32,128]{2,1,0:T(8,128)(2,1)S(1)}, bf16[3,32,128]{2,1,0:T(8,128)(2,1)S(1)}, u32[]{:S(2)}, u32[]{:S(2)}) collective-permute-start(bf16[3,32,128]{2,1,0:T(8,128)(2,1)S(1)} %get-tuple-element.32.strip_ref), channel_id=1, source_target_pairs={{0,1},{2,3},{4,5},{6,7},{1,0},{3,2},{5,4},{7,6},{8,9},{10,11},{12,... | collective-permute-start | bytes 73736 | tf_op jit(solution)/shard_map/ppermute | solution.py:288
  92.7 1.2 %collective-permute-done.6.even_strip = bf16[3,32,128]{2,1,0:T(8,128)(2,1)S(1)} collective-permute-done((bf16[3,32,128]{2,1,0:T(8,128)(2,1)S(1)}, bf16[3,32,128]{2,1,0:T(8,128)(2,1)S(1)}, u32[]{:S(2)}, u32[]{:S(2)}) %collective-permute-start.6) | collective-permute-done | bytes 24608 | tf_op jit(solution)/shard_map/ppermute | solution.py:288
  93.9 2.1 %back_kernel.1 = bf16[32,64,128]{2,1,0:T(8,128)(2,1)} custom-call(bf16[64,32,128]{2,1,0:T(8,128)(2,1)S(1)} %get-tuple-element.31.map_ref, bf16[3,32,128]{2,1,0:T(8,128)(2,1)S(1)} %get-tuple-element.32.strip_ref, bf16[3,32,128]{2,1,0:T(8,128)(2,1)S(1)} %collective-permute-done.6.even_strip, bf16[3,32,128]{2,1,0:T(8,128)(2,1)S(1)} %collective-permute-done.7.other_strip, ...), custom_call_target="tpu_custom_call" | custom-call | bytes 1048576 | tf_op jit(solution)/shard_map/back_kernel/pallas_call | solution.py:271
  (20 shorter events, 0.1 us)
Async XLA Ops:
  0.0 1.0 %copy-start = (bf16[32,64,128]{2,1,0:T(8,128)(2,1)S(1)}, bf16[32,64,128]{2,1,0:T(8,128)(2,1)}, u32[]{:S(2)}) copy-start(bf16[32,64,128]{2,1,0:T(8,128)(2,1)} %x_ref.1) | copy-start | bytes 1572868
  1.5 8.3 %collective-permute-start.1 = (bf16[32,128]{1,0:T(8,128)(2,1)S(1)}, bf16[32,128]{1,0:T(8,128)(2,1)S(1)}, u32[]{:S(2)}, u32[]{:S(2)}) collective-permute-start(bf16[32,128]{1,0:T(8,128)(2,1)S(1)} %get-tuple-element.20), channel_id=1, source_target_pairs={{0,8},{16,24},{32,40},{48,56},{64,72},{80,88},{96,104},{112,120},{... | collective-permute-start | bytes 24584 | tf_op jit(solution)/shard_map/ppermute | solution.py:288
  5.5 4.4 %collective-permute-start = (bf16[32,128]{1,0:T(8,128)(2,1)S(1)}, bf16[32,128]{1,0:T(8,128)(2,1)S(1)}, u32[]{:S(2)}, u32[]{:S(2)}) collective-permute-start(bf16[32,128]{1,0:T(8,128)(2,1)S(1)} %get-tuple-element.20), channel_id=1, source_target_pairs={{8,16},{24,32},{40,48},{56,64},{72,80},{88,96},{104,112},{120,128}... | collective-permute-start | bytes 24584 | tf_op jit(solution)/shard_map/ppermute | solution.py:288
  6.1 1.2 %copy-start.6 = (bf16[2048,256]{1,0:T(8,128)(2,1)S(1)}, bf16[2048,256]{1,0:T(8,128)(2,1)}, u32[]{:S(2)}) copy-start(bf16[2048,256]{1,0:T(8,128)(2,1)} %embed_ref.1) | copy-start | bytes 3145732
  7.4 1.2 %copy-start.7 = (bf16[256,2048]{1,0:T(8,128)(2,1)S(1)}, bf16[256,2048]{1,0:T(8,128)(2,1)}, u32[]{:S(2)}) copy-start(bf16[256,2048]{1,0:T(8,128)(2,1)} %unpatch_ref.1) | copy-start | bytes 3145732
  8.6 9.6 %copy-start.1 = (bf16[256,768]{1,0:T(8,128)(2,1)S(1)}, bf16[256,768]{1,0:T(8,128)(2,1)}, u32[]{:S(2)}) copy-start(bf16[256,768]{1,0:T(8,128)(2,1)} %qkv_ref.1) | copy-start | bytes 1179652
  9.9 8.3 %copy-start.3 = (bf16[32,288]{1,0:T(8,128)(2,1)S(1)}, bf16[32,288]{1,0:T(8,128)(2,1)}, u32[]{:S(2)}) copy-start(bf16[32,288]{1,0:T(8,128)(2,1)} %conv_ref.2) | copy-start | bytes 55300
  9.9 8.3 %copy-start.5 = (bf16[16,8,8]{0,2,1:T(8,128)(2,1)S(1)}, bf16[16,8,8]{0,2,1:T(8,128)(2,1)}, u32[]{:S(2)}) copy-start(bf16[16,8,8]{0,2,1:T(8,128)(2,1)} %param.12) | copy-start | bytes 6148
  9.9 7.4 %collective-permute-start.3 = (bf16[3,32,128]{2,1,0:T(8,128)(2,1)S(1)}, bf16[3,32,128]{2,1,0:T(8,128)(2,1)S(1)}, u32[]{:S(2)}, u32[]{:S(2)}) collective-permute-start(bf16[3,32,128]{2,1,0:T(8,128)(2,1)S(1)} %pad_maximum_fusion.strip_ref), channel_id=1, source_target_pairs={{1,2},{3,4},{5,6},{2,1},{4,3},{6,5},{9,10},{11,12},{13,14},{10,9},... | collective-permute-start | bytes 73736 | tf_op jit(solution)/shard_map/ppermute | solution.py:288
  14.0 4.2 %collective-permute-start.2 = (bf16[3,32,128]{2,1,0:T(8,128)(2,1)S(1)}, bf16[3,32,128]{2,1,0:T(8,128)(2,1)S(1)}, u32[]{:S(2)}, u32[]{:S(2)}) collective-permute-start(bf16[3,32,128]{2,1,0:T(8,128)(2,1)S(1)} %pad_maximum_fusion.strip_ref), channel_id=1, source_target_pairs={{0,1},{2,3},{4,5},{6,7},{1,0},{3,2},{5,4},{7,6},{8,9},{10,11},{12,... | collective-permute-start | bytes 73736 | tf_op jit(solution)/shard_map/ppermute | solution.py:288
  63.0 20.9 %copy-start.2 = (bf16[256,256]{1,0:T(8,128)(2,1)S(1)}, bf16[256,256]{1,0:T(8,128)(2,1)}, u32[]{:S(2)}) copy-start(bf16[256,256]{1,0:T(8,128)(2,1)} %out_weight_ref.1) | copy-start | bytes 393220
  63.0 20.9 %all-to-all-start.1 = ((bf16[64,8,128]{2,1,0:T(8,128)(2,1)}), bf16[64,8,128]{2,1,0:T(8,128)(2,1)S(1)}, u32[]{:S(2)}, u32[]{:S(2)}) async-start(bf16[64,8,128]{2,1,0:T(8,128)(2,1)} %attention_kernel.1), calls=%async_computation.1 | async-start | bytes 262144 | tf_op jit(solution)/shard_map/all_to_all | solution.py:330
  70.4 6.0 %collective-permute-start.5 = (bf16[2,32,128]{2,1,0:T(8,128)(2,1)S(1)}, bf16[2,32,128]{2,1,0:T(8,128)(2,1)S(1)}, u32[]{:S(2)}, u32[]{:S(2)}) collective-permute-start(bf16[2,32,128]{2,1,0:T(8,128)(2,1)S(1)} %get-tuple-element.28), channel_id=1, source_target_pairs={{8,16},{24,32},{40,48},{56,64},{72,80},{88,96},{104,112},{120,128}... | collective-permute-start | bytes 49160 | tf_op jit(solution)/shard_map/ppermute | solution.py:288
  71.1 6.8 %collective-permute-start.4 = (bf16[2,32,128]{2,1,0:T(8,128)(2,1)S(1)}, bf16[2,32,128]{2,1,0:T(8,128)(2,1)S(1)}, u32[]{:S(2)}, u32[]{:S(2)}) collective-permute-start(bf16[2,32,128]{2,1,0:T(8,128)(2,1)S(1)} %get-tuple-element.28), channel_id=1, source_target_pairs={{0,8},{16,24},{32,40},{48,56},{64,72},{80,88},{96,104},{112,120},{... | collective-permute-start | bytes 49160 | tf_op jit(solution)/shard_map/ppermute | solution.py:288
  83.9 10.0 %copy-start.4 = (bf16[32,288]{1,0:T(8,128)(2,1)S(1)}, bf16[32,288]{1,0:T(8,128)(2,1)}, u32[]{:S(2)}) copy-start(bf16[32,288]{1,0:T(8,128)(2,1)} %conv_ref.3) | copy-start | bytes 55300
  86.0 6.8 %collective-permute-start.7 = (bf16[3,32,128]{2,1,0:T(8,128)(2,1)S(1)}, bf16[3,32,128]{2,1,0:T(8,128)(2,1)S(1)}, u32[]{:S(2)}, u32[]{:S(2)}) collective-permute-start(bf16[3,32,128]{2,1,0:T(8,128)(2,1)S(1)} %get-tuple-element.32.strip_ref), channel_id=1, source_target_pairs={{1,2},{3,4},{5,6},{2,1},{4,3},{6,5},{9,10},{11,12},{13,14},{10,9},... | collective-permute-start | bytes 73736 | tf_op jit(solution)/shard_map/ppermute | solution.py:288
  90.8 3.1 %collective-permute-start.6 = (bf16[3,32,128]{2,1,0:T(8,128)(2,1)S(1)}, bf16[3,32,128]{2,1,0:T(8,128)(2,1)S(1)}, u32[]{:S(2)}, u32[]{:S(2)}) collective-permute-start(bf16[3,32,128]{2,1,0:T(8,128)(2,1)S(1)} %get-tuple-element.32.strip_ref), channel_id=1, source_target_pairs={{0,1},{2,3},{4,5},{6,7},{1,0},{3,2},{5,4},{7,6},{8,9},{10,11},{12,... | collective-permute-start | bytes 73736 | tf_op jit(solution)/shard_map/ppermute | solution.py:288

commit v6 on v5

--- a/solution.py
+++ b/solution.py
@@ -327,6 +327,7 @@
         ],
         arrived,
     )
+    heads_out, even_rim, other_rim = lax.optimization_barrier((heads_out, even_rim, other_rim))
     returned = lax.all_to_all(heads_out, "rows", split_axis=0, concat_axis=0, tiled=True)
     merged, strip = call(
         merge_kernel,

time: 96.5 us -> 99.4 us (1.030)
  starting transfers between devices: 32.2 us -> 49.9 us
  blocking collectives: 38 us -> 22.2 us
    all_to_all x1, starting transfers between devices: 7.42 us -> 23.9 us  [per_device(): lax.all_to_all(packed, 'rows', split_axis=0, concat_axis=0, tiled=True)]
    all_to_all x1, blocking collectives: 38 us -> 22.2 us  [per_device(): lax.all_to_all(heads_out, 'rows', split_axis=0, concat_axis=0, tiled=True)]
    all_to_all x1, waiting for transfers between devices: 6.01 us -> 8.38 us  [per_device(): lax.all_to_all(packed, 'rows', split_axis=0, concat_axis=0, tiled=True)]
    ppermute x8, waiting for transfers between devices: 3.42 us -> 1.98 us  [exchange(): swaps.append(lax.ppermute(block, axis, pairs + [(j, i) for i, j in pairs]))]
    ppermute x8, starting transfers between devices: 24.7 us -> 26.1 us  [exchange(): swaps.append(lax.ppermute(block, axis, pairs + [(j, i) for i, j in pairs]))]
  transfers between devices with their start and end apart: 9 -> 9, of which waited for: 4 -> 3; matrix products, arithmetic and copies ran while one was open for 0% -> 0% of each run, Pallas kernels for 1% -> 4%
where the time goes in v6:
time: 99.4 us; the launch traced here: 98.8 us
  starting transfers between devices  49.9 us (50%)
  blocking collectives  22.2 us (22%)
  Pallas kernels  12.7 us (13%)
  waiting for transfers between devices  10.4 us (10%)
  local copies, waits for them, and re-layouts  3.51 us (4%)
    ppermute x8, starting transfers between devices, exchange(): swaps.append(lax.ppermute(block, axis, pairs + [(j, i) for i, j in pairs]))  26.1 us
    all_to_all x1, starting transfers between devices, per_device(): lax.all_to_all(packed, 'rows', split_axis=0, concat_axis=0, tiled=True)  23.9 us
    all_to_all x1, blocking collectives, per_device(): lax.all_to_all(heads_out, 'rows', split_axis=0, concat_axis=0, tiled=True)  22.2 us
    pallas_call x6, Pallas kernels, call(): pl.pallas_call(kernel, out_shape=outs, in_specs=[pl.BlockSpec(memory_spac...  12.7 us
    all_to_all x1, waiting for transfers between devices, per_device(): lax.all_to_all(packed, 'rows', split_axis=0, concat_axis=0, tiled=True)  8.38 us
    unnamed x16, local copies, waits for them, and re-layouts  3.51 us
  transfers between devices with their start and end apart: 9, of which 3 were waited for; matrix products, arithmetic and copies ran while one was open for 0% of the time, Pallas kernels for 4%

profile of v6, /device:TPU:1, one launch (start us, length us, event | category | flops | bytes accessed | tf_op | source)
XLA Modules:
  0.0 98.8 jit_solution(16800351446062276820)
XLA Ops:
  0.0 1.0 %copy-done = bf16[32,64,128]{2,1,0:T(8,128)(2,1)S(1)} copy-done((bf16[32,64,128]{2,1,0:T(8,128)(2,1)S(1)}, bf16[32,64,128]{2,1,0:T(8,128)(2,1)}, u32[]{:S(2)}) %copy-start) | copy-done | bytes 524312
  1.0 0.5 turn_kernel.1
  1.5 3.9 %collective-permute-start.1 = (bf16[32,128]{1,0:T(8,128)(2,1)S(1)}, bf16[32,128]{1,0:T(8,128)(2,1)S(1)}, u32[]{:S(2)}, u32[]{:S(2)}) collective-permute-start(bf16[32,128]{1,0:T(8,128)(2,1)S(1)} %get-tuple-element.23), channel_id=1, source_target_pairs={{0,8},{16,24},{32,40},{48,56},{64,72},{80,88},{96,104},{112,120},{... | collective-permute-start | bytes 24584 | tf_op jit(solution)/shard_map/ppermute | solution.py:288
  5.5 0.7 collective-permute-start
  6.2 1.2 %copy-done.6 = bf16[2048,256]{1,0:T(8,128)(2,1)S(1)} copy-done((bf16[2048,256]{1,0:T(8,128)(2,1)S(1)}, bf16[2048,256]{1,0:T(8,128)(2,1)}, u32[]{:S(2)}) %copy-start.6) | copy-done | bytes 1048600
  7.4 1.2 %copy-done.7 = bf16[256,2048]{1,0:T(8,128)(2,1)S(1)} copy-done((bf16[256,2048]{1,0:T(8,128)(2,1)S(1)}, bf16[256,2048]{1,0:T(8,128)(2,1)}, u32[]{:S(2)}) %copy-start.7) | copy-done | bytes 1048600
  8.6 1.2 %weights_kernel.1 = (bf16[8,256,256]{2,1,0:T(8,128)(2,1)S(1)}, bf16[8,256,256]{2,1,0:T(8,128)(2,1)S(1)}) custom-call(bf16[2048,256]{1,0:T(8,128)(2,1)S(1)} %copy-done.6, bf16[256,2048]{1,0:T(8,128)(2,1)S(1)} %copy-done.7), custom_call_target="tpu_custom_call" | custom-call | flops 4294967296 | bytes 1048576 | tf_op jit(solution)/shard_map/weights_kernel/pallas_call | solution.py:271
  9.9 0.0 copy-start.3
  9.9 0.0 copy-start.5
  9.9 4.0 %collective-permute-start.3 = (bf16[3,32,128]{2,1,0:T(8,128)(2,1)S(1)}, bf16[3,32,128]{2,1,0:T(8,128)(2,1)S(1)}, u32[]{:S(2)}, u32[]{:S(2)}) collective-permute-start(bf16[3,32,128]{2,1,0:T(8,128)(2,1)S(1)} %pad_maximum_fusion.strip_ref), channel_id=1, source_target_pairs={{1,2},{3,4},{5,6},{2,1},{4,3},{6,5},{9,10},{11,12},{13,14},{10,9},... | collective-permute-start | bytes 73736 | tf_op jit(solution)/shard_map/ppermute | solution.py:288
  14.0 3.3 %collective-permute-start.2 = (bf16[3,32,128]{2,1,0:T(8,128)(2,1)S(1)}, bf16[3,32,128]{2,1,0:T(8,128)(2,1)S(1)}, u32[]{:S(2)}, u32[]{:S(2)}) collective-permute-start(bf16[3,32,128]{2,1,0:T(8,128)(2,1)S(1)} %pad_maximum_fusion.strip_ref), channel_id=1, source_target_pairs={{0,1},{2,3},{4,5},{6,7},{1,0},{3,2},{5,4},{7,6},{8,9},{10,11},{12,... | collective-permute-start | bytes 73736 | tf_op jit(solution)/shard_map/ppermute | solution.py:288
  17.4 0.8 collective-permute-done.2.even_strip
  18.2 4.5 %front_kernel.1 = (bf16[64,32,128]{2,1,0:T(8,128)(2,1)S(1)}, bf16[128,256]{1,0:T(8,128)(2,1)S(1)}, bf16[64,16,128]{2,1,0:T(8,128)(2,1)}, bf16[2,32,128]{2,1,0:T(8,128)(2,1)S(1)}) custom-call(bf16[64,32,128]{2,1,0:T(8,128)(2,1)S(1)} %get-tuple-element.22.map_ref, bf16[3,32,128]{2,1,0:T(8,128)(2,1)S(1)} %pad_maximum_fusion.strip_ref, ...), custom_call_target="tpu_custom_call" | custom-call | bytes 1048576 | tf_op jit(solution)/shard_map/front_kernel/pallas_call | solution.py:271
  22.7 23.9 %all-to-all-start = ((bf16[64,16,128]{2,1,0:T(8,128)(2,1)}), bf16[64,16,128]{2,1,0:T(8,128)(2,1)S(1)}, u32[]{:S(2)}, u32[]{:S(2)}) async-start(bf16[64,16,128]{2,1,0:T(8,128)(2,1)} %get-tuple-element.29), calls=%async_computation | async-start | bytes 524288 | tf_op jit(solution)/shard_map/all_to_all | solution.py:320
  46.5 0.7 collective-permute-start.5
  47.2 5.3 %collective-permute-start.4 = (bf16[2,32,128]{2,1,0:T(8,128)(2,1)S(1)}, bf16[2,32,128]{2,1,0:T(8,128)(2,1)S(1)}, u32[]{:S(2)}, u32[]{:S(2)}) collective-permute-start(bf16[2,32,128]{2,1,0:T(8,128)(2,1)S(1)} %get-tuple-element.30), channel_id=1, source_target_pairs={{0,8},{16,24},{32,40},{48,56},{64,72},{80,88},{96,104},{112,120},{... | collective-permute-start | bytes 49160 | tf_op jit(solution)/shard_map/ppermute | solution.py:288
  52.6 8.4 %all-to-all-done.packed_ref = bf16[64,16,128]{2,1,0:T(8,128)(2,1)S(1)} async-done(((bf16[64,16,128]{2,1,0:T(8,128)(2,1)}), bf16[64,16,128]{2,1,0:T(8,128)(2,1)S(1)}, u32[]{:S(2)}, u32[]{:S(2)}) %all-to-all-start) | async-done | bytes 262176 | tf_op jit(solution)/shard_map/all_to_all | solution.py:320
  60.9 2.3 %attention_kernel.1 = bf16[64,8,128]{2,1,0:T(8,128)(2,1)S(1)} custom-call(bf16[64,16,128]{2,1,0:T(8,128)(2,1)S(1)} %all-to-all-done.packed_ref), custom_call_target="tpu_custom_call" | custom-call | bytes 1048576 | tf_op jit(solution)/shard_map/attention_kernel/pallas_call | solution.py:271
  63.3 22.2 %all_to_all.10.returned_ref = bf16[64,8,128]{2,1,0:T(8,128)(2,1)S(1)} all-to-all(bf16[64,8,128]{2,1,0:T(8,128)(2,1)S(1)} %attention_kernel.1), channel_id=1, replica_groups=mesh['rows'=64,'cols'=8] {'rows'}, dimensions={0} | all-to-all | bytes 262144 | tf_op jit(solution)/shard_map/all_to_all | solution.py:331
  85.5 2.0 %merge_kernel.1 = (bf16[64,32,128]{2,1,0:T(8,128)(2,1)S(1)}, bf16[3,32,128]{2,1,0:T(8,128)(2,1)S(1)}) custom-call(bf16[64,8,128]{2,1,0:T(8,128)(2,1)S(1)} %all_to_all.10.returned_ref, bf16[128,256]{1,0:T(8,128)(2,1)S(1)} %get-tuple-element.32.tokens_ref, bf16[2,32,128]{2,1,0:T(8,128)(2,1)S(1)} %collective-permute-done.4.even_rim, ...), custom_call_target="tpu_custom_call" | custom-call | bytes 1048576 | tf_op jit(solution)/shard_map/merge_kernel/pallas_call | solution.py:271
  87.5 6.1 %collective-permute-start.7 = (bf16[3,32,128]{2,1,0:T(8,128)(2,1)S(1)}, bf16[3,32,128]{2,1,0:T(8,128)(2,1)S(1)}, u32[]{:S(2)}, u32[]{:S(2)}) collective-permute-start(bf16[3,32,128]{2,1,0:T(8,128)(2,1)S(1)} %get-tuple-element.38.strip_ref), channel_id=1, source_target_pairs={{1,2},{3,4},{5,6},{2,1},{4,3},{6,5},{9,10},{11,12},{13,14},{10,9},... | collective-permute-start | bytes 73736 | tf_op jit(solution)/shard_map/ppermute | solution.py:288
  93.7 1.9 %collective-permute-start.6 = (bf16[3,32,128]{2,1,0:T(8,128)(2,1)S(1)}, bf16[3,32,128]{2,1,0:T(8,128)(2,1)S(1)}, u32[]{:S(2)}, u32[]{:S(2)}) collective-permute-start(bf16[3,32,128]{2,1,0:T(8,128)(2,1)S(1)} %get-tuple-element.38.strip_ref), channel_id=1, source_target_pairs={{0,1},{2,3},{4,5},{6,7},{1,0},{3,2},{5,4},{7,6},{8,9},{10,11},{12,... | collective-permute-start | bytes 73736 | tf_op jit(solution)/shard_map/ppermute | solution.py:288
  95.6 1.2 %collective-permute-done.6.even_strip = bf16[3,32,128]{2,1,0:T(8,128)(2,1)S(1)} collective-permute-done((bf16[3,32,128]{2,1,0:T(8,128)(2,1)S(1)}, bf16[3,32,128]{2,1,0:T(8,128)(2,1)S(1)}, u32[]{:S(2)}, u32[]{:S(2)}) %collective-permute-start.6) | collective-permute-done | bytes 24608 | tf_op jit(solution)/shard_map/ppermute | solution.py:288
  96.8 2.1 %back_kernel.1 = bf16[32,64,128]{2,1,0:T(8,128)(2,1)} custom-call(bf16[64,32,128]{2,1,0:T(8,128)(2,1)S(1)} %get-tuple-element.37.map_ref, bf16[3,32,128]{2,1,0:T(8,128)(2,1)S(1)} %get-tuple-element.38.strip_ref, bf16[3,32,128]{2,1,0:T(8,128)(2,1)S(1)} %collective-permute-done.6.even_strip, bf16[3,32,128]{2,1,0:T(8,128)(2,1)S(1)} %collective-permute-done.7.other_strip, ...), custom_call_target="tpu_custom_call" | custom-call | bytes 1048576 | tf_op jit(solution)/shard_map/back_kernel/pallas_call | solution.py:271
  (20 shorter events, 0.1 us)
Async XLA Ops:
  0.0 1.0 %copy-start = (bf16[32,64,128]{2,1,0:T(8,128)(2,1)S(1)}, bf16[32,64,128]{2,1,0:T(8,128)(2,1)}, u32[]{:S(2)}) copy-start(bf16[32,64,128]{2,1,0:T(8,128)(2,1)} %x_ref.1) | copy-start | bytes 1572868
  1.5 8.3 %collective-permute-start.1 = (bf16[32,128]{1,0:T(8,128)(2,1)S(1)}, bf16[32,128]{1,0:T(8,128)(2,1)S(1)}, u32[]{:S(2)}, u32[]{:S(2)}) collective-permute-start(bf16[32,128]{1,0:T(8,128)(2,1)S(1)} %get-tuple-element.23), channel_id=1, source_target_pairs={{0,8},{16,24},{32,40},{48,56},{64,72},{80,88},{96,104},{112,120},{... | collective-permute-start | bytes 24584 | tf_op jit(solution)/shard_map/ppermute | solution.py:288
  5.5 4.4 %collective-permute-start = (bf16[32,128]{1,0:T(8,128)(2,1)S(1)}, bf16[32,128]{1,0:T(8,128)(2,1)S(1)}, u32[]{:S(2)}, u32[]{:S(2)}) collective-permute-start(bf16[32,128]{1,0:T(8,128)(2,1)S(1)} %get-tuple-element.23), channel_id=1, source_target_pairs={{8,16},{24,32},{40,48},{56,64},{72,80},{88,96},{104,112},{120,128}... | collective-permute-start | bytes 24584 | tf_op jit(solution)/shard_map/ppermute | solution.py:288
  6.1 1.2 %copy-start.6 = (bf16[2048,256]{1,0:T(8,128)(2,1)S(1)}, bf16[2048,256]{1,0:T(8,128)(2,1)}, u32[]{:S(2)}) copy-start(bf16[2048,256]{1,0:T(8,128)(2,1)} %embed_ref.1) | copy-start | bytes 3145732
  7.4 1.2 %copy-start.7 = (bf16[256,2048]{1,0:T(8,128)(2,1)S(1)}, bf16[256,2048]{1,0:T(8,128)(2,1)}, u32[]{:S(2)}) copy-start(bf16[256,2048]{1,0:T(8,128)(2,1)} %unpatch_ref.1) | copy-start | bytes 3145732
  8.6 9.6 %copy-start.1 = (bf16[256,768]{1,0:T(8,128)(2,1)S(1)}, bf16[256,768]{1,0:T(8,128)(2,1)}, u32[]{:S(2)}) copy-start(bf16[256,768]{1,0:T(8,128)(2,1)} %qkv_ref.1) | copy-start | bytes 1179652
  9.9 8.3 %copy-start.3 = (bf16[32,288]{1,0:T(8,128)(2,1)S(1)}, bf16[32,288]{1,0:T(8,128)(2,1)}, u32[]{:S(2)}) copy-start(bf16[32,288]{1,0:T(8,128)(2,1)} %conv_ref.2) | copy-start | bytes 55300
  9.9 8.3 %copy-start.5 = (bf16[16,8,8]{0,2,1:T(8,128)(2,1)S(1)}, bf16[16,8,8]{0,2,1:T(8,128)(2,1)}, u32[]{:S(2)}) copy-start(bf16[16,8,8]{0,2,1:T(8,128)(2,1)} %param.12) | copy-start | bytes 6148
  9.9 7.4 %collective-permute-start.3 = (bf16[3,32,128]{2,1,0:T(8,128)(2,1)S(1)}, bf16[3,32,128]{2,1,0:T(8,128)(2,1)S(1)}, u32[]{:S(2)}, u32[]{:S(2)}) collective-permute-start(bf16[3,32,128]{2,1,0:T(8,128)(2,1)S(1)} %pad_maximum_fusion.strip_ref), channel_id=1, source_target_pairs={{1,2},{3,4},{5,6},{2,1},{4,3},{6,5},{9,10},{11,12},{13,14},{10,9},... | collective-permute-start | bytes 73736 | tf_op jit(solution)/shard_map/ppermute | solution.py:288
  14.0 4.2 %collective-permute-start.2 = (bf16[3,32,128]{2,1,0:T(8,128)(2,1)S(1)}, bf16[3,32,128]{2,1,0:T(8,128)(2,1)S(1)}, u32[]{:S(2)}, u32[]{:S(2)}) collective-permute-start(bf16[3,32,128]{2,1,0:T(8,128)(2,1)S(1)} %pad_maximum_fusion.strip_ref), channel_id=1, source_target_pairs={{0,1},{2,3},{4,5},{6,7},{1,0},{3,2},{5,4},{7,6},{8,9},{10,11},{12,... | collective-permute-start | bytes 73736 | tf_op jit(solution)/shard_map/ppermute | solution.py:288
  22.7 38.3 %all-to-all-start = ((bf16[64,16,128]{2,1,0:T(8,128)(2,1)}), bf16[64,16,128]{2,1,0:T(8,128)(2,1)S(1)}, u32[]{:S(2)}, u32[]{:S(2)}) async-start(bf16[64,16,128]{2,1,0:T(8,128)(2,1)} %get-tuple-element.29), calls=%async_computation | async-start | bytes 524288 | tf_op jit(solution)/shard_map/all_to_all | solution.py:320
  46.5 16.8 %collective-permute-start.5 = (bf16[2,32,128]{2,1,0:T(8,128)(2,1)S(1)}, bf16[2,32,128]{2,1,0:T(8,128)(2,1)S(1)}, u32[]{:S(2)}, u32[]{:S(2)}) collective-permute-start(bf16[2,32,128]{2,1,0:T(8,128)(2,1)S(1)} %get-tuple-element.30), channel_id=1, source_target_pairs={{8,16},{24,32},{40,48},{56,64},{72,80},{88,96},{104,112},{120,128}... | collective-permute-start | bytes 49160 | tf_op jit(solution)/shard_map/ppermute | solution.py:288
  47.2 16.1 %collective-permute-start.4 = (bf16[2,32,128]{2,1,0:T(8,128)(2,1)S(1)}, bf16[2,32,128]{2,1,0:T(8,128)(2,1)S(1)}, u32[]{:S(2)}, u32[]{:S(2)}) collective-permute-start(bf16[2,32,128]{2,1,0:T(8,128)(2,1)S(1)} %get-tuple-element.30), channel_id=1, source_target_pairs={{0,8},{16,24},{32,40},{48,56},{64,72},{80,88},{96,104},{112,120},{... | collective-permute-start | bytes 49160 | tf_op jit(solution)/shard_map/ppermute | solution.py:288
  63.3 22.2 %copy-start.2 = (bf16[256,256]{1,0:T(8,128)(2,1)S(1)}, bf16[256,256]{1,0:T(8,128)(2,1)}, u32[]{:S(2)}) copy-start(bf16[256,256]{1,0:T(8,128)(2,1)} %out_weight_ref.1) | copy-start | bytes 393220
  85.5 11.3 %copy-start.4 = (bf16[32,288]{1,0:T(8,128)(2,1)S(1)}, bf16[32,288]{1,0:T(8,128)(2,1)}, u32[]{:S(2)}) copy-start(bf16[32,288]{1,0:T(8,128)(2,1)} %conv_ref.3) | copy-start | bytes 55300
  87.5 8.1 %collective-permute-start.7 = (bf16[3,32,128]{2,1,0:T(8,128)(2,1)S(1)}, bf16[3,32,128]{2,1,0:T(8,128)(2,1)S(1)}, u32[]{:S(2)}, u32[]{:S(2)}) collective-permute-start(bf16[3,32,128]{2,1,0:T(8,128)(2,1)S(1)} %get-tuple-element.38.strip_ref), channel_id=1, source_target_pairs={{1,2},{3,4},{5,6},{2,1},{4,3},{6,5},{9,10},{11,12},{13,14},{10,9},... | collective-permute-start | bytes 73736 | tf_op jit(solution)/shard_map/ppermute | solution.py:288
  93.7 3.1 %collective-permute-start.6 = (bf16[3,32,128]{2,1,0:T(8,128)(2,1)S(1)}, bf16[3,32,128]{2,1,0:T(8,128)(2,1)S(1)}, u32[]{:S(2)}, u32[]{:S(2)}) collective-permute-start(bf16[3,32,128]{2,1,0:T(8,128)(2,1)S(1)} %get-tuple-element.38.strip_ref), channel_id=1, source_target_pairs={{0,1},{2,3},{4,5},{6,7},{1,0},{3,2},{5,4},{7,6},{8,9},{10,11},{12,... | collective-permute-start | bytes 73736 | tf_op jit(solution)/shard_map/ppermute | solution.py:288

commit v7 on v5

--- a/solution.py
+++ b/solution.py
@@ -148,29 +148,24 @@
             packed_ref[p * HEADS + h] = tile[p * PR : (p + 1) * PR]
 
 
-def attention_kernel(packed_ref, out_ref, rows_f32, padded, windows):
+def attention_kernel(packed_ref, out_ref, rows_f32, bias_f32, padded, windows):
     rows = packed_ref[...].reshape(SEQ, L)
-    lane = iota((SEQ, L), 1)
     wide = rows.astype(f32)
-    rows_f32[...] = pltpu.roll(jnp.where(lane < HEAD_DIM, wide, 0.0), HEAD_DIM, 1)
-    pick = one_hot((iota((8, L), 1) == 3 * HEAD_DIM))
-    bias = lax.dot_general(pick, rows, NT, preferred_element_type=f32)[0:1]
-    values = jnp.where((lane >= 2 * HEAD_DIM) & (lane < 3 * HEAD_DIM), wide, 0.0)
+    rows_f32[...] = pltpu.roll(jnp.where(iota((SEQ, L), 1) < HEAD_DIM, wide, 0.0), HEAD_DIM, 1)
+    bias_f32[...] = jnp.broadcast_to(wide[:, 3 * HEAD_DIM : 3 * HEAD_DIM + 1] * LOG2_E, (SEQ, L))
+    values = jnp.concatenate(
+        [wide.T[2 * HEAD_DIM : 3 * HEAD_DIM], jnp.ones((16, SEQ), f32)], axis=0
+    ).astype(bf16)
     scale = HEAD_DIM ** (-0.5) * LOG2_E
-    bias = bias * LOG2_E
-    block_of = iota((SEQ // 4, L), 1) // HEAD_DIM
-    total = jnp.zeros((SEQ // 4, L), f32)
+    quarters = []
     for quarter in range(4):
         queries = rows_f32[pl.ds(quarter, SEQ // 4, stride=4), :].astype(bf16)
-        scores = lax.dot_general(queries, rows, NT, preferred_element_type=f32) * scale + bias
-        peak = jnp.max(scores, axis=1, keepdims=True)
-        weights = jnp.exp2(scores - peak).astype(bf16)
-        shift = (quarter * HEAD_DIM - 2 * HEAD_DIM) % L
-        placed = pltpu.roll(values, shift, 1) if shift else values
-        placed = jnp.where(lane // HEAD_DIM == quarter, placed, 1.0).astype(bf16)
-        product = jnp.dot(weights, placed, preferred_element_type=f32)
-        sums = pltpu.roll(product, HEAD_DIM, 1)
-        total = jnp.where(block_of == quarter, product / sums, total)
+        scores = lax.dot_general(rows, queries, NT, preferred_element_type=f32) * scale
+        scores = scores + jnp.concatenate([bias_f32[...]] * (SEQ // 4 // L), axis=1)
+        weights = jnp.exp2(scores - jnp.max(scores, axis=0, keepdims=True)).astype(bf16)
+        product = jnp.dot(values, weights, preferred_element_type=f32)
+        quarters.append(product[:HEAD_DIM] / product[HEAD_DIM : HEAD_DIM + 1])
+    total = jnp.concatenate(quarters, axis=0).T
     pad = jnp.zeros((8, L), f32)
     padded[0:8, :] = pad
     padded[8 : 8 + SEQ // 4, :] = total
@@ -322,7 +317,7 @@
         attention_kernel,
         shape(GROUPS, WINDOW, L),
         [
-            pltpu.VMEM((SEQ, L), f32), pltpu.VMEM((SEQ // 4 + 16, L), f32),
+            pltpu.VMEM((SEQ, L), f32), pltpu.VMEM((SEQ, L), f32), pltpu.VMEM((SEQ // 4 + 16, L), f32),
             pltpu.VMEM((GROUPS * WINDOW, L), f32),
         ],
         arrived,

time: 96.5 us -> 97.1 us (level)
  no operation moved by 1% of the time
where the time goes in v7:
time: 97.1 us; the launch traced here: 96.6 us
  blocking collectives  38 us (39%)
  starting transfers between devices  32.1 us (33%)
  Pallas kernels  13.2 us (14%)
  waiting for transfers between devices  9.43 us (10%)
  local copies, waits for them, and re-layouts  3.51 us (4%)
    all_to_all x1, blocking collectives, per_device(): lax.all_to_all(packed, 'rows', split_axis=0, concat_axis=0, tiled=True)  38 us
    ppermute x8, starting transfers between devices, exchange(): swaps.append(lax.ppermute(block, axis, pairs + [(j, i) for i, j in pairs]))  24.7 us
    pallas_call x6, Pallas kernels, call(): pl.pallas_call(kernel, out_shape=outs, in_specs=[pl.BlockSpec(memory_spac...  13.2 us
    all_to_all x1, starting transfers between devices, per_device(): lax.all_to_all(heads_out, 'rows', split_axis=0, concat_axis=0, tiled=True)  7.41 us
    all_to_all x1, waiting for transfers between devices, per_device(): lax.all_to_all(heads_out, 'rows', split_axis=0, concat_axis=0, tiled=True)  6.01 us
    unnamed x16, local copies, waits for them, and re-layouts  3.51 us
    ppermute x8, waiting for transfers between devices, exchange(): swaps.append(lax.ppermute(block, axis, pairs + [(j, i) for i, j in pairs]))  3.42 us
  transfers between devices with their start and end apart: 9, of which 4 were waited for; matrix products, arithmetic and copies ran while one was open for 0% of the time, Pallas kernels for 1%

profile of v7, /device:TPU:1, one launch (start us, length us, event | category | flops | bytes accessed | tf_op | source)
XLA Modules:
  0.0 96.6 jit_solution(8595859286267010)
XLA Ops:
  0.0 1.0 %copy-done = bf16[32,64,128]{2,1,0:T(8,128)(2,1)S(1)} copy-done((bf16[32,64,128]{2,1,0:T(8,128)(2,1)S(1)}, bf16[32,64,128]{2,1,0:T(8,128)(2,1)}, u32[]{:S(2)}) %copy-start) | copy-done | bytes 524312
  1.0 0.5 turn_kernel.1
  1.5 3.9 %collective-permute-start.1 = (bf16[32,128]{1,0:T(8,128)(2,1)S(1)}, bf16[32,128]{1,0:T(8,128)(2,1)S(1)}, u32[]{:S(2)}, u32[]{:S(2)}) collective-permute-start(bf16[32,128]{1,0:T(8,128)(2,1)S(1)} %get-tuple-element.20), channel_id=1, source_target_pairs={{0,8},{16,24},{32,40},{48,56},{64,72},{80,88},{96,104},{112,120},{... | collective-permute-start | bytes 24584 | tf_op jit(solution)/shard_map/ppermute | solution.py:283
  5.5 0.7 collective-permute-start
  6.2 1.2 %copy-done.6 = bf16[2048,256]{1,0:T(8,128)(2,1)S(1)} copy-done((bf16[2048,256]{1,0:T(8,128)(2,1)S(1)}, bf16[2048,256]{1,0:T(8,128)(2,1)}, u32[]{:S(2)}) %copy-start.6) | copy-done | bytes 1048600
  7.4 1.2 %copy-done.7 = bf16[256,2048]{1,0:T(8,128)(2,1)S(1)} copy-done((bf16[256,2048]{1,0:T(8,128)(2,1)S(1)}, bf16[256,2048]{1,0:T(8,128)(2,1)}, u32[]{:S(2)}) %copy-start.7) | copy-done | bytes 1048600
  8.6 1.2 %weights_kernel.1 = (bf16[8,256,256]{2,1,0:T(8,128)(2,1)S(1)}, bf16[8,256,256]{2,1,0:T(8,128)(2,1)S(1)}) custom-call(bf16[2048,256]{1,0:T(8,128)(2,1)S(1)} %copy-done.6, bf16[256,2048]{1,0:T(8,128)(2,1)S(1)} %copy-done.7), custom_call_target="tpu_custom_call" | custom-call | flops 4294967296 | bytes 1048576 | tf_op jit(solution)/shard_map/weights_kernel/pallas_call | solution.py:266
  9.9 0.0 copy-start.5
  9.9 4.0 %collective-permute-start.3 = (bf16[3,32,128]{2,1,0:T(8,128)(2,1)S(1)}, bf16[3,32,128]{2,1,0:T(8,128)(2,1)S(1)}, u32[]{:S(2)}, u32[]{:S(2)}) collective-permute-start(bf16[3,32,128]{2,1,0:T(8,128)(2,1)S(1)} %pad_maximum_fusion.strip_ref), channel_id=1, source_target_pairs={{1,2},{3,4},{5,6},{2,1},{4,3},{6,5},{9,10},{11,12},{13,14},{10,9},... | collective-permute-start | bytes 73736 | tf_op jit(solution)/shard_map/ppermute | solution.py:283
  14.0 3.3 %collective-permute-start.2 = (bf16[3,32,128]{2,1,0:T(8,128)(2,1)S(1)}, bf16[3,32,128]{2,1,0:T(8,128)(2,1)S(1)}, u32[]{:S(2)}, u32[]{:S(2)}) collective-permute-start(bf16[3,32,128]{2,1,0:T(8,128)(2,1)S(1)} %pad_maximum_fusion.strip_ref), channel_id=1, source_target_pairs={{0,1},{2,3},{4,5},{6,7},{1,0},{3,2},{5,4},{7,6},{8,9},{10,11},{12,... | collective-permute-start | bytes 73736 | tf_op jit(solution)/shard_map/ppermute | solution.py:283
  17.4 0.8 collective-permute-done.2.even_strip
  18.2 3.8 %front_kernel.1 = (bf16[64,32,128]{2,1,0:T(8,128)(2,1)S(1)}, bf16[128,256]{1,0:T(8,128)(2,1)S(1)}, bf16[64,16,128]{2,1,0:T(8,128)(2,1)S(1)}, bf16[2,32,128]{2,1,0:T(8,128)(2,1)S(1)}) custom-call(bf16[64,32,128]{2,1,0:T(8,128)(2,1)S(1)} %get-tuple-element.19.map_ref, bf16[3,32,128]{2,1,0:T(8,128)(2,1)S(1)} %pad_maximum_fusion.strip_ref, ...), custom_call_target="tpu_custom_call" | custom-call | bytes 1048576 | tf_op jit(solution)/shard_map/front_kernel/pallas_call | solution.py:266
  22.0 38.0 %all_to_all.10.packed_ref = bf16[64,16,128]{2,1,0:T(8,128)(2,1)S(1)} all-to-all(bf16[64,16,128]{2,1,0:T(8,128)(2,1)S(1)} %get-tuple-element.26), channel_id=1, replica_groups=mesh['rows'=64,'cols'=8] {'rows'}, dimensions={0} | all-to-all | bytes 524288 | tf_op jit(solution)/shard_map/all_to_all | solution.py:315
  60.0 3.6 %attention_kernel.1 = bf16[64,8,128]{2,1,0:T(8,128)(2,1)} custom-call(bf16[64,16,128]{2,1,0:T(8,128)(2,1)S(1)} %all_to_all.10.packed_ref), custom_call_target="tpu_custom_call" | custom-call | bytes 1048576 | tf_op jit(solution)/shard_map/attention_kernel/pallas_call | solution.py:266
  63.6 7.4 %all-to-all-start.1 = ((bf16[64,8,128]{2,1,0:T(8,128)(2,1)}), bf16[64,8,128]{2,1,0:T(8,128)(2,1)S(1)}, u32[]{:S(2)}, u32[]{:S(2)}) async-start(bf16[64,8,128]{2,1,0:T(8,128)(2,1)} %attention_kernel.1), calls=%async_computation.1 | async-start | bytes 262144 | tf_op jit(solution)/shard_map/all_to_all | solution.py:325
  71.0 0.7 collective-permute-start.5
  71.7 5.3 %collective-permute-start.4 = (bf16[2,32,128]{2,1,0:T(8,128)(2,1)S(1)}, bf16[2,32,128]{2,1,0:T(8,128)(2,1)S(1)}, u32[]{:S(2)}, u32[]{:S(2)}) collective-permute-start(bf16[2,32,128]{2,1,0:T(8,128)(2,1)S(1)} %get-tuple-element.28), channel_id=1, source_target_pairs={{0,8},{16,24},{32,40},{48,56},{64,72},{80,88},{96,104},{112,120},{... | collective-permute-start | bytes 49160 | tf_op jit(solution)/shard_map/ppermute | solution.py:283
  77.1 1.4 %collective-permute-done.4.even_rim = bf16[2,32,128]{2,1,0:T(8,128)(2,1)S(1)} collective-permute-done((bf16[2,32,128]{2,1,0:T(8,128)(2,1)S(1)}, bf16[2,32,128]{2,1,0:T(8,128)(2,1)S(1)}, u32[]{:S(2)}, u32[]{:S(2)}) %collective-permute-start.4) | collective-permute-done | bytes 16416 | tf_op jit(solution)/shard_map/ppermute | solution.py:283
  78.5 6.0 %all-to-all-done.1.returned_ref = bf16[64,8,128]{2,1,0:T(8,128)(2,1)S(1)} async-done(((bf16[64,8,128]{2,1,0:T(8,128)(2,1)}), bf16[64,8,128]{2,1,0:T(8,128)(2,1)S(1)}, u32[]{:S(2)}, u32[]{:S(2)}) %all-to-all-start.1) | async-done | bytes 131104 | tf_op jit(solution)/shard_map/all_to_all | solution.py:325
  84.5 2.0 %merge_kernel.1 = (bf16[64,32,128]{2,1,0:T(8,128)(2,1)S(1)}, bf16[3,32,128]{2,1,0:T(8,128)(2,1)S(1)}) custom-call(bf16[64,8,128]{2,1,0:T(8,128)(2,1)S(1)} %all-to-all-done.1.returned_ref, bf16[128,256]{1,0:T(8,128)(2,1)S(1)} %get-tuple-element.27.tokens_ref, bf16[2,32,128]{2,1,0:T(8,128)(2,1)S(1)} %collective-permute-done.4.even_rim, ...), custom_call_target="tpu_custom_call" | custom-call | bytes 1048576 | tf_op jit(solution)/shard_map/merge_kernel/pallas_call | solution.py:266
  86.6 4.8 %collective-permute-start.7 = (bf16[3,32,128]{2,1,0:T(8,128)(2,1)S(1)}, bf16[3,32,128]{2,1,0:T(8,128)(2,1)S(1)}, u32[]{:S(2)}, u32[]{:S(2)}) collective-permute-start(bf16[3,32,128]{2,1,0:T(8,128)(2,1)S(1)} %get-tuple-element.32.strip_ref), channel_id=1, source_target_pairs={{1,2},{3,4},{5,6},{2,1},{4,3},{6,5},{9,10},{11,12},{13,14},{10,9},... | collective-permute-start | bytes 73736 | tf_op jit(solution)/shard_map/ppermute | solution.py:283
  91.4 1.9 %collective-permute-start.6 = (bf16[3,32,128]{2,1,0:T(8,128)(2,1)S(1)}, bf16[3,32,128]{2,1,0:T(8,128)(2,1)S(1)}, u32[]{:S(2)}, u32[]{:S(2)}) collective-permute-start(bf16[3,32,128]{2,1,0:T(8,128)(2,1)S(1)} %get-tuple-element.32.strip_ref), channel_id=1, source_target_pairs={{0,1},{2,3},{4,5},{6,7},{1,0},{3,2},{5,4},{7,6},{8,9},{10,11},{12,... | collective-permute-start | bytes 73736 | tf_op jit(solution)/shard_map/ppermute | solution.py:283
  93.3 1.2 %collective-permute-done.6.even_strip = bf16[3,32,128]{2,1,0:T(8,128)(2,1)S(1)} collective-permute-done((bf16[3,32,128]{2,1,0:T(8,128)(2,1)S(1)}, bf16[3,32,128]{2,1,0:T(8,128)(2,1)S(1)}, u32[]{:S(2)}, u32[]{:S(2)}) %collective-permute-start.6) | collective-permute-done | bytes 24608 | tf_op jit(solution)/shard_map/ppermute | solution.py:283
  94.5 2.1 %back_kernel.1 = bf16[32,64,128]{2,1,0:T(8,128)(2,1)} custom-call(bf16[64,32,128]{2,1,0:T(8,128)(2,1)S(1)} %get-tuple-element.31.map_ref, bf16[3,32,128]{2,1,0:T(8,128)(2,1)S(1)} %get-tuple-element.32.strip_ref, bf16[3,32,128]{2,1,0:T(8,128)(2,1)S(1)} %collective-permute-done.6.even_strip, bf16[3,32,128]{2,1,0:T(8,128)(2,1)S(1)} %collective-permute-done.7.other_strip, ...), custom_call_target="tpu_custom_call" | custom-call | bytes 1048576 | tf_op jit(solution)/shard_map/back_kernel/pallas_call | solution.py:266
  (20 shorter events, 0.1 us)
Async XLA Ops:
  0.0 1.0 %copy-start = (bf16[32,64,128]{2,1,0:T(8,128)(2,1)S(1)}, bf16[32,64,128]{2,1,0:T(8,128)(2,1)}, u32[]{:S(2)}) copy-start(bf16[32,64,128]{2,1,0:T(8,128)(2,1)} %x_ref.1) | copy-start | bytes 1572868
  1.5 8.3 %collective-permute-start.1 = (bf16[32,128]{1,0:T(8,128)(2,1)S(1)}, bf16[32,128]{1,0:T(8,128)(2,1)S(1)}, u32[]{:S(2)}, u32[]{:S(2)}) collective-permute-start(bf16[32,128]{1,0:T(8,128)(2,1)S(1)} %get-tuple-element.20), channel_id=1, source_target_pairs={{0,8},{16,24},{32,40},{48,56},{64,72},{80,88},{96,104},{112,120},{... | collective-permute-start | bytes 24584 | tf_op jit(solution)/shard_map/ppermute | solution.py:283
  5.5 4.4 %collective-permute-start = (bf16[32,128]{1,0:T(8,128)(2,1)S(1)}, bf16[32,128]{1,0:T(8,128)(2,1)S(1)}, u32[]{:S(2)}, u32[]{:S(2)}) collective-permute-start(bf16[32,128]{1,0:T(8,128)(2,1)S(1)} %get-tuple-element.20), channel_id=1, source_target_pairs={{8,16},{24,32},{40,48},{56,64},{72,80},{88,96},{104,112},{120,128}... | collective-permute-start | bytes 24584 | tf_op jit(solution)/shard_map/ppermute | solution.py:283
  6.1 1.2 %copy-start.6 = (bf16[2048,256]{1,0:T(8,128)(2,1)S(1)}, bf16[2048,256]{1,0:T(8,128)(2,1)}, u32[]{:S(2)}) copy-start(bf16[2048,256]{1,0:T(8,128)(2,1)} %embed_ref.1) | copy-start | bytes 3145732
  7.4 1.2 %copy-start.7 = (bf16[256,2048]{1,0:T(8,128)(2,1)S(1)}, bf16[256,2048]{1,0:T(8,128)(2,1)}, u32[]{:S(2)}) copy-start(bf16[256,2048]{1,0:T(8,128)(2,1)} %unpatch_ref.1) | copy-start | bytes 3145732
  8.6 9.6 %copy-start.1 = (bf16[256,768]{1,0:T(8,128)(2,1)S(1)}, bf16[256,768]{1,0:T(8,128)(2,1)}, u32[]{:S(2)}) copy-start(bf16[256,768]{1,0:T(8,128)(2,1)} %qkv_ref.1) | copy-start | bytes 1179652
  9.9 8.3 %copy-start.3 = (bf16[32,288]{1,0:T(8,128)(2,1)S(1)}, bf16[32,288]{1,0:T(8,128)(2,1)}, u32[]{:S(2)}) copy-start(bf16[32,288]{1,0:T(8,128)(2,1)} %conv_ref.2) | copy-start | bytes 55300
  9.9 8.3 %copy-start.5 = (bf16[16,8,8]{0,2,1:T(8,128)(2,1)S(1)}, bf16[16,8,8]{0,2,1:T(8,128)(2,1)}, u32[]{:S(2)}) copy-start(bf16[16,8,8]{0,2,1:T(8,128)(2,1)} %param.12) | copy-start | bytes 6148
  9.9 7.4 %collective-permute-start.3 = (bf16[3,32,128]{2,1,0:T(8,128)(2,1)S(1)}, bf16[3,32,128]{2,1,0:T(8,128)(2,1)S(1)}, u32[]{:S(2)}, u32[]{:S(2)}) collective-permute-start(bf16[3,32,128]{2,1,0:T(8,128)(2,1)S(1)} %pad_maximum_fusion.strip_ref), channel_id=1, source_target_pairs={{1,2},{3,4},{5,6},{2,1},{4,3},{6,5},{9,10},{11,12},{13,14},{10,9},... | collective-permute-start | bytes 73736 | tf_op jit(solution)/shard_map/ppermute | solution.py:283
  14.0 4.2 %collective-permute-start.2 = (bf16[3,32,128]{2,1,0:T(8,128)(2,1)S(1)}, bf16[3,32,128]{2,1,0:T(8,128)(2,1)S(1)}, u32[]{:S(2)}, u32[]{:S(2)}) collective-permute-start(bf16[3,32,128]{2,1,0:T(8,128)(2,1)S(1)} %pad_maximum_fusion.strip_ref), channel_id=1, source_target_pairs={{0,1},{2,3},{4,5},{6,7},{1,0},{3,2},{5,4},{7,6},{8,9},{10,11},{12,... | collective-permute-start | bytes 73736 | tf_op jit(solution)/shard_map/ppermute | solution.py:283
  63.6 20.9 %copy-start.2 = (bf16[256,256]{1,0:T(8,128)(2,1)S(1)}, bf16[256,256]{1,0:T(8,128)(2,1)}, u32[]{:S(2)}) copy-start(bf16[256,256]{1,0:T(8,128)(2,1)} %out_weight_ref.1) | copy-start | bytes 393220
  63.6 20.9 %all-to-all-start.1 = ((bf16[64,8,128]{2,1,0:T(8,128)(2,1)}), bf16[64,8,128]{2,1,0:T(8,128)(2,1)S(1)}, u32[]{:S(2)}, u32[]{:S(2)}) async-start(bf16[64,8,128]{2,1,0:T(8,128)(2,1)} %attention_kernel.1), calls=%async_computation.1 | async-start | bytes 262144 | tf_op jit(solution)/shard_map/all_to_all | solution.py:325
  71.0 6.0 %collective-permute-start.5 = (bf16[2,32,128]{2,1,0:T(8,128)(2,1)S(1)}, bf16[2,32,128]{2,1,0:T(8,128)(2,1)S(1)}, u32[]{:S(2)}, u32[]{:S(2)}) collective-permute-start(bf16[2,32,128]{2,1,0:T(8,128)(2,1)S(1)} %get-tuple-element.28), channel_id=1, source_target_pairs={{8,16},{24,32},{40,48},{56,64},{72,80},{88,96},{104,112},{120,128}... | collective-permute-start | bytes 49160 | tf_op jit(solution)/shard_map/ppermute | solution.py:283
  71.7 6.8 %collective-permute-start.4 = (bf16[2,32,128]{2,1,0:T(8,128)(2,1)S(1)}, bf16[2,32,128]{2,1,0:T(8,128)(2,1)S(1)}, u32[]{:S(2)}, u32[]{:S(2)}) collective-permute-start(bf16[2,32,128]{2,1,0:T(8,128)(2,1)S(1)} %get-tuple-element.28), channel_id=1, source_target_pairs={{0,8},{16,24},{32,40},{48,56},{64,72},{80,88},{96,104},{112,120},{... | collective-permute-start | bytes 49160 | tf_op jit(solution)/shard_map/ppermute | solution.py:283
  84.5 10.0 %copy-start.4 = (bf16[32,288]{1,0:T(8,128)(2,1)S(1)}, bf16[32,288]{1,0:T(8,128)(2,1)}, u32[]{:S(2)}) copy-start(bf16[32,288]{1,0:T(8,128)(2,1)} %conv_ref.3) | copy-start | bytes 55300
  86.6 6.8 %collective-permute-start.7 = (bf16[3,32,128]{2,1,0:T(8,128)(2,1)S(1)}, bf16[3,32,128]{2,1,0:T(8,128)(2,1)S(1)}, u32[]{:S(2)}, u32[]{:S(2)}) collective-permute-start(bf16[3,32,128]{2,1,0:T(8,128)(2,1)S(1)} %get-tuple-element.32.strip_ref), channel_id=1, source_target_pairs={{1,2},{3,4},{5,6},{2,1},{4,3},{6,5},{9,10},{11,12},{13,14},{10,9},... | collective-permute-start | bytes 73736 | tf_op jit(solution)/shard_map/ppermute | solution.py:283
  91.4 3.1 %collective-permute-start.6 = (bf16[3,32,128]{2,1,0:T(8,128)(2,1)S(1)}, bf16[3,32,128]{2,1,0:T(8,128)(2,1)S(1)}, u32[]{:S(2)}, u32[]{:S(2)}) collective-permute-start(bf16[3,32,128]{2,1,0:T(8,128)(2,1)S(1)} %get-tuple-element.32.strip_ref), channel_id=1, source_target_pairs={{0,1},{2,3},{4,5},{6,7},{1,0},{3,2},{5,4},{7,6},{8,9},{10,11},{12,... | collective-permute-start | bytes 73736 | tf_op jit(solution)/shard_map/ppermute | solution.py:283
